TPU v7x, 32 devices: a whole 2x2x4 slice. The times are simulated.
32 devices in a mesh: band: 4 (over y, x), ga: 8 (over z, core).
Axes of the slice: x: 2, y: 2, z: 4, core: 2. Of those that a mesh axis runs over, the one named last changes fastest.
Arguments:
- wavefunctions: bfloat16 [512, 98304], P('band', 'ga'), may hold values from -6 to 6
- projectors: bfloat16 [2048, 98304], P('band', 'ga'), may hold values from -0.125 to 0.125
- kinetic_diag: float32 [98304], P('ga'), may hold values from 0.1 to 4
- species_index: int32 [256], replicated, may hold values from 0 to 3
- coupling: float32 [4, 8, 8], replicated, may hold values from -5 to 5
Outputs:
- applied: bfloat16 [512, 98304], P('band', 'ga')
All inputs are finite; a program needn't handle non-finite values.
Results may differ from a plain program's by a relative error of at most 0.015.
Values may be sent and summed in bfloat16 or wider, within the bound.
No kernel may reach another device: no remote copies, remote signals or barrier semaphores. Data moves between devices by JAX's collectives and lax.ppermute only.
A program may use at most 64 MiB of HBM per device.

v0:
```python
import jax
import jax.numpy as jnp
from jax import lax
from jax.sharding import PartitionSpec as P

NPA = 8


def apply_blocks(correlations, species_index, coupling, atom_start):
    rows = correlations.shape[0]
    count = correlations.shape[1] // NPA
    local_species = lax.dynamic_slice_in_dim(species_index, atom_start, count)
    onehot = (
        local_species[:, None] == jnp.arange(coupling.shape[0], dtype=jnp.int32)[None, :]
    ).astype(jnp.float32)
    blocks = jnp.einsum("as,sij->aij", onehot, coupling, precision=lax.Precision.HIGHEST)
    mixed = jnp.einsum(
        "baj,aij->bai",
        correlations.reshape(rows, count, NPA),
        blocks,
        precision=lax.Precision.HIGHEST,
    )
    return mixed.reshape(rows, count * NPA).astype(jnp.bfloat16)


def reduce_and_mix(partial_value, species_index, coupling, first_proj):
    total = lax.psum(partial_value.astype(jnp.bfloat16), "ga").astype(jnp.float32)
    return apply_blocks(total, species_index, coupling, first_proj // NPA)


def local(wavefunctions, projectors, kinetic_diag, species_index, coupling):
    proj_local = projectors.shape[0]
    band_index = lax.axis_index("band")
    partial_value = jnp.einsum(
        "bg,pg->bp",
        lax.all_gather(wavefunctions, "band", axis=0, tiled=True),
        projectors,
        preferred_element_type=jnp.float32,
    )
    mixed = reduce_and_mix(partial_value, species_index, coupling, band_index * proj_local)
    nonlocal_term = lax.psum_scatter(
        jnp.dot(mixed, projectors, preferred_element_type=jnp.float32).astype(jnp.bfloat16),
        "band",
        scatter_dimension=0,
        tiled=True,
    ).astype(jnp.float32)
    return (kinetic_diag[None, :] * wavefunctions.astype(jnp.float32) + nonlocal_term).astype(
        jnp.bfloat16
    )


def solution(mesh):
    in_specs = (P("band", "ga"), P("band", "ga"), P("ga"), P(), P())
    out_specs = P("band", "ga")
    return jax.shard_map(local, mesh=mesh, in_specs=in_specs, out_specs=out_specs, check_vma=False)
```

profile of v0, /device:TPU:0, one launch (start us, length us, event | category | flops | bytes accessed | tf_op | source)
XLA Modules:
  0.0 351.6 jit_solution(8717082280470450847)
XLA Ops:
  6.5 0.0 copy-start
  6.5 0.0 all-gather.2.cloned.1.call-start
  6.5 0.7 all-gather.2.cloned.1.call-update
  7.3 0.0 copy-start.3
  7.3 0.0 all-reduce.2.cloned.1.call-start
  7.3 127.0 %all-gather.2.cloned.1.call-done = bf16[512,12288]{1,0:T(8,128)(2,1)} async-done(((bf16[128,12288]{1,0:T(8,128)(2,1)}), bf16[512,12288]{1,0:T(8,128)(2,1)}) %all-gather.2.cloned.1.call-update) | async-done | bytes 12582928 | tf_op jit(solution)/shard_map/all_gather | solution.py:36
  134.3 14.0 %fusion.1 = bf16[512,64,8]{0,2,1:T(8,128)(2,1)} fusion(bf16[512,12288]{1,0:T(8,128)(2,1)} %all-gather.2.cloned.1.call-done, bf16[512,12288]{1,0:T(8,128)(2,1)} %param.6), kind=kOutput, calls=%fused_computation.5 | convolution fusion | flops 6442713088 | bytes 25690112 | tf_op jit(solution)/shard_map/bg,pg->bp/dot_general | solution.py:34
  148.3 0.0 all-reduce.2.cloned.1.call-update
  148.3 0.0 reduce-scatter.2.cloned.1.call-start
  148.4 0.0 copy-done.3
  148.4 0.1 dynamic_slice.3
  148.5 0.0 copy-done
  148.5 0.2 fusion.3
  148.8 0.1 copy.7
  148.9 56.1 %all-reduce.2.cloned.1.call-done = bf16[512,64,8]{0,2,1:T(8,128)(2,1)} async-done(((bf16[512,64,8]{0,2,1:T(8,128)(2,1)}), bf16[512,64,8]{0,2,1:T(8,128)(2,1)}) %all-reduce.2.cloned.1.call-update) | async-done | bytes 524304 | tf_op jit(solution)/shard_map/psum | solution.py:27
  205.0 1.6 fusion
  206.6 14.2 %convolution_convert_fusion = bf16[512,12288]{1,0:T(8,128)(2,1)} fusion(bf16[512,512]{0,1:T(8,128)(2,1)S(1)} %fusion, bf16[512,12288]{1,0:T(8,128)(2,1)} %param.6), kind=kOutput, calls=%fused_computation | convolution fusion | flops 6448742400 | bytes 25690112 | tf_op jit(solution)/shard_map/dot_general | solution.py:42
  220.8 0.0 copy-start.1
  220.8 0.0 copy-start.2
  220.8 0.0 reduce-scatter.2.cloned.1.call-update
  220.8 119.8 %reduce-scatter.2.cloned.1.call-done = bf16[128,12288]{1,0:T(8,128)(2,1)} async-done(((bf16[512,12288]{1,0:T(8,128)(2,1)}), bf16[128,12288]{1,0:T(8,128)(2,1)}) %reduce-scatter.2.cloned.1.call-update) | async-done | bytes 3145744 | tf_op jit(solution)/shard_map/reduce_scatter | solution.py:41
  340.6 0.0 copy-done.1
  340.6 0.0 copy-done.2
  340.6 4.5 %add_convert_fusion = bf16[128,12288]{1,0:T(8,128)(2,1)} fusion(bf16[128,12288]{1,0:T(8,128)(2,1)} %reduce-scatter.2.cloned.1.call-done, bf16[128,12288]{1,0:T(8,128)(2,1)S(1)} %copy-done.1, f32[12288]{0:T(1024)S(1)} %copy-done.2), kind=kLoop, calls=%fused_computation.1 | loop fusion | flops 7864320 | bytes 9486336 | tf_op jit(solution)/shard_map/convert_element_type | solution.py:47
Async XLA Ops:
  6.5 142.0 %copy-start = (f32[4,8,8]{2,1,0:T(8,128)S(1)}, f32[4,8,8]{2,1,0:T(8,128)}, u32[]{:S(2)}) copy-start(f32[4,8,8]{2,1,0:T(8,128)} %param.9) | copy-start | bytes 3076
  6.5 127.8 %all-gather.2.cloned.1.call-start = ((), (), s32[]{:S(2)}) async-start(), calls=%async_computation.1 | async-start | bytes 15728640 | tf_op jit(solution)/shard_map/all_gather | solution.py:36
  7.3 141.2 %copy-start.3 = (s32[256]{0:T(256)S(1)}, s32[256]{0:T(256)}, u32[]{:S(2)}) copy-start(s32[256]{0:T(256)} %param.8) | copy-start | bytes 3076
  7.3 197.7 %all-reduce.2.cloned.1.call-start = ((), (), s32[]{:S(2)}) async-start(), calls=%async_computation.2 | async-start | bytes 1048576 | tf_op jit(solution)/shard_map/psum | solution.py:27
  148.3 192.3 %reduce-scatter.2.cloned.1.call-start = ((), (), s32[]{:S(2)}) async-start(), calls=%async_computation.3 | async-start | bytes 15728640 | tf_op jit(solution)/shard_map/reduce_scatter | solution.py:41
  220.8 119.9 %copy-start.1 = (bf16[128,12288]{1,0:T(8,128)(2,1)S(1)}, bf16[128,12288]{1,0:T(8,128)(2,1)}, u32[]{:S(2)}) copy-start(bf16[128,12288]{1,0:T(8,128)(2,1)} %param.5) | copy-start | bytes 9437188
  220.8 119.9 %copy-start.2 = (f32[12288]{0:T(1024)S(1)}, f32[12288]{0:T(1024)}, u32[]{:S(2)}) copy-start(f32[12288]{0:T(1024)} %param.7) | copy-start | bytes 147460
Sparse Core Ops, SparseCore 0:
  9.2 125.0 all-gather.1
  148.5 56.4 all-reduce.1
  220.9 119.6 reduce-scatter.1
where the time goes:
time: 352 us
  waiting for transfers between devices  304 us (86%)
  matrix products  30 us (9%)
  between operations  13.2 us (4%)
  other arithmetic  4.48 us (1%)
    all_gather x1, waiting for transfers between devices, local(): lax.all_gather(wavefunctions, 'band', axis=0, tiled=True)  127 us
    reduce_scatter x1, waiting for transfers between devices, local(): lax.psum_scatter(jnp.dot(mixed, projectors, preferred_element_type=jnp.fl...  120 us
    psum x1, waiting for transfers between devices, reduce_and_mix(): lax.psum(partial_value.astype(jnp.bfloat16), 'ga').astype(jnp.float32)  56.1 us
    dot_general x1, matrix products, local(): jnp.dot(mixed, projectors, preferred_element_type=jnp.float32)  14.2 us
    dot_general x1, matrix products, local(): jnp.einsum('bg,pg->bp', lax.all_gather(wavefunctions, 'band', axis=0, til...  14 us
  transfers between devices with their start and end apart: 3, of which 3 were waited for; matrix products, arithmetic and copies ran while one was open for 0% of the time, Pallas kernels for 0%

commit v1 on v0

v1 whole, which is shorter than its diff:
```python
import functools

import jax
import jax.numpy as jnp
from jax import lax
from jax.experimental import pallas as pl
from jax.experimental.pallas import tpu as pltpu
from jax.sharding import PartitionSpec as P


NPA = 8


def apply_blocks(correlations, species_index, coupling, atom_start):
    rows = correlations.shape[0]
    count = correlations.shape[1] // NPA
    local_species = lax.dynamic_slice_in_dim(species_index, atom_start, count)
    onehot = (
        local_species[:, None] == jnp.arange(coupling.shape[0], dtype=jnp.int32)[None, :]
    ).astype(jnp.float32)
    blocks = jnp.einsum("as,sij->aij", onehot, coupling, precision=lax.Precision.HIGHEST)
    mixed = jnp.einsum(
        "baj,aij->bai",
        correlations.reshape(rows, count, NPA),
        blocks,
        precision=lax.Precision.HIGHEST,
    )
    return mixed.reshape(rows, count * NPA).astype(jnp.bfloat16)


def local_any(wavefunctions, projectors, kinetic_diag, species_index, coupling):
    proj_local = projectors.shape[0]
    partial_value = jnp.einsum(
        "bg,pg->bp",
        lax.all_gather(wavefunctions, "band", axis=0, tiled=True),
        projectors,
        preferred_element_type=jnp.float32,
    )
    total = lax.psum(partial_value.astype(jnp.bfloat16), "ga").astype(jnp.float32)
    first_atom = lax.axis_index("band") * proj_local // NPA
    mixed = apply_blocks(total, species_index, coupling, first_atom)
    nonlocal_term = lax.psum_scatter(
        jnp.dot(mixed, projectors, preferred_element_type=jnp.float32).astype(jnp.bfloat16),
        "band",
        scatter_dimension=0,
        tiled=True,
    ).astype(jnp.float32)
    return (kinetic_diag[None, :] * wavefunctions.astype(jnp.float32) + nonlocal_term).astype(
        jnp.bfloat16
    )


def swap(parts, bit, flag):
    return [jnp.where(flag, parts[i ^ bit], part) for i, part in enumerate(parts)]


def mixing_matrix(species_index, coupling, first_atom, count):
    species = lax.dynamic_slice_in_dim(species_index, first_atom, count)
    onehot = (
        species[:, None] == jnp.arange(coupling.shape[0], dtype=jnp.int32)[None, :]
    ).astype(jnp.float32)
    blocks = jnp.einsum("as,sij->aji", onehot, coupling, precision=lax.Precision.HIGHEST)
    tall = blocks.reshape(count * NPA, NPA)
    wide = jnp.tile(tall, (1, count))
    size = count * NPA
    row = lax.broadcasted_iota(jnp.int32, (size, size), 0) // NPA
    col = lax.broadcasted_iota(jnp.int32, (size, size), 1) // NPA
    return jnp.where(row == col, wide, 0.0)


def chunk_rows(rows, ga):
    unit = max(32, ga * 4)
    if rows % (4 * unit):
        return [(0, rows)]
    return [(0, rows // 4), (rows // 4, rows // 2), (3 * rows // 4, rows // 4)]


def stage_order(n):
    order = [("Wd", 0), ("We", 0), ("T", 0), ("Wf", 0), ("Wd", 1), ("We", 1), ("A", 0), ("B", 0)]
    order += [("Wf", 1), ("Wd", 2), ("We", 2)]
    for c in range(n):
        order += [("A", c), ("Wf", c + 1), ("B", c), ("C", c)]
        order += [("I", c - 2), ("H", c - 1), ("E", c), ("G", c), ("K", c), ("Wd", c + 3), ("We", c + 3)]
    order += [("I", n - 2), ("H", n - 1), ("I", n - 1)]
    seen, kept = set(), []
    for item in order:
        if 0 <= item[1] < n and item not in seen:
            seen.add(item)
            kept.append(item)
    return kept


def tile_of(width, parts=4):
    while parts > 1 and width % (128 * parts):
        parts -= 1
    return width // parts


def piece_row(piece, rows, index, band):
    first = index * piece
    return pl.multiple_of(((first // rows) ^ band) * rows + first % rows, piece)


def transpose_kernel(value, out):
    out[...] = value[...].T


def transpose(value):
    block, width = value.shape
    tile = tile_of(width, 12)
    return pl.pallas_call(
        transpose_kernel,
        grid=(width // tile,),
        in_specs=[pl.BlockSpec((block, tile), lambda k: (0, k))],
        out_specs=pl.BlockSpec((tile, block), lambda k: (k, 0)),
        out_shape=jax.ShapeDtypeStruct((width, block), value.dtype),
        cost_estimate=pl.CostEstimate(
            flops=16 * block * width, bytes_accessed=4 * block * width, transcendentals=0
        ),
        name="transpose",
    )(value)


def correlate_kernel(nz, where, *refs):
    halves, (proj, kept, sent, acc) = refs[:8], refs[8:]
    step = pl.program_id(0)
    band, core = where[0], where[1]
    bands = jnp.concatenate([half[...] for half in halves], axis=0)
    part = jnp.dot(bands, proj[...], preferred_element_type=jnp.float32)

    @pl.when(step == 0)
    def _():
        acc[...] = part

    @pl.when(step > 0)
    def _():
        acc[...] += part

    @pl.when(step == pl.num_programs(0) - 1)
    def _():
        rows = 2 * halves[0].shape[0]
        piece = kept.shape[1]
        for k in range(nz):
            at = piece_row(piece, rows, 2 * k + core, band)
            kept[k] = acc[pl.ds(at, piece), :].astype(kept.dtype)
            at = piece_row(piece, rows, 2 * k + 1 - core, band)
            sent[k] = acc[pl.ds(at, piece), :].astype(sent.dtype)


def correlate(where, nz, halves, proj):
    half, width = halves[0].shape
    block = proj.shape[1]
    piece = 8 * half // (2 * nz)
    tile = tile_of(width)
    out = jax.ShapeDtypeStruct((nz, piece, block), jnp.bfloat16)
    whole = pl.BlockSpec((nz, piece, block), lambda k, w: (0, 0, 0))
    return pl.pallas_call(
        functools.partial(correlate_kernel, nz),
        grid_spec=pltpu.PrefetchScalarGridSpec(
            num_scalar_prefetch=1,
            grid=(width // tile,),
            in_specs=[pl.BlockSpec((half, tile), lambda k, w: (0, k))] * 8
            + [pl.BlockSpec((tile, block), lambda k, w: (k, 0))],
            out_specs=[whole, whole],
            scratch_shapes=[pltpu.VMEM((8 * half, block), jnp.float32)],
        ),
        out_shape=[out, out],
        cost_estimate=pl.CostEstimate(
            flops=16 * half * width * block,
            bytes_accessed=2 * (8 * half + block) * width,
            transcendentals=0,
        ),
        name="correlate",
    )(where, *halves, proj)


def expand_kernel(nz, where, here, there, proj, *refs):
    outs, (pieces, mixed) = refs[:8], refs[8:]
    band, core = where[0], where[1]
    half = outs[0].shape[0]
    rows = 2 * half
    piece = here.shape[1]

    @pl.when(pl.program_id(0) == 0)
    def _():
        for k in range(nz):
            pieces[piece_row(piece, rows, 2 * k + core, band) // piece] = here[k]
            pieces[piece_row(piece, rows, 2 * k + 1 - core, band) // piece] = there[k]
        mixed[...] = jnp.concatenate([pieces[k] for k in range(2 * nz)], axis=0)

    value = jnp.dot(mixed[...], proj[...], preferred_element_type=jnp.float32)
    for k, out in enumerate(outs):
        out[...] = value[k * half : (k + 1) * half].astype(out.dtype)


def expand(where, nz, rows, here, there, proj):
    block, width = proj.shape
    piece = here.shape[1]
    tile = tile_of(width)
    whole = pl.BlockSpec((nz, piece, block), lambda k, w: (0, 0, 0))

    def out(count):
        return jax.ShapeDtypeStruct((count, width), jnp.bfloat16)

    def spec(count):
        return pl.BlockSpec((count, tile), lambda k, w: (0, k))

    counts = [rows // 2] * 8
    return pl.pallas_call(
        functools.partial(expand_kernel, nz),
        grid_spec=pltpu.PrefetchScalarGridSpec(
            num_scalar_prefetch=1,
            grid=(width // tile,),
            in_specs=[whole, whole, spec(block)],
            out_specs=[spec(n) for n in counts],
            scratch_shapes=[
                pltpu.VMEM((2 * nz, piece, block), jnp.bfloat16),
                pltpu.VMEM((4 * rows, block), jnp.bfloat16),
            ],
        ),
        out_shape=[out(n) for n in counts],
        cost_estimate=pl.CostEstimate(
            flops=8 * rows * width * block,
            bytes_accessed=2 * (4 * rows + block) * width,
            transcendentals=0,
        ),
        name="expand",
    )(where, here, there, proj)


def local_square(nga, W, Pr, kinetic, species_index, coupling):
    bf, f32 = jnp.bfloat16, jnp.float32
    rows, _ = W.shape
    block = Pr.shape[0]
    nz = nga // 2

    band = lax.axis_index("band")
    ga = lax.axis_index("ga")
    core, z = ga % 2, ga // 2
    where = jnp.stack([band, core])

    def band_swap(value, bit):
        return lax.ppermute(value, "band", [(i, i ^ bit) for i in range(4)])

    def ga_swap(value, bit):
        return lax.ppermute(value, "ga", [(i, i ^ bit) for i in range(nga)])

    chunks = chunk_rows(rows, nga)
    matrix = mixing_matrix(species_index, coupling, band * block // NPA, block // NPA)
    clock = [()]

    def now(*values):
        out = lax.optimization_barrier((*values, *clock[0]))
        return out[: len(values)]

    state = [dict() for _ in chunks]
    shared = {"out": jnp.zeros_like(W)}

    def stage_Wd(c, s):
        first, count = chunks[c]
        half = count // 2
        (bands,) = now(W)
        s["own"] = [lax.slice_in_dim(bands, at, at + half, axis=0) for at in (first, first + half)]
        s["x0"] = band_swap(s["own"][0], 1)
        s["y1"] = band_swap(s["own"][1], 2)
        return tuple(s["own"])

    def stage_We(c, s):
        own = now(*s["own"])
        s["x1"] = band_swap(own[1], 1)
        s["y0"] = band_swap(own[0], 2)
        return tuple(own)

    def stage_T(c, s):
        (turned,) = now(Pr)
        shared["turned"] = transpose(turned)
        return (shared["turned"],)

    def stage_Wf(c, s):
        x0, y1 = now(s["x0"], s["y1"])
        s["far0"] = band_swap(x0, 2)
        s["far1"] = band_swap(y1, 1)
        return x0, y1

    def stage_A(c, s):
        x1, y0, far0, far1 = now(s["x1"], s["y0"], s["far0"], s["far1"])
        halves = [*s["own"], s["x0"], x1, y0, s["y1"], far0, far1]
        s["kept"], sent = correlate(where, nz, halves, shared["turned"])
        s["core"] = ga_swap(sent, 1)
        return s["kept"], sent

    def stage_B(c, s):
        (other,) = now(s["core"])
        half = (s["kept"].astype(f32) + other.astype(f32)).astype(bf)
        outs = [
            lax.dynamic_index_in_dim(half, z ^ m, 0, keepdims=False) for m in range(1, nz)
        ]
        s["mine"] = lax.dynamic_index_in_dim(half, z, 0, keepdims=False)
        s["z"] = [ga_swap(out, 2 * m) for m, out in enumerate(outs, 1)]
        return tuple(outs)

    def stage_C(c, s):
        parts = now(*s["z"])
        total = s["mine"].astype(f32)
        for part in parts:
            total = total + part.astype(f32)
        mixed = jnp.dot(total, matrix, precision=lax.Precision.HIGHEST).astype(bf)
        s["mixed"] = [mixed] + [ga_swap(mixed, 2 * m) for m in range(1, nz)]
        return (mixed,)

    def stage_E(c, s):
        parts = list(now(*s["mixed"]))
        bit = 1
        while bit < nz:
            parts = swap(parts, bit, (z & bit) != 0)
            bit *= 2
        s["here"] = jnp.stack(parts)
        s["there"] = ga_swap(s["here"], 1)
        return (s["here"],)

    def stage_G(c, s):
        here, there = now(s["here"], s["there"])
        s["o"] = expand(where, nz, chunks[c][1], here, there, Pr)
        s["first_y"] = band_swap(s["o"][6], 2)
        s["first_x"] = band_swap(s["o"][7], 1)
        return s["o"][6], s["o"][7]

    def stage_K(c, s):
        to_y, to_x = now(s["o"][4], s["o"][3])
        s["near0"] = band_swap(to_y, 2)
        s["near1"] = band_swap(to_x, 1)
        return to_y, to_x

    def stage_H(c, s):
        first_x, first_y = now(s["first_x"], s["first_y"])
        to_x = (s["o"][2].astype(f32) + first_y.astype(f32)).astype(bf)
        to_y = (s["o"][5].astype(f32) + first_x.astype(f32)).astype(bf)
        s["second0"] = band_swap(to_x, 1)
        s["second1"] = band_swap(to_y, 2)
        return to_x, to_y

    def stage_I(c, s):
        parts = now(s["near0"], s["near1"], s["second0"], s["second1"])
        first, count = chunks[c]
        done = []
        for k in range(2):
            own = s["o"][k].astype(f32) + parts[k].astype(f32) + parts[2 + k].astype(f32)
            at = first + k * (count // 2)
            bands = lax.slice_in_dim(W, at, at + count // 2, axis=0).astype(f32)
            done.append((kinetic[None, :] * bands + own).astype(bf))
            shared["out"] = lax.dynamic_update_slice(shared["out"], done[k], (at, 0))
        return tuple(done)

    stages = dict(
        Wd=stage_Wd, We=stage_We, T=stage_T, Wf=stage_Wf, A=stage_A, B=stage_B, C=stage_C,
        E=stage_E, G=stage_G, K=stage_K, H=stage_H, I=stage_I,
    )
    for name, c in stage_order(len(chunks)):
        clock[0] = stages[name](c, state[c])
    return shared["out"]


def solution(mesh):
    in_specs = (P("band", "ga"), P("band", "ga"), P("ga"), P(), P())
    out_specs = P("band", "ga")
    nband, nga = mesh.shape["band"], mesh.shape["ga"]
    square = nband == 4 and nga >= 4 and nga & (nga - 1) == 0

    def local(*args):
        return local_square(nga, *args) if square else local_any(*args)

    def step(*args):
        f = jax.shard_map(
            local, mesh=mesh, in_specs=in_specs, out_specs=out_specs, check_vma=False
        )
        return f(*args)

    return step
```

time: 352 us -> 253 us (0.72)
  waiting for transfers between devices: 304 us -> 91.1 us
  Pallas kernels: 0 us -> 67.7 us
  starting transfers between devices: 0.08 us -> 61.6 us
  matrix products: 30 us -> 4.4 us
  other arithmetic: 4.48 us -> 17.4 us
  between operations: 13.2 us -> 0.41 us
  local copies, waits for them, and re-layouts: 0.24 us -> 9.19 us
    all_gather x1 -> x0, waiting for transfers between devices: 127 us -> none  [local(): lax.all_gather(wavefunctions, 'band', axis=0, tiled=True)]
    reduce_scatter x1 -> x0, waiting for transfers between devices: 120 us -> none  [local(): lax.psum_scatter(jnp.dot(mixed, projectors, preferred_element_type=jnp.fl...]
    ppermute x0 -> x60, waiting for transfers between devices: none -> 91.1 us  [the longest x36 47.8 us: band_swap(): return lax.ppermute(value, 'band', [(i, i ^ bit) for i in range(4)])]
    pallas_call x0 -> x7, Pallas kernels: none -> 67.7 us  [the longest x3 26.9 us: correlate(): pl.pallas_call(functools.partial(correlate_kernel, nz), grid_spec=pltpu.P...]
    ppermute x0 -> x60, starting transfers between devices: none -> 61.6 us  [the longest x36 38.7 us: band_swap(): return lax.ppermute(value, 'band', [(i, i ^ bit) for i in range(4)])]
    psum x1 -> x0, waiting for transfers between devices: 56.1 us -> none  [reduce_and_mix(): lax.psum(partial_value.astype(jnp.bfloat16), 'ga').astype(jnp.float32)]
    dot_general x4, matrix products: 30 us -> 4.4 us  [the longest x3 4.19 us: stage_C(): mixed = jnp.dot(total, matrix, precision=lax.Precision.HIGHEST).astype(bf)]
    dynamic_update_slice x0 -> x5, other arithmetic: none -> 8.65 us  [stage_I(): shared['out'] = lax.dynamic_update_slice(shared['out'], done[k], (at, 0))]
  transfers between devices with their start and end apart: 3 -> 60, of which waited for: 3 -> 25; matrix products, arithmetic and copies ran while one was open for 0% -> 10% of each run, Pallas kernels for 0% -> 24%
where the time goes in v1:
time: 253 us; the launch traced here: 252 us
  waiting for transfers between devices  91.1 us (36%)
  Pallas kernels  67.7 us (27%)
  starting transfers between devices  61.6 us (24%)
  other arithmetic  17.4 us (7%)
  local copies, waits for them, and re-layouts  9.19 us (4%)
  matrix products  4.4 us (2%)
    ppermute x36, waiting for transfers between devices, band_swap(): return lax.ppermute(value, 'band', [(i, i ^ bit) for i in range(4)])  47.8 us
    ppermute x24, waiting for transfers between devices, ga_swap(): return lax.ppermute(value, 'ga', [(i, i ^ bit) for i in range(nga)])  43.3 us
    ppermute x36, starting transfers between devices, band_swap(): return lax.ppermute(value, 'band', [(i, i ^ bit) for i in range(4)])  38.7 us
    pallas_call x3, Pallas kernels, correlate(): pl.pallas_call(functools.partial(correlate_kernel, nz), grid_spec=pltpu.P...  26.9 us
    pallas_call x3, Pallas kernels, expand(): pl.pallas_call(functools.partial(expand_kernel, nz), grid_spec=pltpu.Pref...  26.1 us
    ppermute x24, starting transfers between devices, ga_swap(): return lax.ppermute(value, 'ga', [(i, i ^ bit) for i in range(nga)])  22.9 us
    pallas_call x1, Pallas kernels, transpose(): pl.pallas_call(transpose_kernel, grid=(width // tile,), in_specs=[pl.Bloc...  14.7 us
    dynamic_update_slice x5, other arithmetic, stage_I(): shared['out'] = lax.dynamic_update_slice(shared['out'], done[k], (at, 0))  8.65 us
  transfers between devices with their start and end apart: 60, of which 25 were waited for; matrix products, arithmetic and copies ran while one was open for 10% of the time, Pallas kernels for 24%

profile of v1, /device:TPU:0, one launch (start us, length us, event | category | flops | bytes accessed | tf_op | source)
XLA Modules:
  0.0 251.8 jit_solution(896612911409570332)
XLA Ops:
  0.0 1.9 fusion.65
  1.9 3.0 %collective-permute-start = (bf16[16,12288]{1,0:T(8,128)(2,1)}, bf16[16,12288]{1,0:T(8,128)(2,1)}, u32[]{:S(2)}, u32[]{:S(2)}) collective-permute-start(bf16[16,12288]{1,0:T(8,128)(2,1)} %get-tuple-element.117.refs_0_), channel_id=1, source_target_pairs={{0,8},{8,0},{16,24},{24,16},{1,9},{9,1},{17,25},{25,17},{2,10},{10... | collective-permute-start | bytes 1179656 | tf_op jit(solution)/shard_map/ppermute | solution.py:243
  4.9 1.5 collective-permute-start.3
  8.8 14.7 %transpose.14.refs_8_ = bf16[12288,512]{1,0:T(8,128)(2,1)} custom-call(bf16[512,12288]{1,0:T(8,128)(2,1)} %proj.5), custom_call_target="tpu_custom_call" | custom-call | flops 100663296 | bytes 25165824 | tf_op jit(solution)/shard_map/transpose/pallas_call | solution.py:111
  23.5 2.1 collective-permute-start.4
  25.6 1.5 collective-permute-start.5
  27.1 1.3 fusion.64
  29.7 6.2 %collective-permute-done.4.refs_6_ = bf16[16,12288]{1,0:T(8,128)(2,1)} collective-permute-done((bf16[16,12288]{1,0:T(8,128)(2,1)}, bf16[16,12288]{1,0:T(8,128)(2,1)}, u32[]{:S(2)}, u32[]{:S(2)}) %collective-permute-start.4) | collective-permute-done | bytes 393248 | tf_op jit(solution)/shard_map/ppermute | solution.py:243
  35.9 2.0 collective-permute-done.5.refs_7_
  37.9 8.4 %correlate.3 = (bf16[4,16,512]{2,1,0:T(8,128)(2,1)}, bf16[4,16,512]{2,1,0:T(8,128)(2,1)}) custom-call(s32[2]{0:T(128)} %pad_add_fusion.where, bf16[16,12288]{1,0:T(8,128)(2,1)} %get-tuple-element.117.refs_0_, bf16[16,12288]{1,0:T(8,128)(2,1)} %copy-done.4, bf16[16,12288]{1,0:T(8,128)(2,1)} %collective-permute-done.refs_2_, ...), custom_call_target="tpu_custom_call" | custom-call | flops 1610612736 | bytes 15728640 | tf_op jit(solution)/shard_map/correlate/pallas_call | solution.py:157
  46.4 1.6 collective-permute-start.20
  49.3 1.6 collective-permute-start.7
  51.0 3.6 %collective-permute-done.10.refs_2_ = bf16[32,12288]{1,0:T(8,128)(2,1)} collective-permute-done((bf16[32,12288]{1,0:T(8,128)(2,1)}, bf16[32,12288]{1,0:T(8,128)(2,1)}, u32[]{:S(2)}, u32[]{:S(2)}) %collective-permute-start.10) | collective-permute-done | bytes 786464 | tf_op jit(solution)/shard_map/ppermute | solution.py:243
  54.6 2.6 %collective-permute-start.8 = (bf16[16,512]{1,0:T(8,128)(2,1)S(1)}, bf16[16,512]{1,0:T(8,128)(2,1)S(1)}, u32[]{:S(2)}, u32[]{:S(2)}) collective-permute-start(bf16[16,512]{1,0:T(8,128)(2,1)S(1)} %get-tuple-element.258), channel_id=1, source_target_pairs={{0,4},{1,5},{2,6},{3,7},{4,0},{5,1},{6,2},{7,3},{8,12},{9,13},{10,... | collective-permute-start | bytes 49160 | tf_op jit(solution)/shard_map/ppermute | solution.py:246
  57.2 1.3 collective-permute-start.9
  60.0 1.5 collective-permute-start.23
  61.5 1.2 collective-permute-done.9
  63.9 3.7 %collective-permute-done.12 = bf16[16,512]{1,0:T(8,128)(2,1)S(1)} collective-permute-done((bf16[16,512]{1,0:T(8,128)(2,1)S(1)}, bf16[16,512]{1,0:T(8,128)(2,1)S(1)}, u32[]{:S(2)}, u32[]{:S(2)}) %collective-permute-start.12) | collective-permute-done | bytes 16416 | tf_op jit(solution)/shard_map/ppermute | solution.py:246
  68.2 4.0 %collective-permute-done.13 = bf16[16,512]{1,0:T(8,128)(2,1)S(1)} collective-permute-done((bf16[16,512]{1,0:T(8,128)(2,1)S(1)}, bf16[16,512]{1,0:T(8,128)(2,1)S(1)}, u32[]{:S(2)}, u32[]{:S(2)}) %collective-permute-start.13) | collective-permute-done | bytes 16416 | tf_op jit(solution)/shard_map/ppermute | solution.py:246
  72.3 1.8 collective-permute-start.14
  74.1 3.8 %collective-permute-done.14 = bf16[16,512]{1,0:T(8,128)(2,1)S(1)} collective-permute-done((bf16[16,512]{1,0:T(8,128)(2,1)S(1)}, bf16[16,512]{1,0:T(8,128)(2,1)S(1)}, u32[]{:S(2)}, u32[]{:S(2)}) %collective-permute-start.14) | collective-permute-done | bytes 16416 | tf_op jit(solution)/shard_map/ppermute | solution.py:246
  77.9 1.2 collective-permute-done.15.there
  79.2 1.5 collective-permute-start.25
  80.7 8.1 %expand.3 = (bf16[16,12288]{1,0:T(8,128)(2,1)}, bf16[16,12288]{1,0:T(8,128)(2,1)}, bf16[16,12288]{1,0:T(8,128)(2,1)}, bf16[16,12288]{1,0:T(8,128)(2,1)}, bf16[16...) custom-call(s32[2]{0:T(128)} %pad_add_fusion.where, ...), custom_call_target="tpu_custom_call" | custom-call | flops 1610612736 | bytes 15728640 | tf_op jit(solution)/shard_map/expand/pallas_call | solution.py:209
  89.4 10.0 %correlate.4 = (bf16[4,32,512]{2,1,0:T(8,128)(2,1)}, bf16[4,32,512]{2,1,0:T(8,128)(2,1)}) custom-call(s32[2]{0:T(128)} %pad_add_fusion.where, bf16[32,12288]{1,0:T(8,128)(2,1)} %get-tuple-element.122.refs_0_, bf16[32,12288]{1,0:T(8,128)(2,1)} %get-tuple-element.123.refs_1_, bf16[32,12288]{1,0:T(8,128)(2,1)} %collective-permute-done.10.refs_2_, ...), custom_call_target="tpu_custom_call" | custom-call | flops 3221225472 | bytes 18874368 | tf_op jit(solution)/shard_map/correlate/pallas_call | solution.py:157
  100.2 1.5 collective-permute-start.19
  103.1 2.6 %collective-permute-start.28 = (bf16[32,512]{1,0:T(8,128)(2,1)S(1)}, bf16[32,512]{1,0:T(8,128)(2,1)S(1)}, u32[]{:S(2)}, u32[]{:S(2)}) collective-permute-start(bf16[32,512]{1,0:T(8,128)(2,1)S(1)} %get-tuple-element.244), channel_id=1, source_target_pairs={{0,4},{1,5},{2,6},{3,7},{4,0},{5,1},{6,2},{7,3},{8,12},{9,13},{10,... | collective-permute-start | bytes 98312 | tf_op jit(solution)/shard_map/ppermute | solution.py:246
  105.7 1.5 collective-permute-start.29
  107.2 1.3 collective-permute-done.28
  108.5 2.9 %collective-permute-done.29 = bf16[32,512]{1,0:T(8,128)(2,1)S(1)} collective-permute-done((bf16[32,512]{1,0:T(8,128)(2,1)S(1)}, bf16[32,512]{1,0:T(8,128)(2,1)S(1)}, u32[]{:S(2)}, u32[]{:S(2)}) %collective-permute-start.29) | collective-permute-done | bytes 32800 | tf_op jit(solution)/shard_map/ppermute | solution.py:246
  111.4 1.9 convolution_convert_fusion
  113.4 2.0 collective-permute-start.37
  115.5 2.3 collective-permute-start.38
  119.5 1.6 collective-permute-done.38
  121.3 1.5 collective-permute-start.32
  123.3 1.5 collective-permute-start.34
  126.1 9.8 %expand.4 = (bf16[32,12288]{1,0:T(8,128)(2,1)}, bf16[32,12288]{1,0:T(8,128)(2,1)}, bf16[32,12288]{1,0:T(8,128)(2,1)}, bf16[32,12288]{1,0:T(8,128)(2,1)}, bf16[32...) custom-call(s32[2]{0:T(128)} %pad_add_fusion.where, ...), custom_call_target="tpu_custom_call" | custom-call | flops 3221225472 | bytes 18874368 | tf_op jit(solution)/shard_map/expand/pallas_call | solution.py:209
  135.9 6.8 %collective-permute-done.34.refs_6_ = bf16[16,12288]{1,0:T(8,128)(2,1)} collective-permute-done((bf16[16,12288]{1,0:T(8,128)(2,1)}, bf16[16,12288]{1,0:T(8,128)(2,1)}, u32[]{:S(2)}, u32[]{:S(2)}) %collective-permute-start.34) | collective-permute-done | bytes 393248 | tf_op jit(solution)/shard_map/ppermute | solution.py:243
  142.7 8.4 %correlate.5 = (bf16[4,16,512]{2,1,0:T(8,128)(2,1)}, bf16[4,16,512]{2,1,0:T(8,128)(2,1)}) custom-call(s32[2]{0:T(128)} %pad_add_fusion.where, bf16[16,12288]{1,0:T(8,128)(2,1)} %get-tuple-element.134.refs_0_, bf16[16,12288]{1,0:T(8,128)(2,1)} %get-tuple-element.135.refs_1_, bf16[16,12288]{1,0:T(8,128)(2,1)} %collective-permute-done.25.refs_2_, ...), custom_call_target="tpu_custom_call" | custom-call | flops 1610612736 | bytes 15728640 | tf_op jit(solution)/shard_map/correlate/pallas_call | solution.py:157
  152.7 1.2 collective-permute-start.31
  153.9 1.4 collective-permute-start.30
  156.2 3.7 %collective-permute-done.41 = bf16[16,512]{1,0:T(8,128)(2,1)S(1)} collective-permute-done((bf16[16,512]{1,0:T(8,128)(2,1)S(1)}, bf16[16,512]{1,0:T(8,128)(2,1)S(1)}, u32[]{:S(2)}, u32[]{:S(2)}) %collective-permute-start.41) | collective-permute-done | bytes 16416 | tf_op jit(solution)/shard_map/ppermute | solution.py:246
  160.4 4.2 %collective-permute-done.42 = bf16[16,512]{1,0:T(8,128)(2,1)S(1)} collective-permute-done((bf16[16,512]{1,0:T(8,128)(2,1)S(1)}, bf16[16,512]{1,0:T(8,128)(2,1)S(1)}, u32[]{:S(2)}, u32[]{:S(2)}) %collective-permute-start.42) | collective-permute-done | bytes 16416 | tf_op jit(solution)/shard_map/ppermute | solution.py:246
  164.6 1.9 collective-permute-start.43
  166.5 3.6 %collective-permute-done.43 = bf16[16,512]{1,0:T(8,128)(2,1)S(1)} collective-permute-done((bf16[16,512]{1,0:T(8,128)(2,1)S(1)}, bf16[16,512]{1,0:T(8,128)(2,1)S(1)}, u32[]{:S(2)}, u32[]{:S(2)}) %collective-permute-start.43) | collective-permute-done | bytes 16416 | tf_op jit(solution)/shard_map/ppermute | solution.py:246
  172.8 1.2 collective-permute-start.44
  174.0 1.4 collective-permute-start.45
  175.4 1.2 add_convert_fusion.9
  176.7 1.9 dynamic_update_slice.18
  179.6 11.1 %collective-permute-done.46 = bf16[32,12288]{1,0:T(8,128)(2,1)S(1)} collective-permute-done((bf16[32,12288]{1,0:T(8,128)(2,1)}, bf16[32,12288]{1,0:T(8,128)(2,1)S(1)}, u32[]{:S(2)}, u32[]{:S(2)}) %collective-permute-start.46) | collective-permute-done | bytes 786464 | tf_op jit(solution)/shard_map/ppermute | solution.py:243
  190.8 1.8 collective-permute-done.47
  196.8 3.7 %collective-permute-done.50 = bf16[16,512]{1,0:T(8,128)(2,1)S(1)} collective-permute-done((bf16[16,512]{1,0:T(8,128)(2,1)S(1)}, bf16[16,512]{1,0:T(8,128)(2,1)S(1)}, u32[]{:S(2)}, u32[]{:S(2)}) %collective-permute-start.50) | collective-permute-done | bytes 16416 | tf_op jit(solution)/shard_map/ppermute | solution.py:246
  201.5 3.7 %collective-permute-done.51 = bf16[16,512]{1,0:T(8,128)(2,1)S(1)} collective-permute-done((bf16[16,512]{1,0:T(8,128)(2,1)S(1)}, bf16[16,512]{1,0:T(8,128)(2,1)S(1)}, u32[]{:S(2)}, u32[]{:S(2)}) %collective-permute-start.51) | collective-permute-done | bytes 16416 | tf_op jit(solution)/shard_map/ppermute | solution.py:246
  205.2 2.4 collective-permute-start.52
  207.6 3.2 %collective-permute-done.52 = bf16[16,512]{1,0:T(8,128)(2,1)S(1)} collective-permute-done((bf16[16,512]{1,0:T(8,128)(2,1)S(1)}, bf16[16,512]{1,0:T(8,128)(2,1)S(1)}, u32[]{:S(2)}, u32[]{:S(2)}) %collective-permute-start.52) | collective-permute-done | bytes 16416 | tf_op jit(solution)/shard_map/ppermute | solution.py:246
  210.8 1.2 collective-permute-done.53.there
  212.7 8.2 %expand.5 = (bf16[16,12288]{1,0:T(8,128)(2,1)}, bf16[16,12288]{1,0:T(8,128)(2,1)}, bf16[16,12288]{1,0:T(8,128)(2,1)}, bf16[16,12288]{1,0:T(8,128)(2,1)}, bf16[16...) custom-call(s32[2]{0:T(128)} %pad_add_fusion.where, ...), custom_call_target="tpu_custom_call" | custom-call | flops 1610612736 | bytes 15728640 | tf_op jit(solution)/shard_map/expand/pallas_call | solution.py:209
  225.0 3.0 %constant_dynamic-update-slice_fusion.1 = bf16[128,12288]{1,0:T(8,128)(2,1)} fusion(bf16[128,12288]{1,0:T(8,128)(2,1)} %constant_dynamic-update-slice_fusion.2, bf16[32,12288]{1,0:T(8,128)(2,1)} %collective-permute-done.48, bf16[32,12288]{1,0:T(8,128)(2,1)} %collective-permute-done.44, bf16[32,12288]{1,0:T(8,128)(2,1)} %get-tuple-element.195, ...), kind=kLoop, calls=%fused_computation.109 | loop fusion | flops 3538944 | bytes 3981312 | tf_op jit(solution)/shard_map/dynamic_update_slice | solution.py:351
  228.0 2.8 %constant_dynamic-update-slice_fusion = bf16[128,12288]{1,0:T(8,128)(2,1)} fusion(bf16[128,12288]{1,0:T(8,128)(2,1)} %constant_dynamic-update-slice_fusion.1, bf16[32,12288]{1,0:T(8,128)(2,1)} %collective-permute-done.49, bf16[32,12288]{1,0:T(8,128)(2,1)} %collective-permute-done.45, bf16[32,12288]{1,0:T(8,128)(2,1)S(1)} %copy-done.7, ...), kind=kLoop, calls=%fused_computation.108 | loop fusion | flops 3538944 | bytes 3981312 | tf_op jit(solution)/shard_map/dynamic_update_slice | solution.py:351
  230.8 2.4 collective-permute-done.56
  234.1 1.2 collective-permute-start.59
  235.5 1.5 collective-permute-start.58
  236.9 5.5 %collective-permute-done.54 = bf16[16,12288]{1,0:T(8,128)(2,1)S(1)} collective-permute-done((bf16[16,12288]{1,0:T(8,128)(2,1)}, bf16[16,12288]{1,0:T(8,128)(2,1)S(1)}, u32[]{:S(2)}, u32[]{:S(2)}) %collective-permute-start.54) | collective-permute-done | bytes 393248 | tf_op jit(solution)/shard_map/ppermute | solution.py:243
  242.5 7.3 %collective-permute-done.59 = bf16[16,12288]{1,0:T(8,128)(2,1)S(1)} collective-permute-done((bf16[16,12288]{1,0:T(8,128)(2,1)S(1)}, bf16[16,12288]{1,0:T(8,128)(2,1)S(1)}, u32[]{:S(2)}, u32[]{:S(2)}) %collective-permute-start.59) | collective-permute-done | bytes 393248 | tf_op jit(solution)/shard_map/ppermute | solution.py:243
  (159 shorter events, 34.5 us)
Async XLA Ops:
  1.9 21.6 %collective-permute-start = (bf16[16,12288]{1,0:T(8,128)(2,1)}, bf16[16,12288]{1,0:T(8,128)(2,1)}, u32[]{:S(2)}, u32[]{:S(2)}) collective-permute-start(bf16[16,12288]{1,0:T(8,128)(2,1)} %get-tuple-element.117.refs_0_), channel_id=1, source_target_pairs={{0,8},{8,0},{16,24},{24,16},{1,9},{9,1},{17,25},{25,17},{2,10},{10... | collective-permute-start | bytes 1179656 | tf_op jit(solution)/shard_map/ppermute | solution.py:243
  4.9 18.6 %collective-permute-start.3 = (bf16[16,12288]{1,0:T(8,128)(2,1)S(1)}, bf16[16,12288]{1,0:T(8,128)(2,1)}, u32[]{:S(2)}, u32[]{:S(2)}) collective-permute-start(bf16[16,12288]{1,0:T(8,128)(2,1)S(1)} %get-tuple-element.116.refs_1_), channel_id=1, source_target_pairs={{0,16},{8,24},{16,0},{24,8},{1,17},{9,25},{17,1},{25,9},{2,18},{10... | collective-permute-start | bytes 1179656 | tf_op jit(solution)/shard_map/ppermute | solution.py:243
  6.4 22.5 %collective-permute-start.1 = (bf16[16,12288]{1,0:T(8,128)(2,1)S(1)}, bf16[16,12288]{1,0:T(8,128)(2,1)}, u32[]{:S(2)}, u32[]{:S(2)}) collective-permute-start(bf16[16,12288]{1,0:T(8,128)(2,1)S(1)} %get-tuple-element.116.refs_1_), channel_id=1, source_target_pairs={{0,8},{8,0},{16,24},{24,16},{1,9},{9,1},{17,25},{25,17},{2,10},{10... | collective-permute-start | bytes 1179656 | tf_op jit(solution)/shard_map/ppermute | solution.py:243
  7.0 22.7 %collective-permute-start.2 = (bf16[16,12288]{1,0:T(8,128)(2,1)}, bf16[16,12288]{1,0:T(8,128)(2,1)}, u32[]{:S(2)}, u32[]{:S(2)}) collective-permute-start(bf16[16,12288]{1,0:T(8,128)(2,1)} %get-tuple-element.117.refs_0_), channel_id=1, source_target_pairs={{0,16},{8,24},{16,0},{24,8},{1,17},{9,25},{17,1},{25,9},{2,18},{10... | collective-permute-start | bytes 1179656 | tf_op jit(solution)/shard_map/ppermute | solution.py:243
  23.5 12.4 %collective-permute-start.4 = (bf16[16,12288]{1,0:T(8,128)(2,1)}, bf16[16,12288]{1,0:T(8,128)(2,1)}, u32[]{:S(2)}, u32[]{:S(2)}) collective-permute-start(bf16[16,12288]{1,0:T(8,128)(2,1)} %collective-permute-done.refs_2_), channel_id=1, source_target_pairs={{0,16},{8,24},{16,0},{24,8},{1,17},{9,25},{17,1},{25,9},{2,18},{10... | collective-permute-start | bytes 1179656 | tf_op jit(solution)/shard_map/ppermute | solution.py:243
  25.6 12.3 %collective-permute-start.5 = (bf16[16,12288]{1,0:T(8,128)(2,1)}, bf16[16,12288]{1,0:T(8,128)(2,1)}, u32[]{:S(2)}, u32[]{:S(2)}) collective-permute-start(bf16[16,12288]{1,0:T(8,128)(2,1)} %collective-permute-done.3.refs_5_), channel_id=1, source_target_pairs={{0,8},{8,0},{16,24},{24,16},{1,9},{9,1},{17,25},{25,17},{2,10},{10... | collective-permute-start | bytes 1179656 | tf_op jit(solution)/shard_map/ppermute | solution.py:243
  28.4 26.2 %collective-permute-start.10 = (bf16[32,12288]{1,0:T(8,128)(2,1)}, bf16[32,12288]{1,0:T(8,128)(2,1)}, u32[]{:S(2)}, u32[]{:S(2)}) collective-permute-start(bf16[32,12288]{1,0:T(8,128)(2,1)} %get-tuple-element.122.refs_0_), channel_id=1, source_target_pairs={{0,8},{8,0},{16,24},{24,16},{1,9},{9,1},{17,25},{25,17},{2,10},{10... | collective-permute-start | bytes 2359304 | tf_op jit(solution)/shard_map/ppermute | solution.py:243
  28.9 28.3 %collective-permute-start.11 = (bf16[32,12288]{1,0:T(8,128)(2,1)}, bf16[32,12288]{1,0:T(8,128)(2,1)}, u32[]{:S(2)}, u32[]{:S(2)}) collective-permute-start(bf16[32,12288]{1,0:T(8,128)(2,1)} %get-tuple-element.123.refs_1_), channel_id=1, source_target_pairs={{0,16},{8,24},{16,0},{24,8},{1,17},{9,25},{17,1},{25,9},{2,18},{10... | collective-permute-start | bytes 2359304 | tf_op jit(solution)/shard_map/ppermute | solution.py:243
  46.4 2.1 collective-permute-start.6
  46.4 42.5 %collective-permute-start.20 = (bf16[32,12288]{1,0:T(8,128)(2,1)}, bf16[32,12288]{1,0:T(8,128)(2,1)}, u32[]{:S(2)}, u32[]{:S(2)}) collective-permute-start(bf16[32,12288]{1,0:T(8,128)(2,1)} %get-tuple-element.123.refs_1_), channel_id=1, source_target_pairs={{0,8},{8,0},{16,24},{24,16},{1,9},{9,1},{17,25},{25,17},{2,10},{10... | collective-permute-start | bytes 2359304 | tf_op jit(solution)/shard_map/ppermute | solution.py:243
  48.0 41.5 %collective-permute-start.21 = (bf16[32,12288]{1,0:T(8,128)(2,1)}, bf16[32,12288]{1,0:T(8,128)(2,1)}, u32[]{:S(2)}, u32[]{:S(2)}) collective-permute-start(bf16[32,12288]{1,0:T(8,128)(2,1)} %get-tuple-element.122.refs_0_), channel_id=1, source_target_pairs={{0,16},{8,24},{16,0},{24,8},{1,17},{9,25},{17,1},{25,9},{2,18},{10... | collective-permute-start | bytes 2359304 | tf_op jit(solution)/shard_map/ppermute | solution.py:243
  49.3 10.2 %collective-permute-start.7 = (bf16[16,512]{1,0:T(8,128)(2,1)S(1)}, bf16[16,512]{1,0:T(8,128)(2,1)S(1)}, u32[]{:S(2)}, u32[]{:S(2)}) collective-permute-start(bf16[16,512]{1,0:T(8,128)(2,1)S(1)} %get-tuple-element.259), channel_id=1, source_target_pairs={{0,2},{1,3},{2,0},{3,1},{4,6},{5,7},{6,4},{7,5},{8,10},{9,11},{10,... | collective-permute-start | bytes 49160 | tf_op jit(solution)/shard_map/ppermute | solution.py:246
  54.6 5.4 %collective-permute-start.8 = (bf16[16,512]{1,0:T(8,128)(2,1)S(1)}, bf16[16,512]{1,0:T(8,128)(2,1)S(1)}, u32[]{:S(2)}, u32[]{:S(2)}) collective-permute-start(bf16[16,512]{1,0:T(8,128)(2,1)S(1)} %get-tuple-element.258), channel_id=1, source_target_pairs={{0,4},{1,5},{2,6},{3,7},{4,0},{5,1},{6,2},{7,3},{8,12},{9,13},{10,... | collective-permute-start | bytes 49160 | tf_op jit(solution)/shard_map/ppermute | solution.py:246
  57.2 5.5 %collective-permute-start.9 = (bf16[16,512]{1,0:T(8,128)(2,1)S(1)}, bf16[16,512]{1,0:T(8,128)(2,1)S(1)}, u32[]{:S(2)}, u32[]{:S(2)}) collective-permute-start(bf16[16,512]{1,0:T(8,128)(2,1)S(1)} %get-tuple-element.257), channel_id=1, source_target_pairs={{0,6},{1,7},{2,4},{3,5},{4,2},{5,3},{6,0},{7,1},{8,14},{9,15},{10,... | collective-permute-start | bytes 49160 | tf_op jit(solution)/shard_map/ppermute | solution.py:246
  59.5 29.9 %collective-permute-start.22 = (bf16[32,12288]{1,0:T(8,128)(2,1)}, bf16[32,12288]{1,0:T(8,128)(2,1)}, u32[]{:S(2)}, u32[]{:S(2)}) collective-permute-start(bf16[32,12288]{1,0:T(8,128)(2,1)} %collective-permute-done.10.refs_2_), channel_id=1, source_target_pairs={{0,16},{8,24},{16,0},{24,8},{1,17},{9,25},{17,1},{25,9},{2,18},{10... | collective-permute-start | bytes 2359304 | tf_op jit(solution)/shard_map/ppermute | solution.py:243
  60.0 29.4 %collective-permute-start.23 = (bf16[32,12288]{1,0:T(8,128)(2,1)}, bf16[32,12288]{1,0:T(8,128)(2,1)}, u32[]{:S(2)}, u32[]{:S(2)}) collective-permute-start(bf16[32,12288]{1,0:T(8,128)(2,1)} %collective-permute-done.11.refs_5_), channel_id=1, source_target_pairs={{0,8},{8,0},{16,24},{24,16},{1,9},{9,1},{17,25},{25,17},{2,10},{10... | collective-permute-start | bytes 2359304 | tf_op jit(solution)/shard_map/ppermute | solution.py:243
  63.9 3.8 %collective-permute-start.12 = (bf16[16,512]{1,0:T(8,128)(2,1)S(1)}, bf16[16,512]{1,0:T(8,128)(2,1)S(1)}, u32[]{:S(2)}, u32[]{:S(2)}) collective-permute-start(bf16[16,512]{1,0:T(8,128)(2,1)S(1)} %convolution_convert_fusion.2), channel_id=1, source_target_pairs={{0,2},{1,3},{2,0},{3,1},{4,6},{5,7},{6,4},{7,5},{8,10},{9,11},{10,... | collective-permute-start | bytes 49160 | tf_op jit(solution)/shard_map/ppermute | solution.py:246
  67.6 4.6 %collective-permute-start.13 = (bf16[16,512]{1,0:T(8,128)(2,1)S(1)}, bf16[16,512]{1,0:T(8,128)(2,1)S(1)}, u32[]{:S(2)}, u32[]{:S(2)}) collective-permute-start(bf16[16,512]{1,0:T(8,128)(2,1)S(1)} %convolution_convert_fusion.2), channel_id=1, source_target_pairs={{0,4},{1,5},{2,6},{3,7},{4,0},{5,1},{6,2},{7,3},{8,12},{9,13},{10,... | collective-permute-start | bytes 49160 | tf_op jit(solution)/shard_map/ppermute | solution.py:246
  72.3 5.5 %collective-permute-start.14 = (bf16[16,512]{1,0:T(8,128)(2,1)S(1)}, bf16[16,512]{1,0:T(8,128)(2,1)S(1)}, u32[]{:S(2)}, u32[]{:S(2)}) collective-permute-start(bf16[16,512]{1,0:T(8,128)(2,1)S(1)} %convolution_convert_fusion.2), channel_id=1, source_target_pairs={{0,6},{1,7},{2,4},{3,5},{4,2},{5,3},{6,0},{7,1},{8,14},{9,15},{10,... | collective-permute-start | bytes 49160 | tf_op jit(solution)/shard_map/ppermute | solution.py:246
  77.9 1.3 collective-permute-start.15
  79.2 22.6 %collective-permute-start.25 = (bf16[16,12288]{1,0:T(8,128)(2,1)}, bf16[16,12288]{1,0:T(8,128)(2,1)}, u32[]{:S(2)}, u32[]{:S(2)}) collective-permute-start(bf16[16,12288]{1,0:T(8,128)(2,1)} %get-tuple-element.134.refs_0_), channel_id=1, source_target_pairs={{0,8},{8,0},{16,24},{24,16},{1,9},{9,1},{17,25},{25,17},{2,10},{10... | collective-permute-start | bytes 1179656 | tf_op jit(solution)/shard_map/ppermute | solution.py:243
  88.9 12.9 %collective-permute-start.26 = (bf16[16,12288]{1,0:T(8,128)(2,1)}, bf16[16,12288]{1,0:T(8,128)(2,1)}, u32[]{:S(2)}, u32[]{:S(2)}) collective-permute-start(bf16[16,12288]{1,0:T(8,128)(2,1)} %get-tuple-element.135.refs_1_), channel_id=1, source_target_pairs={{0,16},{8,24},{16,0},{24,8},{1,17},{9,25},{17,1},{25,9},{2,18},{10... | collective-permute-start | bytes 1179656 | tf_op jit(solution)/shard_map/ppermute | solution.py:243
  99.5 2.3 collective-permute-start.24
  99.5 18.3 %collective-permute-start.18 = (bf16[16,12288]{1,0:T(8,128)(2,1)}, bf16[16,12288]{1,0:T(8,128)(2,1)S(1)}, u32[]{:S(2)}, u32[]{:S(2)}) collective-permute-start(bf16[16,12288]{1,0:T(8,128)(2,1)} %get-tuple-element.149), channel_id=1, source_target_pairs={{0,8},{8,0},{16,24},{24,16},{1,9},{9,1},{17,25},{25,17},{2,10},{10... | collective-permute-start | bytes 1179656 | tf_op jit(solution)/shard_map/ppermute | solution.py:243
  100.2 17.6 %collective-permute-start.19 = (bf16[16,12288]{1,0:T(8,128)(2,1)}, bf16[16,12288]{1,0:T(8,128)(2,1)S(1)}, u32[]{:S(2)}, u32[]{:S(2)}) collective-permute-start(bf16[16,12288]{1,0:T(8,128)(2,1)} %get-tuple-element.148), channel_id=1, source_target_pairs={{0,16},{8,24},{16,0},{24,8},{1,17},{9,25},{17,1},{25,9},{2,18},{10... | collective-permute-start | bytes 1179656 | tf_op jit(solution)/shard_map/ppermute | solution.py:243
  102.7 4.5 %collective-permute-start.27 = (bf16[32,512]{1,0:T(8,128)(2,1)S(1)}, bf16[32,512]{1,0:T(8,128)(2,1)S(1)}, u32[]{:S(2)}, u32[]{:S(2)}) collective-permute-start(bf16[32,512]{1,0:T(8,128)(2,1)S(1)} %get-tuple-element.245), channel_id=1, source_target_pairs={{0,2},{1,3},{2,0},{3,1},{4,6},{5,7},{6,4},{7,5},{8,10},{9,11},{10,... | collective-permute-start | bytes 98312 | tf_op jit(solution)/shard_map/ppermute | solution.py:246
  103.1 5.4 %collective-permute-start.28 = (bf16[32,512]{1,0:T(8,128)(2,1)S(1)}, bf16[32,512]{1,0:T(8,128)(2,1)S(1)}, u32[]{:S(2)}, u32[]{:S(2)}) collective-permute-start(bf16[32,512]{1,0:T(8,128)(2,1)S(1)} %get-tuple-element.244), channel_id=1, source_target_pairs={{0,4},{1,5},{2,6},{3,7},{4,0},{5,1},{6,2},{7,3},{8,12},{9,13},{10,... | collective-permute-start | bytes 98312 | tf_op jit(solution)/shard_map/ppermute | solution.py:246
  105.7 5.7 %collective-permute-start.29 = (bf16[32,512]{1,0:T(8,128)(2,1)S(1)}, bf16[32,512]{1,0:T(8,128)(2,1)S(1)}, u32[]{:S(2)}, u32[]{:S(2)}) collective-permute-start(bf16[32,512]{1,0:T(8,128)(2,1)S(1)} %get-tuple-element.243), channel_id=1, source_target_pairs={{0,6},{1,7},{2,4},{3,5},{4,2},{5,3},{6,0},{7,1},{8,14},{9,15},{10,... | collective-permute-start | bytes 98312 | tf_op jit(solution)/shard_map/ppermute | solution.py:246
  113.4 6.2 %collective-permute-start.36 = (bf16[32,512]{1,0:T(8,128)(2,1)S(1)}, bf16[32,512]{1,0:T(8,128)(2,1)S(1)}, u32[]{:S(2)}, u32[]{:S(2)}) collective-permute-start(bf16[32,512]{1,0:T(8,128)(2,1)S(1)} %convolution_convert_fusion), channel_id=1, source_target_pairs={{0,2},{1,3},{2,0},{3,1},{4,6},{5,7},{6,4},{7,5},{8,10},{9,11},{10,... | collective-permute-start | bytes 98312 | tf_op jit(solution)/shard_map/ppermute | solution.py:246
  113.4 6.1 %collective-permute-start.37 = (bf16[32,512]{1,0:T(8,128)(2,1)S(1)}, bf16[32,512]{1,0:T(8,128)(2,1)S(1)}, u32[]{:S(2)}, u32[]{:S(2)}) collective-permute-start(bf16[32,512]{1,0:T(8,128)(2,1)S(1)} %convolution_convert_fusion), channel_id=1, source_target_pairs={{0,4},{1,5},{2,6},{3,7},{4,0},{5,1},{6,2},{7,3},{8,12},{9,13},{10,... | collective-permute-start | bytes 98312 | tf_op jit(solution)/shard_map/ppermute | solution.py:246
  115.5 5.7 %collective-permute-start.38 = (bf16[32,512]{1,0:T(8,128)(2,1)S(1)}, bf16[32,512]{1,0:T(8,128)(2,1)S(1)}, u32[]{:S(2)}, u32[]{:S(2)}) collective-permute-start(bf16[32,512]{1,0:T(8,128)(2,1)S(1)} %convolution_convert_fusion), channel_id=1, source_target_pairs={{0,6},{1,7},{2,4},{3,5},{4,2},{5,3},{6,0},{7,1},{8,14},{9,15},{10,... | collective-permute-start | bytes 98312 | tf_op jit(solution)/shard_map/ppermute | solution.py:246
  121.2 4.2 %collective-permute-start.39 = (bf16[4,32,512]{2,1,0:T(8,128)(2,1)S(1)}, bf16[4,32,512]{2,1,0:T(8,128)(2,1)S(1)}, u32[]{:S(2)}, u32[]{:S(2)}) collective-permute-start(bf16[4,32,512]{2,1,0:T(8,128)(2,1)S(1)} %pad_maximum_fusion.here), channel_id=1, source_target_pairs={{0,1},{1,0},{2,3},{3,2},{4,5},{5,4},{6,7},{7,6},{8,9},{9,8},{10,11... | collective-permute-start | bytes 393224 | tf_op jit(solution)/shard_map/ppermute | solution.py:246
  121.3 14.6 %collective-permute-start.32 = (bf16[16,12288]{1,0:T(8,128)(2,1)}, bf16[16,12288]{1,0:T(8,128)(2,1)}, u32[]{:S(2)}, u32[]{:S(2)}) collective-permute-start(bf16[16,12288]{1,0:T(8,128)(2,1)} %get-tuple-element.135.refs_1_), channel_id=1, source_target_pairs={{0,8},{8,0},{16,24},{24,16},{1,9},{9,1},{17,25},{25,17},{2,10},{10... | collective-permute-start | bytes 1179656 | tf_op jit(solution)/shard_map/ppermute | solution.py:243
  122.8 13.1 %collective-permute-start.33 = (bf16[16,12288]{1,0:T(8,128)(2,1)}, bf16[16,12288]{1,0:T(8,128)(2,1)}, u32[]{:S(2)}, u32[]{:S(2)}) collective-permute-start(bf16[16,12288]{1,0:T(8,128)(2,1)} %get-tuple-element.134.refs_0_), channel_id=1, source_target_pairs={{0,16},{8,24},{16,0},{24,8},{1,17},{9,25},{17,1},{25,9},{2,18},{10... | collective-permute-start | bytes 1179656 | tf_op jit(solution)/shard_map/ppermute | solution.py:243
  123.3 19.4 %collective-permute-start.34 = (bf16[16,12288]{1,0:T(8,128)(2,1)}, bf16[16,12288]{1,0:T(8,128)(2,1)}, u32[]{:S(2)}, u32[]{:S(2)}) collective-permute-start(bf16[16,12288]{1,0:T(8,128)(2,1)} %collective-permute-done.25.refs_2_), channel_id=1, source_target_pairs={{0,16},{8,24},{16,0},{24,8},{1,17},{9,25},{17,1},{25,9},{2,18},{10... | collective-permute-start | bytes 1179656 | tf_op jit(solution)/shard_map/ppermute | solution.py:243
  124.8 17.9 %collective-permute-start.35 = (bf16[16,12288]{1,0:T(8,128)(2,1)}, bf16[16,12288]{1,0:T(8,128)(2,1)}, u32[]{:S(2)}, u32[]{:S(2)}) collective-permute-start(bf16[16,12288]{1,0:T(8,128)(2,1)} %collective-permute-done.26.refs_5_), channel_id=1, source_target_pairs={{0,8},{8,0},{16,24},{24,16},{1,9},{9,1},{17,25},{25,17},{2,10},{10... | collective-permute-start | bytes 1179656 | tf_op jit(solution)/shard_map/ppermute | solution.py:243
  135.9 34.9 %copy-start.24 = (s32[512]{0:T(512)S(1)}, s32[512]{0:T(512)}, u32[]{:S(2)}) copy-start(s32[512]{0:T(512)} %copy-done.23) | copy-start | bytes 6148
  135.9 34.9 %copy-start.26 = (s32[512]{0:T(512)S(1)}, s32[512]{0:T(512)}, u32[]{:S(2)}) copy-start(s32[512]{0:T(512)} %copy-done.25) | copy-start | bytes 6148
  135.9 34.9 %copy-start.28 = (pred[512]{0:T(512)(128)(4,1)S(1)}, pred[512]{0:T(512)(128)(4,1)}, u32[]{:S(2)}) copy-start(pred[512]{0:T(512)(128)(4,1)} %copy-done.27) | copy-start | bytes 1540
  135.9 39.5 %copy-start.3 = (f32[12288]{0:T(1024)S(1)}, f32[12288]{0:T(1024)}, u32[]{:S(2)}) copy-start(f32[12288]{0:T(1024)} %param.7) | copy-start | bytes 147460
  151.1 4.1 %collective-permute-start.40 = (bf16[4,16,512]{2,1,0:T(8,128)(2,1)}, bf16[4,16,512]{2,1,0:T(8,128)(2,1)S(1)}, u32[]{:S(2)}, u32[]{:S(2)}) collective-permute-start(bf16[4,16,512]{2,1,0:T(8,128)(2,1)} %get-tuple-element.185), channel_id=1, source_target_pairs={{0,1},{1,0},{2,3},{3,2},{4,5},{5,4},{6,7},{7,6},{8,9},{9,8},{10,11... | collective-permute-start | bytes 196616 | tf_op jit(solution)/shard_map/ppermute | solution.py:246
  151.1 20.8 %collective-permute-start.16 = (bf16[16,12288]{1,0:T(8,128)(2,1)}, bf16[16,12288]{1,0:T(8,128)(2,1)S(1)}, u32[]{:S(2)}, u32[]{:S(2)}) collective-permute-start(bf16[16,12288]{1,0:T(8,128)(2,1)} %get-tuple-element.150), channel_id=1, source_target_pairs={{0,16},{8,24},{16,0},{24,8},{1,17},{9,25},{17,1},{25,9},{2,18},{10... | collective-permute-start | bytes 1179656 | tf_op jit(solution)/shard_map/ppermute | solution.py:243
  151.7 21.1 %collective-permute-start.17 = (bf16[16,12288]{1,0:T(8,128)(2,1)}, bf16[16,12288]{1,0:T(8,128)(2,1)S(1)}, u32[]{:S(2)}, u32[]{:S(2)}) collective-permute-start(bf16[16,12288]{1,0:T(8,128)(2,1)} %get-tuple-element.151), channel_id=1, source_target_pairs={{0,8},{8,0},{16,24},{24,16},{1,9},{9,1},{17,25},{25,17},{2,10},{10... | collective-permute-start | bytes 1179656 | tf_op jit(solution)/shard_map/ppermute | solution.py:243
  152.7 21.3 %collective-permute-start.31 = (bf16[16,12288]{1,0:T(8,128)(2,1)}, bf16[16,12288]{1,0:T(8,128)(2,1)S(1)}, u32[]{:S(2)}, u32[]{:S(2)}) collective-permute-start(bf16[16,12288]{1,0:T(8,128)(2,1)} %add_convert_fusion.10), channel_id=1, source_target_pairs={{0,16},{8,24},{16,0},{24,8},{1,17},{9,25},{17,1},{25,9},{2,18},{10... | collective-permute-start | bytes 1179656 | tf_op jit(solution)/shard_map/ppermute | solution.py:243
  153.9 21.6 %collective-permute-start.30 = (bf16[16,12288]{1,0:T(8,128)(2,1)}, bf16[16,12288]{1,0:T(8,128)(2,1)S(1)}, u32[]{:S(2)}, u32[]{:S(2)}) collective-permute-start(bf16[16,12288]{1,0:T(8,128)(2,1)} %add_convert_fusion.11), channel_id=1, source_target_pairs={{0,8},{8,0},{16,24},{24,16},{1,9},{9,1},{17,25},{25,17},{2,10},{10... | collective-permute-start | bytes 1179656 | tf_op jit(solution)/shard_map/ppermute | solution.py:243
  156.1 3.8 %collective-permute-start.41 = (bf16[16,512]{1,0:T(8,128)(2,1)S(1)}, bf16[16,512]{1,0:T(8,128)(2,1)S(1)}, u32[]{:S(2)}, u32[]{:S(2)}) collective-permute-start(bf16[16,512]{1,0:T(8,128)(2,1)S(1)} %get-tuple-element.252), channel_id=1, source_target_pairs={{0,2},{1,3},{2,0},{3,1},{4,6},{5,7},{6,4},{7,5},{8,10},{9,11},{10,... | collective-permute-start | bytes 49160 | tf_op jit(solution)/shard_map/ppermute | solution.py:246
  160.0 4.6 %collective-permute-start.42 = (bf16[16,512]{1,0:T(8,128)(2,1)S(1)}, bf16[16,512]{1,0:T(8,128)(2,1)S(1)}, u32[]{:S(2)}, u32[]{:S(2)}) collective-permute-start(bf16[16,512]{1,0:T(8,128)(2,1)S(1)} %get-tuple-element.251), channel_id=1, source_target_pairs={{0,4},{1,5},{2,6},{3,7},{4,0},{5,1},{6,2},{7,3},{8,12},{9,13},{10,... | collective-permute-start | bytes 49160 | tf_op jit(solution)/shard_map/ppermute | solution.py:246
  164.6 5.5 %collective-permute-start.43 = (bf16[16,512]{1,0:T(8,128)(2,1)S(1)}, bf16[16,512]{1,0:T(8,128)(2,1)S(1)}, u32[]{:S(2)}, u32[]{:S(2)}) collective-permute-start(bf16[16,512]{1,0:T(8,128)(2,1)S(1)} %get-tuple-element.250), channel_id=1, source_target_pairs={{0,6},{1,7},{2,4},{3,5},{4,2},{5,3},{6,0},{7,1},{8,14},{9,15},{10,... | collective-permute-start | bytes 49160 | tf_op jit(solution)/shard_map/ppermute | solution.py:246
  170.1 20.6 %collective-permute-start.46 = (bf16[32,12288]{1,0:T(8,128)(2,1)}, bf16[32,12288]{1,0:T(8,128)(2,1)S(1)}, u32[]{:S(2)}, u32[]{:S(2)}) collective-permute-start(bf16[32,12288]{1,0:T(8,128)(2,1)} %get-tuple-element.177), channel_id=1, source_target_pairs={{0,8},{8,0},{16,24},{24,16},{1,9},{9,1},{17,25},{25,17},{2,10},{10... | collective-permute-start | bytes 2359304 | tf_op jit(solution)/shard_map/ppermute | solution.py:243
  171.9 20.7 %collective-permute-start.47 = (bf16[32,12288]{1,0:T(8,128)(2,1)}, bf16[32,12288]{1,0:T(8,128)(2,1)S(1)}, u32[]{:S(2)}, u32[]{:S(2)}) collective-permute-start(bf16[32,12288]{1,0:T(8,128)(2,1)} %get-tuple-element.176), channel_id=1, source_target_pairs={{0,16},{8,24},{16,0},{24,8},{1,17},{9,25},{17,1},{25,9},{2,18},{10... | collective-permute-start | bytes 2359304 | tf_op jit(solution)/shard_map/ppermute | solution.py:243
  172.8 49.0 %collective-permute-start.44 = (bf16[32,12288]{1,0:T(8,128)(2,1)}, bf16[32,12288]{1,0:T(8,128)(2,1)}, u32[]{:S(2)}, u32[]{:S(2)}) collective-permute-start(bf16[32,12288]{1,0:T(8,128)(2,1)} %get-tuple-element.178), channel_id=1, source_target_pairs={{0,16},{8,24},{16,0},{24,8},{1,17},{9,25},{17,1},{25,9},{2,18},{10... | collective-permute-start | bytes 2359304 | tf_op jit(solution)/shard_map/ppermute | solution.py:243
  174.0 49.0 %collective-permute-start.45 = (bf16[32,12288]{1,0:T(8,128)(2,1)}, bf16[32,12288]{1,0:T(8,128)(2,1)}, u32[]{:S(2)}, u32[]{:S(2)}) collective-permute-start(bf16[32,12288]{1,0:T(8,128)(2,1)} %get-tuple-element.179), channel_id=1, source_target_pairs={{0,8},{8,0},{16,24},{24,16},{1,9},{9,1},{17,25},{25,17},{2,10},{10... | collective-permute-start | bytes 2359304 | tf_op jit(solution)/shard_map/ppermute | solution.py:243
  193.7 30.2 %collective-permute-start.49 = (bf16[32,12288]{1,0:T(8,128)(2,1)}, bf16[32,12288]{1,0:T(8,128)(2,1)}, u32[]{:S(2)}, u32[]{:S(2)}) collective-permute-start(bf16[32,12288]{1,0:T(8,128)(2,1)} %add_convert_fusion.2), channel_id=1, source_target_pairs={{0,16},{8,24},{16,0},{24,8},{1,17},{9,25},{17,1},{25,9},{2,18},{10... | collective-permute-start | bytes 2359304 | tf_op jit(solution)/shard_map/ppermute | solution.py:243
  195.6 29.4 %collective-permute-start.48 = (bf16[32,12288]{1,0:T(8,128)(2,1)}, bf16[32,12288]{1,0:T(8,128)(2,1)}, u32[]{:S(2)}, u32[]{:S(2)}) collective-permute-start(bf16[32,12288]{1,0:T(8,128)(2,1)} %add_convert_fusion.3), channel_id=1, source_target_pairs={{0,8},{8,0},{16,24},{24,16},{1,9},{9,1},{17,25},{25,17},{2,10},{10... | collective-permute-start | bytes 2359304 | tf_op jit(solution)/shard_map/ppermute | solution.py:243
  196.8 3.7 %collective-permute-start.50 = (bf16[16,512]{1,0:T(8,128)(2,1)S(1)}, bf16[16,512]{1,0:T(8,128)(2,1)S(1)}, u32[]{:S(2)}, u32[]{:S(2)}) collective-permute-start(bf16[16,512]{1,0:T(8,128)(2,1)S(1)} %convolution_convert_fusion.1), channel_id=1, source_target_pairs={{0,2},{1,3},{2,0},{3,1},{4,6},{5,7},{6,4},{7,5},{8,10},{9,11},{10,... | collective-permute-start | bytes 49160 | tf_op jit(solution)/shard_map/ppermute | solution.py:246
  200.5 4.6 %collective-permute-start.51 = (bf16[16,512]{1,0:T(8,128)(2,1)S(1)}, bf16[16,512]{1,0:T(8,128)(2,1)S(1)}, u32[]{:S(2)}, u32[]{:S(2)}) collective-permute-start(bf16[16,512]{1,0:T(8,128)(2,1)S(1)} %convolution_convert_fusion.1), channel_id=1, source_target_pairs={{0,4},{1,5},{2,6},{3,7},{4,0},{5,1},{6,2},{7,3},{8,12},{9,13},{10,... | collective-permute-start | bytes 49160 | tf_op jit(solution)/shard_map/ppermute | solution.py:246
  205.2 5.5 %collective-permute-start.52 = (bf16[16,512]{1,0:T(8,128)(2,1)S(1)}, bf16[16,512]{1,0:T(8,128)(2,1)S(1)}, u32[]{:S(2)}, u32[]{:S(2)}) collective-permute-start(bf16[16,512]{1,0:T(8,128)(2,1)S(1)} %convolution_convert_fusion.1), channel_id=1, source_target_pairs={{0,6},{1,7},{2,4},{3,5},{4,2},{5,3},{6,0},{7,1},{8,14},{9,15},{10,... | collective-permute-start | bytes 49160 | tf_op jit(solution)/shard_map/ppermute | solution.py:246
  210.8 1.3 collective-permute-start.53
  220.9 12.3 %collective-permute-start.56 = (bf16[16,12288]{1,0:T(8,128)(2,1)}, bf16[16,12288]{1,0:T(8,128)(2,1)S(1)}, u32[]{:S(2)}, u32[]{:S(2)}) collective-permute-start(bf16[16,12288]{1,0:T(8,128)(2,1)} %get-tuple-element.209), channel_id=1, source_target_pairs={{0,8},{8,0},{16,24},{24,16},{1,9},{9,1},{17,25},{25,17},{2,10},{10... | collective-permute-start | bytes 1179656 | tf_op jit(solution)/shard_map/ppermute | solution.py:243
  221.8 12.2 %collective-permute-start.57 = (bf16[16,12288]{1,0:T(8,128)(2,1)}, bf16[16,12288]{1,0:T(8,128)(2,1)S(1)}, u32[]{:S(2)}, u32[]{:S(2)}) collective-permute-start(bf16[16,12288]{1,0:T(8,128)(2,1)} %get-tuple-element.208), channel_id=1, source_target_pairs={{0,16},{8,24},{16,0},{24,8},{1,17},{9,25},{17,1},{25,9},{2,18},{10... | collective-permute-start | bytes 1179656 | tf_op jit(solution)/shard_map/ppermute | solution.py:243
  223.0 19.5 %collective-permute-start.54 = (bf16[16,12288]{1,0:T(8,128)(2,1)}, bf16[16,12288]{1,0:T(8,128)(2,1)S(1)}, u32[]{:S(2)}, u32[]{:S(2)}) collective-permute-start(bf16[16,12288]{1,0:T(8,128)(2,1)} %get-tuple-element.210), channel_id=1, source_target_pairs={{0,16},{8,24},{16,0},{24,8},{1,17},{9,25},{17,1},{25,9},{2,18},{10... | collective-permute-start | bytes 1179656 | tf_op jit(solution)/shard_map/ppermute | solution.py:243
  223.9 18.6 %collective-permute-start.55 = (bf16[16,12288]{1,0:T(8,128)(2,1)}, bf16[16,12288]{1,0:T(8,128)(2,1)S(1)}, u32[]{:S(2)}, u32[]{:S(2)}) collective-permute-start(bf16[16,12288]{1,0:T(8,128)(2,1)} %get-tuple-element.211), channel_id=1, source_target_pairs={{0,8},{8,0},{16,24},{24,16},{1,9},{9,1},{17,25},{25,17},{2,10},{10... | collective-permute-start | bytes 1179656 | tf_op jit(solution)/shard_map/ppermute | solution.py:243
  234.1 15.7 %collective-permute-start.59 = (bf16[16,12288]{1,0:T(8,128)(2,1)S(1)}, bf16[16,12288]{1,0:T(8,128)(2,1)S(1)}, u32[]{:S(2)}, u32[]{:S(2)}) collective-permute-start(bf16[16,12288]{1,0:T(8,128)(2,1)S(1)} %add_convert_fusion.6), channel_id=1, source_target_pairs={{0,16},{8,24},{16,0},{24,8},{1,17},{9,25},{17,1},{25,9},{2,18},{10... | collective-permute-start | bytes 1179656 | tf_op jit(solution)/shard_map/ppermute | solution.py:243
  235.5 14.3 %collective-permute-start.58 = (bf16[16,12288]{1,0:T(8,128)(2,1)S(1)}, bf16[16,12288]{1,0:T(8,128)(2,1)S(1)}, u32[]{:S(2)}, u32[]{:S(2)}) collective-permute-start(bf16[16,12288]{1,0:T(8,128)(2,1)S(1)} %add_convert_fusion.7), channel_id=1, source_target_pairs={{0,8},{8,0},{16,24},{24,16},{1,9},{9,1},{17,25},{25,17},{2,10},{10... | collective-permute-start | bytes 1179656 | tf_op jit(solution)/shard_map/ppermute | solution.py:243
  (25 other events, 378.3 us)

commit v2 on v1

--- a/solution.py
+++ b/solution.py
@@ -72,16 +72,17 @@
     unit = max(32, ga * 4)
     if rows % (4 * unit):
         return [(0, rows)]
-    return [(0, rows // 4), (rows // 4, rows // 2), (3 * rows // 4, rows // 4)]
+    return [(rows // 2, rows // 4), (0, rows // 2), (3 * rows // 4, rows // 4)]
 
 
 def stage_order(n):
-    order = [("Wd", 0), ("We", 0), ("T", 0), ("Wf", 0), ("Wd", 1), ("We", 1), ("A", 0), ("B", 0)]
-    order += [("Wf", 1), ("Wd", 2), ("We", 2)]
+    order = [("Wd", 0), ("We", 0), ("T", 0), ("Wf", 0), ("Wd", 1), ("We", 1), ("M", 0)]
+    order += [("A", 0), ("B", 0), ("Wf", 1), ("Wd", 2), ("We", 2)]
     for c in range(n):
         order += [("A", c), ("Wf", c + 1), ("B", c), ("C", c)]
-        order += [("I", c - 2), ("H", c - 1), ("E", c), ("G", c), ("K", c), ("Wd", c + 3), ("We", c + 3)]
-    order += [("I", n - 2), ("H", n - 1), ("I", n - 1)]
+        order += [("H", c - 1), ("E", c), ("G", c), ("K", c), ("Wd", c + 3), ("We", c + 3)]
+    order += [("I", c) for c in range(n - 1)]
+    order += [("H", n - 1), ("I", n - 1)]
     seen, kept = set(), []
     for item in order:
         if 0 <= item[1] < n and item not in seen:
@@ -119,6 +120,88 @@
         ),
         name="transpose",
     )(value)
+
+
+def halves_kernel(value, first, second):
+    half = first.shape[0]
+    first[...] = value[:half]
+    second[...] = value[half:]
+
+
+def take_halves(value, first, count):
+    width = value.shape[1]
+    tile = tile_of(width, 2)
+    return pl.pallas_call(
+        halves_kernel,
+        grid=(width // tile,),
+        in_specs=[pl.BlockSpec((count, tile), lambda k: (first // count, k))],
+        out_specs=[pl.BlockSpec((count // 2, tile), lambda k: (0, k))] * 2,
+        out_shape=[jax.ShapeDtypeStruct((count // 2, width), value.dtype)] * 2,
+        cost_estimate=pl.CostEstimate(
+            flops=count * width, bytes_accessed=4 * count * width, transcendentals=0
+        ),
+        name="take",
+    )(value)
+
+
+def join_kernel(a, b, c, d, first, second):
+    f32 = jnp.float32
+    first[...] = (a[...].astype(f32) + b[...].astype(f32)).astype(first.dtype)
+    second[...] = (c[...].astype(f32) + d[...].astype(f32)).astype(second.dtype)
+
+
+def join(a, b, c, d):
+    half, width = a.shape
+    tile = tile_of(width, 2)
+    spec = pl.BlockSpec((half, tile), lambda k: (0, k))
+    return pl.pallas_call(
+        join_kernel,
+        grid=(width // tile,),
+        in_specs=[spec] * 4,
+        out_specs=[spec] * 2,
+        out_shape=[jax.ShapeDtypeStruct(a.shape, a.dtype)] * 2,
+        cost_estimate=pl.CostEstimate(
+            flops=2 * half * width, bytes_accessed=12 * half * width, transcendentals=0
+        ),
+        name="join",
+    )(a, b, c, d)
+
+
+def finish_kernel(bands, kinetic, *refs):
+    terms, out = refs[:6], refs[-1]
+    half = terms[0].shape[0]
+    f32 = jnp.float32
+    for k in range(2):
+        rows = slice(k * half, (k + 1) * half)
+        own = sum(term[...].astype(f32) for term in terms[k::2])
+        out[rows] = (kinetic[...] * bands[rows].astype(f32) + own).astype(out.dtype)
+
+
+def finish(bands, kinetic, terms, first, out):
+    half, width = terms[0].shape
+    count = 2 * half
+    tile = tile_of(width, 2)
+    rows = pl.BlockSpec((count, tile), lambda k: (first // count, k))
+    part = pl.BlockSpec((half, tile), lambda k: (0, k))
+    args = [bands, kinetic[None, :], *terms]
+    specs = [rows, pl.BlockSpec((1, tile), lambda k: (0, k))] + [part] * 6
+    aliases = {}
+    if out is not None:
+        aliases = {len(args): 0}
+        args.append(out)
+        specs.append(pl.BlockSpec(memory_space=pl.ANY))
+    return pl.pallas_call(
+        finish_kernel,
+        grid=(width // tile,),
+        in_specs=specs,
+        out_specs=rows,
+        out_shape=jax.ShapeDtypeStruct(bands.shape, bands.dtype),
+        input_output_aliases=aliases,
+        cost_estimate=pl.CostEstimate(
+            flops=8 * count * width, bytes_accessed=10 * count * width, transcendentals=0
+        ),
+        name="finish",
+    )(*args)
 
 
 def correlate_kernel(nz, where, *refs):
@@ -246,7 +329,6 @@
         return lax.ppermute(value, "ga", [(i, i ^ bit) for i in range(nga)])
 
     chunks = chunk_rows(rows, nga)
-    matrix = mixing_matrix(species_index, coupling, band * block // NPA, block // NPA)
     clock = [()]
 
     def now(*values):
@@ -254,13 +336,12 @@
         return out[: len(values)]
 
     state = [dict() for _ in chunks]
-    shared = {"out": jnp.zeros_like(W)}
+    shared = {}
 
     def stage_Wd(c, s):
         first, count = chunks[c]
-        half = count // 2
         (bands,) = now(W)
-        s["own"] = [lax.slice_in_dim(bands, at, at + half, axis=0) for at in (first, first + half)]
+        s["own"] = take_halves(bands, first, count)
         s["x0"] = band_swap(s["own"][0], 1)
         s["y1"] = band_swap(s["own"][1], 2)
         return tuple(s["own"])
@@ -304,7 +385,7 @@
         total = s["mine"].astype(f32)
         for part in parts:
             total = total + part.astype(f32)
-        mixed = jnp.dot(total, matrix, precision=lax.Precision.HIGHEST).astype(bf)
+        mixed = jnp.dot(total, shared["matrix"], precision=lax.Precision.HIGHEST).astype(bf)
         s["mixed"] = [mixed] + [ga_swap(mixed, 2 * m) for m in range(1, nz)]
         return (mixed,)
 
@@ -333,26 +414,25 @@
 
     def stage_H(c, s):
         first_x, first_y = now(s["first_x"], s["first_y"])
-        to_x = (s["o"][2].astype(f32) + first_y.astype(f32)).astype(bf)
-        to_y = (s["o"][5].astype(f32) + first_x.astype(f32)).astype(bf)
+        to_x, to_y = join(s["o"][2], first_y, s["o"][5], first_x)
         s["second0"] = band_swap(to_x, 1)
         s["second1"] = band_swap(to_y, 2)
         return to_x, to_y
 
     def stage_I(c, s):
         parts = now(s["near0"], s["near1"], s["second0"], s["second1"])
-        first, count = chunks[c]
-        done = []
-        for k in range(2):
-            own = s["o"][k].astype(f32) + parts[k].astype(f32) + parts[2 + k].astype(f32)
-            at = first + k * (count // 2)
-            bands = lax.slice_in_dim(W, at, at + count // 2, axis=0).astype(f32)
-            done.append((kinetic[None, :] * bands + own).astype(bf))
-            shared["out"] = lax.dynamic_update_slice(shared["out"], done[k], (at, 0))
-        return tuple(done)
+        terms = [s["o"][0], s["o"][1], *parts]
+        shared["out"] = finish(W, kinetic, terms, chunks[c][0], shared.get("out"))
+        return ()
+
+    def stage_M(c, s):
+        species, blocks = now(species_index, coupling)
+        first_atom = band * block // NPA
+        shared["matrix"] = mixing_matrix(species, blocks, first_atom, block // NPA)
+        return (shared["matrix"],)
 
     stages = dict(
-        Wd=stage_Wd, We=stage_We, T=stage_T, Wf=stage_Wf, A=stage_A, B=stage_B, C=stage_C,
+        Wd=stage_Wd, We=stage_We, T=stage_T, M=stage_M, Wf=stage_Wf, A=stage_A, B=stage_B, C=stage_C,
         E=stage_E, G=stage_G, K=stage_K, H=stage_H, I=stage_I,
     )
     for name, c in stage_order(len(chunks)):

time: 253 us -> 264 us (1.043)
  Pallas kernels: 67.7 us -> 91.1 us
  other arithmetic: 17.4 us -> 4.53 us
  starting transfers between devices: 61.6 us -> 66.2 us
    pallas_call x0 -> x9, Pallas kernels: none -> 23.5 us  [the longest x3 9.94 us: finish(): pl.pallas_call(finish_kernel, grid=(width // tile,), in_specs=specs, out_...]
    ppermute x24, waiting for transfers between devices: 43.3 us -> 22 us  [ga_swap(): return lax.ppermute(value, 'ga', [(i, i ^ bit) for i in range(nga)])]
    ppermute x36, waiting for transfers between devices: 47.8 us -> 66.8 us  [band_swap(): return lax.ppermute(value, 'band', [(i, i ^ bit) for i in range(4)])]
    dynamic_update_slice x5 -> x0, other arithmetic: 8.65 us -> none  [stage_I(): shared['out'] = lax.dynamic_update_slice(shared['out'], done[k], (at, 0))]
    ppermute x24, starting transfers between devices: 22.9 us -> 28.8 us  [ga_swap(): return lax.ppermute(value, 'ga', [(i, i ^ bit) for i in range(nga)])]
    convert_element_type x7 -> x0, other arithmetic: 5.31 us -> none  [the longest x3 2.07 us: stage_H(): to_y = (s['o'][5].astype(f32) + first_x.astype(f32)).astype(bf)]
    slice x3 -> x0, local copies, waits for them, and re-layouts: 4.18 us -> none  [stage_Wd(): lax.slice_in_dim(bands, at, at + half, axis=0)]
    unnamed x58 -> x68, local copies, waits for them, and re-layouts: 1.38 us -> 5.5 us
  transfers between devices with their start and end apart: 60 -> 60, of which waited for: 25 -> 22; matrix products, arithmetic and copies ran while one was open for 10% -> 4% of each run, Pallas kernels for 24% -> 33%
where the time goes in v2:
time: 264 us; the launch traced here: 263 us
  Pallas kernels  91.1 us (35%)
  waiting for transfers between devices  88.8 us (34%)
  starting transfers between devices  66.2 us (25%)
  local copies, waits for them, and re-layouts  7.18 us (3%)
  matrix products  5.18 us (2%)
  other arithmetic  4.53 us (2%)
    ppermute x36, waiting for transfers between devices, band_swap(): return lax.ppermute(value, 'band', [(i, i ^ bit) for i in range(4)])  66.8 us
    ppermute x36, starting transfers between devices, band_swap(): return lax.ppermute(value, 'band', [(i, i ^ bit) for i in range(4)])  37.3 us
    ppermute x24, starting transfers between devices, ga_swap(): return lax.ppermute(value, 'ga', [(i, i ^ bit) for i in range(nga)])  28.8 us
    pallas_call x3, Pallas kernels, correlate(): pl.pallas_call(functools.partial(correlate_kernel, nz), grid_spec=pltpu.P...  26.9 us
    pallas_call x3, Pallas kernels, expand(): pl.pallas_call(functools.partial(expand_kernel, nz), grid_spec=pltpu.Pref...  26.2 us
    ppermute x24, waiting for transfers between devices, ga_swap(): return lax.ppermute(value, 'ga', [(i, i ^ bit) for i in range(nga)])  22 us
    pallas_call x1, Pallas kernels, transpose(): pl.pallas_call(transpose_kernel, grid=(width // tile,), in_specs=[pl.Bloc...  14.5 us
    pallas_call x3, Pallas kernels, finish(): pl.pallas_call(finish_kernel, grid=(width // tile,), in_specs=specs, out_...  9.94 us
  transfers between devices with their start and end apart: 60, of which 22 were waited for; matrix products, arithmetic and copies ran while one was open for 4% of the time, Pallas kernels for 33%

profile of v2, /device:TPU:0, one launch (start us, length us, event | category | flops | bytes accessed | tf_op | source)
XLA Modules:
  0.0 263.4 jit_solution(8994568482468121685)
XLA Ops:
  0.0 1.9 take.3
  1.9 3.0 %collective-permute-start = (bf16[16,12288]{1,0:T(8,128)(2,1)}, bf16[16,12288]{1,0:T(8,128)(2,1)S(1)}, u32[]{:S(2)}, u32[]{:S(2)}) collective-permute-start(bf16[16,12288]{1,0:T(8,128)(2,1)} %get-tuple-element.132.refs_0_), channel_id=1, source_target_pairs={{0,8},{8,0},{16,24},{24,16},{1,9},{9,1},{17,25},{25,17},{2,10},{10... | collective-permute-start | bytes 1179656 | tf_op jit(solution)/shard_map/ppermute | solution.py:326
  4.9 1.5 collective-permute-start.1
  7.0 14.5 %transpose.11.refs_8_ = bf16[12288,512]{1,0:T(8,128)(2,1)} custom-call(bf16[512,12288]{1,0:T(8,128)(2,1)} %proj.5), custom_call_target="tpu_custom_call" | custom-call | flops 100663296 | bytes 25165824 | tf_op jit(solution)/shard_map/transpose/pallas_call | solution.py:112
  21.5 2.1 collective-permute-start.6
  23.6 1.5 collective-permute-start.7
  26.3 2.4 take.4
  30.1 3.6 %collective-permute-done.6.refs_6_ = bf16[16,12288]{1,0:T(8,128)(2,1)} collective-permute-done((bf16[16,12288]{1,0:T(8,128)(2,1)S(1)}, bf16[16,12288]{1,0:T(8,128)(2,1)}, u32[]{:S(2)}, u32[]{:S(2)}) %collective-permute-start.6) | collective-permute-done | bytes 393248 | tf_op jit(solution)/shard_map/ppermute | solution.py:326
  33.7 2.2 collective-permute-done.7.refs_7_
  35.9 8.4 %correlate.3 = (bf16[4,16,512]{2,1,0:T(8,128)(2,1)}, bf16[4,16,512]{2,1,0:T(8,128)(2,1)}) custom-call(s32[2]{0:T(128)} %pad_add_fusion.where, bf16[16,12288]{1,0:T(8,128)(2,1)} %get-tuple-element.132.refs_0_, bf16[16,12288]{1,0:T(8,128)(2,1)} %get-tuple-element.133.refs_1_, bf16[16,12288]{1,0:T(8,128)(2,1)} %copy-done.18, bf16[16,12288]{1,0:T(8,128)(2,1)} %copy-done.19, ...), custom_call_target="tpu_custom_call" | custom-call | flops 1610612736 | bytes 15728640 | tf_op jit(solution)/shard_map/correlate/pallas_call | solution.py:240
  47.3 1.6 collective-permute-start.17
  48.8 2.6 collective-permute-start.18
  52.2 1.6 collective-permute-start.13
  54.4 1.9 take.5
  56.3 1.5 collective-permute-start.15
  58.3 1.9 convolution_convert_fusion.2
  60.9 3.1 %collective-permute-done.20 = bf16[16,512]{1,0:T(8,128)(2,1)S(1)} collective-permute-done((bf16[16,512]{1,0:T(8,128)(2,1)S(1)}, bf16[16,512]{1,0:T(8,128)(2,1)S(1)}, u32[]{:S(2)}, u32[]{:S(2)}) %collective-permute-start.20) | collective-permute-done | bytes 16416 | tf_op jit(solution)/shard_map/ppermute | solution.py:329
  64.0 2.1 collective-permute-start.21
  66.1 2.5 collective-permute-done.21
  68.6 3.6 %collective-permute-start.22 = (bf16[16,512]{1,0:T(8,128)(2,1)S(1)}, bf16[16,512]{1,0:T(8,128)(2,1)S(1)}, u32[]{:S(2)}, u32[]{:S(2)}) collective-permute-start(bf16[16,512]{1,0:T(8,128)(2,1)S(1)} %convolution_convert_fusion.2), channel_id=1, source_target_pairs={{0,6},{1,7},{2,4},{3,5},{4,2},{5,3},{6,0},{7,1},{8,14},{9,15},{10,... | collective-permute-start | bytes 49160 | tf_op jit(solution)/shard_map/ppermute | solution.py:329
  72.2 1.9 collective-permute-done.22
  74.8 1.3 collective-permute-done.23.there
  77.0 8.2 %expand.3 = (bf16[16,12288]{1,0:T(8,128)(2,1)}, bf16[16,12288]{1,0:T(8,128)(2,1)}, bf16[16,12288]{1,0:T(8,128)(2,1)}, bf16[16,12288]{1,0:T(8,128)(2,1)}, bf16[16...) custom-call(s32[2]{0:T(128)} %pad_add_fusion.where, ...), custom_call_target="tpu_custom_call" | custom-call | flops 1610612736 | bytes 15728640 | tf_op jit(solution)/shard_map/expand/pallas_call | solution.py:292
  85.2 1.8 collective-permute-start.9
  87.0 4.2 %collective-permute-done.15.refs_6_ = bf16[32,12288]{1,0:T(8,128)(2,1)} collective-permute-done((bf16[32,12288]{1,0:T(8,128)(2,1)S(1)}, bf16[32,12288]{1,0:T(8,128)(2,1)}, u32[]{:S(2)}, u32[]{:S(2)}) %collective-permute-start.15) | collective-permute-done | bytes 786464 | tf_op jit(solution)/shard_map/ppermute | solution.py:326
  91.2 10.0 %correlate.4 = (bf16[4,32,512]{2,1,0:T(8,128)(2,1)}, bf16[4,32,512]{2,1,0:T(8,128)(2,1)}) custom-call(s32[2]{0:T(128)} %pad_add_fusion.where, bf16[32,12288]{1,0:T(8,128)(2,1)} %get-tuple-element.140.refs_0_, bf16[32,12288]{1,0:T(8,128)(2,1)} %get-tuple-element.141.refs_1_, bf16[32,12288]{1,0:T(8,128)(2,1)} %copy-done.2, ...), custom_call_target="tpu_custom_call" | custom-call | flops 3221225472 | bytes 18874368 | tf_op jit(solution)/shard_map/correlate/pallas_call | solution.py:240
  102.9 0.9 add_convert_fusion
  104.6 3.5 %collective-permute-start.28 = (bf16[32,512]{1,0:T(8,128)(2,1)S(1)}, bf16[32,512]{1,0:T(8,128)(2,1)S(1)}, u32[]{:S(2)}, u32[]{:S(2)}) collective-permute-start(bf16[32,512]{1,0:T(8,128)(2,1)S(1)} %get-tuple-element.260), channel_id=1, source_target_pairs={{0,4},{1,5},{2,6},{3,7},{4,0},{5,1},{6,2},{7,3},{8,12},{9,13},{10,... | collective-permute-start | bytes 98312 | tf_op jit(solution)/shard_map/ppermute | solution.py:329
  108.3 2.0 collective-permute-done.28
  110.3 3.4 %collective-permute-done.29 = bf16[32,512]{1,0:T(8,128)(2,1)S(1)} collective-permute-done((bf16[32,512]{1,0:T(8,128)(2,1)S(1)}, bf16[32,512]{1,0:T(8,128)(2,1)S(1)}, u32[]{:S(2)}, u32[]{:S(2)}) %collective-permute-start.29) | collective-permute-done | bytes 32800 | tf_op jit(solution)/shard_map/ppermute | solution.py:329
  113.8 2.0 convolution_convert_fusion
  116.7 3.5 %collective-permute-start.32 = (bf16[32,512]{1,0:T(8,128)(2,1)S(1)}, bf16[32,512]{1,0:T(8,128)(2,1)S(1)}, u32[]{:S(2)}, u32[]{:S(2)}) collective-permute-start(bf16[32,512]{1,0:T(8,128)(2,1)S(1)} %convolution_convert_fusion), channel_id=1, source_target_pairs={{0,6},{1,7},{2,4},{3,5},{4,2},{5,3},{6,0},{7,1},{8,14},{9,15},{10,... | collective-permute-start | bytes 98312 | tf_op jit(solution)/shard_map/ppermute | solution.py:329
  121.1 2.2 join.3
  123.5 1.3 collective-permute-start.10
  124.8 1.5 collective-permute-start.11
  128.3 9.8 %expand.4 = (bf16[32,12288]{1,0:T(8,128)(2,1)}, bf16[32,12288]{1,0:T(8,128)(2,1)}, bf16[32,12288]{1,0:T(8,128)(2,1)}, bf16[32,12288]{1,0:T(8,128)(2,1)}, bf16[32...) custom-call(s32[2]{0:T(128)} %pad_add_fusion.where, ...), custom_call_target="tpu_custom_call" | custom-call | flops 3221225472 | bytes 18874368 | tf_op jit(solution)/shard_map/expand/pallas_call | solution.py:292
  138.1 1.3 collective-permute-start.43
  139.4 1.6 collective-permute-start.44
  141.0 4.3 %collective-permute-done.24.refs_6_ = bf16[16,12288]{1,0:T(8,128)(2,1)} collective-permute-done((bf16[16,12288]{1,0:T(8,128)(2,1)S(1)}, bf16[16,12288]{1,0:T(8,128)(2,1)}, u32[]{:S(2)}, u32[]{:S(2)}) %collective-permute-start.24) | collective-permute-done | bytes 393248 | tf_op jit(solution)/shard_map/ppermute | solution.py:326
  145.3 8.4 %correlate.5 = (bf16[4,16,512]{2,1,0:T(8,128)(2,1)}, bf16[4,16,512]{2,1,0:T(8,128)(2,1)}) custom-call(s32[2]{0:T(128)} %pad_add_fusion.where, bf16[16,12288]{1,0:T(8,128)(2,1)} %get-tuple-element.157.refs_0_, bf16[16,12288]{1,0:T(8,128)(2,1)} %get-tuple-element.156.refs_1_, bf16[16,12288]{1,0:T(8,128)(2,1)} %copy-done.17, bf16[16,12288]{1,0:T(8,128)(2,1)} %copy-done.20, ...), custom_call_target="tpu_custom_call" | custom-call | flops 1610612736 | bytes 15728640 | tf_op jit(solution)/shard_map/correlate/pallas_call | solution.py:240
  153.8 1.5 collective-permute-done.36
  156.2 3.1 %collective-permute-start.38 = (bf16[16,512]{1,0:T(8,128)(2,1)S(1)}, bf16[16,512]{1,0:T(8,128)(2,1)S(1)}, u32[]{:S(2)}, u32[]{:S(2)}) collective-permute-start(bf16[16,512]{1,0:T(8,128)(2,1)S(1)} %get-tuple-element.267), channel_id=1, source_target_pairs={{0,4},{1,5},{2,6},{3,7},{4,0},{5,1},{6,2},{7,3},{8,12},{9,13},{10,... | collective-permute-start | bytes 49160 | tf_op jit(solution)/shard_map/ppermute | solution.py:329
  159.3 1.3 collective-permute-start.39
  161.0 3.8 %collective-permute-done.39 = bf16[16,512]{1,0:T(8,128)(2,1)S(1)} collective-permute-done((bf16[16,512]{1,0:T(8,128)(2,1)S(1)}, bf16[16,512]{1,0:T(8,128)(2,1)S(1)}, u32[]{:S(2)}, u32[]{:S(2)}) %collective-permute-start.39) | collective-permute-done | bytes 16416 | tf_op jit(solution)/shard_map/ppermute | solution.py:329
  164.9 1.1 convolution_convert_fusion.1
  166.0 1.8 collective-permute-start.41
  167.8 2.6 collective-permute-start.42
  170.4 1.5 collective-permute-start.56
  172.8 2.8 %join.4 = (bf16[32,12288]{1,0:T(8,128)(2,1)}, bf16[32,12288]{1,0:T(8,128)(2,1)}) custom-call(bf16[32,12288]{1,0:T(8,128)(2,1)} %get-tuple-element.213.a, bf16[32,12288]{1,0:T(8,128)(2,1)} %copy-done.5, bf16[32,12288]{1,0:T(8,128)(2,1)} %get-tuple-element.215.c, bf16[32,12288]{1,0:T(8,128)(2,1)} %copy-done.4), custom_call_target="tpu_custom_call" | custom-call | flops 786432 | bytes 4718592 | tf_op jit(solution)/shard_map/join/pallas_call | solution.py:157
  175.7 1.2 collective-permute-start.58
  177.0 1.2 collective-permute-done.45.there
  178.9 8.3 %expand.5 = (bf16[16,12288]{1,0:T(8,128)(2,1)}, bf16[16,12288]{1,0:T(8,128)(2,1)}, bf16[16,12288]{1,0:T(8,128)(2,1)}, bf16[16,12288]{1,0:T(8,128)(2,1)}, bf16[16...) custom-call(s32[2]{0:T(128)} %pad_add_fusion.where, ...), custom_call_target="tpu_custom_call" | custom-call | flops 1610612736 | bytes 15728640 | tf_op jit(solution)/shard_map/expand/pallas_call | solution.py:292
  188.6 1.5 collective-permute-start.52
  190.1 1.2 collective-permute-start.53
  192.2 7.4 %collective-permute-done.48.d = bf16[16,12288]{1,0:T(8,128)(2,1)} collective-permute-done((bf16[16,12288]{1,0:T(8,128)(2,1)}, bf16[16,12288]{1,0:T(8,128)(2,1)}, u32[]{:S(2)}, u32[]{:S(2)}) %collective-permute-start.48) | collective-permute-done | bytes 393248 | tf_op jit(solution)/shard_map/ppermute | solution.py:326
  200.4 1.2 collective-permute-start.59
  201.5 2.3 join.5
  203.8 37.6 %collective-permute-done.59.refs_5_ = bf16[16,12288]{1,0:T(8,128)(2,1)} collective-permute-done((bf16[16,12288]{1,0:T(8,128)(2,1)}, bf16[16,12288]{1,0:T(8,128)(2,1)}, u32[]{:S(2)}, u32[]{:S(2)}) %collective-permute-start.59) | collective-permute-done | bytes 393248 | tf_op jit(solution)/shard_map/ppermute | solution.py:326
  241.9 1.2 collective-permute-start.47
  244.0 1.5 collective-permute-start.51
  245.5 2.9 %finish.3.refs_6_ = bf16[128,12288]{1,0:T(8,128)(2,1)} custom-call(bf16[128,12288]{1,0:T(8,128)(2,1)} %bands.5, f32[1,12288]{1,0:T(1,128)} %bitcast.75, bf16[16,12288]{1,0:T(8,128)(2,1)} %get-tuple-element.249.refs_0_, bf16[16,12288]{1,0:T(8,128)(2,1)} %get-tuple-element.250.refs_1_, bf16[16,12288]{1,0:T(8,128)(2,1)} %copy-done.11, ...), custom_call_target="tpu_custom_call" | custom-call | flops 3145728 | bytes 3932160 | tf_op jit(solution)/shard_map/finish/pallas_call | solution.py:193
  249.3 4.1 %finish.4.refs_6_ = bf16[128,12288]{1,0:T(8,128)(2,1)} custom-call(bf16[128,12288]{1,0:T(8,128)(2,1)} %bands.5, f32[1,12288]{1,0:T(1,128)} %bitcast.76, bf16[32,12288]{1,0:T(8,128)(2,1)} %get-tuple-element.243.refs_0_, bf16[32,12288]{1,0:T(8,128)(2,1)} %get-tuple-element.244.refs_1_, bf16[32,12288]{1,0:T(8,128)(2,1)} %copy-done.6, ...), custom_call_target="tpu_custom_call", output_to_operand_aliasing={{}: (8, {})} | custom-call | flops 6291456 | bytes 7864320 | tf_op jit(solution)/shard_map/finish/pallas_call | solution.py:193
  254.2 6.2 %collective-permute-done.50.refs_4_ = bf16[16,12288]{1,0:T(8,128)(2,1)} collective-permute-done((bf16[16,12288]{1,0:T(8,128)(2,1)}, bf16[16,12288]{1,0:T(8,128)(2,1)}, u32[]{:S(2)}, u32[]{:S(2)}) %collective-permute-start.50) | collective-permute-done | bytes 393248 | tf_op jit(solution)/shard_map/ppermute | solution.py:326
  260.5 2.9 %finish.5 = bf16[128,12288]{1,0:T(8,128)(2,1)} custom-call(bf16[128,12288]{1,0:T(8,128)(2,1)} %bands.5, f32[1,12288]{1,0:T(1,128)} %bitcast.77, bf16[16,12288]{1,0:T(8,128)(2,1)} %get-tuple-element.225.refs_0_, bf16[16,12288]{1,0:T(8,128)(2,1)} %get-tuple-element.226.refs_1_, ...), custom_call_target="tpu_custom_call", output_to_operand_aliasing={{}: (8, {})} | custom-call | flops 3145728 | bytes 3932160 | tf_op jit(solution)/shard_map/finish/pallas_call | solution.py:193
  (162 shorter events, 26.2 us)
Async XLA Ops:
  1.9 19.6 %collective-permute-start = (bf16[16,12288]{1,0:T(8,128)(2,1)}, bf16[16,12288]{1,0:T(8,128)(2,1)S(1)}, u32[]{:S(2)}, u32[]{:S(2)}) collective-permute-start(bf16[16,12288]{1,0:T(8,128)(2,1)} %get-tuple-element.132.refs_0_), channel_id=1, source_target_pairs={{0,8},{8,0},{16,24},{24,16},{1,9},{9,1},{17,25},{25,17},{2,10},{10... | collective-permute-start | bytes 1179656 | tf_op jit(solution)/shard_map/ppermute | solution.py:326
  4.9 16.6 %collective-permute-start.1 = (bf16[16,12288]{1,0:T(8,128)(2,1)}, bf16[16,12288]{1,0:T(8,128)(2,1)}, u32[]{:S(2)}, u32[]{:S(2)}) collective-permute-start(bf16[16,12288]{1,0:T(8,128)(2,1)} %get-tuple-element.133.refs_1_), channel_id=1, source_target_pairs={{0,16},{8,24},{16,0},{24,8},{1,17},{9,25},{17,1},{25,9},{2,18},{10... | collective-permute-start | bytes 1179656 | tf_op jit(solution)/shard_map/ppermute | solution.py:326
  6.4 22.8 %collective-permute-start.4 = (bf16[16,12288]{1,0:T(8,128)(2,1)}, bf16[16,12288]{1,0:T(8,128)(2,1)S(1)}, u32[]{:S(2)}, u32[]{:S(2)}) collective-permute-start(bf16[16,12288]{1,0:T(8,128)(2,1)} %get-tuple-element.133.refs_1_), channel_id=1, source_target_pairs={{0,8},{8,0},{16,24},{24,16},{1,9},{9,1},{17,25},{25,17},{2,10},{10... | collective-permute-start | bytes 1179656 | tf_op jit(solution)/shard_map/ppermute | solution.py:326
  7.0 23.1 %collective-permute-start.5 = (bf16[16,12288]{1,0:T(8,128)(2,1)}, bf16[16,12288]{1,0:T(8,128)(2,1)}, u32[]{:S(2)}, u32[]{:S(2)}) collective-permute-start(bf16[16,12288]{1,0:T(8,128)(2,1)} %get-tuple-element.132.refs_0_), channel_id=1, source_target_pairs={{0,16},{8,24},{16,0},{24,8},{1,17},{9,25},{17,1},{25,9},{2,18},{10... | collective-permute-start | bytes 1179656 | tf_op jit(solution)/shard_map/ppermute | solution.py:326
  21.5 12.2 %collective-permute-start.6 = (bf16[16,12288]{1,0:T(8,128)(2,1)S(1)}, bf16[16,12288]{1,0:T(8,128)(2,1)}, u32[]{:S(2)}, u32[]{:S(2)}) collective-permute-start(bf16[16,12288]{1,0:T(8,128)(2,1)S(1)} %collective-permute-done.refs_2_), channel_id=1, source_target_pairs={{0,16},{8,24},{16,0},{24,8},{1,17},{9,25},{17,1},{25,9},{2,18},{10... | collective-permute-start | bytes 1179656 | tf_op jit(solution)/shard_map/ppermute | solution.py:326
  23.6 12.3 %collective-permute-start.7 = (bf16[16,12288]{1,0:T(8,128)(2,1)}, bf16[16,12288]{1,0:T(8,128)(2,1)}, u32[]{:S(2)}, u32[]{:S(2)}) collective-permute-start(bf16[16,12288]{1,0:T(8,128)(2,1)} %collective-permute-done.1.refs_5_), channel_id=1, source_target_pairs={{0,8},{8,0},{16,24},{24,16},{1,9},{9,1},{17,25},{25,17},{2,10},{10... | collective-permute-start | bytes 1179656 | tf_op jit(solution)/shard_map/ppermute | solution.py:326
  28.7 23.5 %collective-permute-start.2 = (bf16[32,12288]{1,0:T(8,128)(2,1)}, bf16[32,12288]{1,0:T(8,128)(2,1)S(1)}, u32[]{:S(2)}, u32[]{:S(2)}) collective-permute-start(bf16[32,12288]{1,0:T(8,128)(2,1)} %get-tuple-element.140.refs_0_), channel_id=1, source_target_pairs={{0,8},{8,0},{16,24},{24,16},{1,9},{9,1},{17,25},{25,17},{2,10},{10... | collective-permute-start | bytes 2359304 | tf_op jit(solution)/shard_map/ppermute | solution.py:326
  30.0 23.8 %collective-permute-start.3 = (bf16[32,12288]{1,0:T(8,128)(2,1)}, bf16[32,12288]{1,0:T(8,128)(2,1)S(1)}, u32[]{:S(2)}, u32[]{:S(2)}) collective-permute-start(bf16[32,12288]{1,0:T(8,128)(2,1)} %get-tuple-element.141.refs_1_), channel_id=1, source_target_pairs={{0,16},{8,24},{16,0},{24,8},{1,17},{9,25},{17,1},{25,9},{2,18},{10... | collective-permute-start | bytes 2359304 | tf_op jit(solution)/shard_map/ppermute | solution.py:326
  44.3 1.5 collective-permute-start.8
  47.3 9.0 %collective-permute-start.17 = (bf16[16,512]{1,0:T(8,128)(2,1)}, bf16[16,512]{1,0:T(8,128)(2,1)}, u32[]{:S(2)}, u32[]{:S(2)}) collective-permute-start(bf16[16,512]{1,0:T(8,128)(2,1)} %get-tuple-element.275), channel_id=1, source_target_pairs={{0,2},{1,3},{2,0},{3,1},{4,6},{5,7},{6,4},{7,5},{8,10},{9,11},{10,... | collective-permute-start | bytes 49160 | tf_op jit(solution)/shard_map/ppermute | solution.py:329
  48.8 8.9 %collective-permute-start.18 = (bf16[16,512]{1,0:T(8,128)(2,1)S(1)}, bf16[16,512]{1,0:T(8,128)(2,1)}, u32[]{:S(2)}, u32[]{:S(2)}) collective-permute-start(bf16[16,512]{1,0:T(8,128)(2,1)S(1)} %get-tuple-element.274), channel_id=1, source_target_pairs={{0,4},{1,5},{2,6},{3,7},{4,0},{5,1},{6,2},{7,3},{8,12},{9,13},{10,... | collective-permute-start | bytes 49160 | tf_op jit(solution)/shard_map/ppermute | solution.py:329
  51.4 6.9 %collective-permute-start.19 = (bf16[16,512]{1,0:T(8,128)(2,1)S(1)}, bf16[16,512]{1,0:T(8,128)(2,1)}, u32[]{:S(2)}, u32[]{:S(2)}) collective-permute-start(bf16[16,512]{1,0:T(8,128)(2,1)S(1)} %get-tuple-element.273), channel_id=1, source_target_pairs={{0,6},{1,7},{2,4},{3,5},{4,2},{5,3},{6,0},{7,1},{8,14},{9,15},{10,... | collective-permute-start | bytes 49160 | tf_op jit(solution)/shard_map/ppermute | solution.py:329
  52.2 32.9 %copy-start.2 = (bf16[32,12288]{1,0:T(8,128)(2,1)}, bf16[32,12288]{1,0:T(8,128)(2,1)S(1)}, u32[]{:S(2)}) copy-start(bf16[32,12288]{1,0:T(8,128)(2,1)S(1)} %collective-permute-done.2.refs_2_) | copy-start | bytes 2359300
  52.2 32.9 %collective-permute-start.13 = (bf16[32,12288]{1,0:T(8,128)(2,1)S(1)}, bf16[32,12288]{1,0:T(8,128)(2,1)}, u32[]{:S(2)}, u32[]{:S(2)}) collective-permute-start(bf16[32,12288]{1,0:T(8,128)(2,1)S(1)} %copy-done.1), channel_id=1, source_target_pairs={{0,8},{8,0},{16,24},{24,16},{1,9},{9,1},{17,25},{25,17},{2,10},{10... | collective-permute-start | bytes 2359304 | tf_op jit(solution)/shard_map/ppermute | solution.py:326
  53.8 31.4 %copy-start.3 = (bf16[32,12288]{1,0:T(8,128)(2,1)}, bf16[32,12288]{1,0:T(8,128)(2,1)S(1)}, u32[]{:S(2)}) copy-start(bf16[32,12288]{1,0:T(8,128)(2,1)S(1)} %collective-permute-done.3.refs_5_) | copy-start | bytes 2359300
  53.8 33.2 %collective-permute-start.14 = (bf16[32,12288]{1,0:T(8,128)(2,1)S(1)}, bf16[32,12288]{1,0:T(8,128)(2,1)}, u32[]{:S(2)}, u32[]{:S(2)}) collective-permute-start(bf16[32,12288]{1,0:T(8,128)(2,1)S(1)} %copy-done), channel_id=1, source_target_pairs={{0,16},{8,24},{16,0},{24,8},{1,17},{9,25},{17,1},{25,9},{2,18},{10... | collective-permute-start | bytes 2359304 | tf_op jit(solution)/shard_map/ppermute | solution.py:326
  56.3 34.9 %collective-permute-start.15 = (bf16[32,12288]{1,0:T(8,128)(2,1)S(1)}, bf16[32,12288]{1,0:T(8,128)(2,1)}, u32[]{:S(2)}, u32[]{:S(2)}) collective-permute-start(bf16[32,12288]{1,0:T(8,128)(2,1)S(1)} %collective-permute-done.2.refs_2_), channel_id=1, source_target_pairs={{0,16},{8,24},{16,0},{24,8},{1,17},{9,25},{17,1},{25,9},{2,18},{10... | collective-permute-start | bytes 2359304 | tf_op jit(solution)/shard_map/ppermute | solution.py:326
  57.8 33.4 %collective-permute-start.16 = (bf16[32,12288]{1,0:T(8,128)(2,1)S(1)}, bf16[32,12288]{1,0:T(8,128)(2,1)}, u32[]{:S(2)}, u32[]{:S(2)}) collective-permute-start(bf16[32,12288]{1,0:T(8,128)(2,1)S(1)} %collective-permute-done.3.refs_5_), channel_id=1, source_target_pairs={{0,8},{8,0},{16,24},{24,16},{1,9},{9,1},{17,25},{25,17},{2,10},{10... | collective-permute-start | bytes 2359304 | tf_op jit(solution)/shard_map/ppermute | solution.py:326
  60.2 3.8 %collective-permute-start.20 = (bf16[16,512]{1,0:T(8,128)(2,1)S(1)}, bf16[16,512]{1,0:T(8,128)(2,1)S(1)}, u32[]{:S(2)}, u32[]{:S(2)}) collective-permute-start(bf16[16,512]{1,0:T(8,128)(2,1)S(1)} %convolution_convert_fusion.2), channel_id=1, source_target_pairs={{0,2},{1,3},{2,0},{3,1},{4,6},{5,7},{6,4},{7,5},{8,10},{9,11},{10,... | collective-permute-start | bytes 49160 | tf_op jit(solution)/shard_map/ppermute | solution.py:329
  64.0 4.6 %collective-permute-start.21 = (bf16[16,512]{1,0:T(8,128)(2,1)S(1)}, bf16[16,512]{1,0:T(8,128)(2,1)S(1)}, u32[]{:S(2)}, u32[]{:S(2)}) collective-permute-start(bf16[16,512]{1,0:T(8,128)(2,1)S(1)} %convolution_convert_fusion.2), channel_id=1, source_target_pairs={{0,4},{1,5},{2,6},{3,7},{4,0},{5,1},{6,2},{7,3},{8,12},{9,13},{10,... | collective-permute-start | bytes 49160 | tf_op jit(solution)/shard_map/ppermute | solution.py:329
  68.6 5.5 %collective-permute-start.22 = (bf16[16,512]{1,0:T(8,128)(2,1)S(1)}, bf16[16,512]{1,0:T(8,128)(2,1)S(1)}, u32[]{:S(2)}, u32[]{:S(2)}) collective-permute-start(bf16[16,512]{1,0:T(8,128)(2,1)S(1)} %convolution_convert_fusion.2), channel_id=1, source_target_pairs={{0,6},{1,7},{2,4},{3,5},{4,2},{5,3},{6,0},{7,1},{8,14},{9,15},{10,... | collective-permute-start | bytes 49160 | tf_op jit(solution)/shard_map/ppermute | solution.py:329
  74.8 1.3 collective-permute-start.23
  76.7 25.5 %collective-permute-start.12 = (bf16[16,12288]{1,0:T(8,128)(2,1)}, bf16[16,12288]{1,0:T(8,128)(2,1)}, u32[]{:S(2)}, u32[]{:S(2)}) collective-permute-start(bf16[16,12288]{1,0:T(8,128)(2,1)} %get-tuple-element.156.refs_1_), channel_id=1, source_target_pairs={{0,16},{8,24},{16,0},{24,8},{1,17},{9,25},{17,1},{25,9},{2,18},{10... | collective-permute-start | bytes 1179656 | tf_op jit(solution)/shard_map/ppermute | solution.py:326
  85.2 17.0 %collective-permute-start.9 = (bf16[16,12288]{1,0:T(8,128)(2,1)S(1)}, bf16[16,12288]{1,0:T(8,128)(2,1)S(1)}, u32[]{:S(2)}, u32[]{:S(2)}) collective-permute-start(bf16[16,12288]{1,0:T(8,128)(2,1)S(1)} %copy-done.15), channel_id=1, source_target_pairs={{0,8},{8,0},{16,24},{24,16},{1,9},{9,1},{17,25},{25,17},{2,10},{10... | collective-permute-start | bytes 1179656 | tf_op jit(solution)/shard_map/ppermute | solution.py:326
  101.2 1.6 collective-permute-start.26
  101.3 18.9 %collective-permute-start.33 = (bf16[16,12288]{1,0:T(8,128)(2,1)}, bf16[16,12288]{1,0:T(8,128)(2,1)S(1)}, u32[]{:S(2)}, u32[]{:S(2)}) collective-permute-start(bf16[16,12288]{1,0:T(8,128)(2,1)} %get-tuple-element.170), channel_id=1, source_target_pairs={{0,8},{8,0},{16,24},{24,16},{1,9},{9,1},{17,25},{25,17},{2,10},{10... | collective-permute-start | bytes 1179656 | tf_op jit(solution)/shard_map/ppermute | solution.py:326
  101.9 18.3 %collective-permute-start.34 = (bf16[16,12288]{1,0:T(8,128)(2,1)}, bf16[16,12288]{1,0:T(8,128)(2,1)S(1)}, u32[]{:S(2)}, u32[]{:S(2)}) collective-permute-start(bf16[16,12288]{1,0:T(8,128)(2,1)} %get-tuple-element.169), channel_id=1, source_target_pairs={{0,16},{8,24},{16,0},{24,8},{1,17},{9,25},{17,1},{25,9},{2,18},{10... | collective-permute-start | bytes 1179656 | tf_op jit(solution)/shard_map/ppermute | solution.py:326
  102.2 35.9 %copy-start.17 = (bf16[16,12288]{1,0:T(8,128)(2,1)}, bf16[16,12288]{1,0:T(8,128)(2,1)S(1)}, u32[]{:S(2)}) copy-start(bf16[16,12288]{1,0:T(8,128)(2,1)S(1)} %collective-permute-done.9.refs_2_) | copy-start | bytes 1179652
  103.8 4.5 %collective-permute-start.27 = (bf16[32,512]{1,0:T(8,128)(2,1)S(1)}, bf16[32,512]{1,0:T(8,128)(2,1)S(1)}, u32[]{:S(2)}, u32[]{:S(2)}) collective-permute-start(bf16[32,512]{1,0:T(8,128)(2,1)S(1)} %get-tuple-element.261), channel_id=1, source_target_pairs={{0,2},{1,3},{2,0},{3,1},{4,6},{5,7},{6,4},{7,5},{8,10},{9,11},{10,... | collective-permute-start | bytes 98312 | tf_op jit(solution)/shard_map/ppermute | solution.py:329
  104.6 5.8 %collective-permute-start.28 = (bf16[32,512]{1,0:T(8,128)(2,1)S(1)}, bf16[32,512]{1,0:T(8,128)(2,1)S(1)}, u32[]{:S(2)}, u32[]{:S(2)}) collective-permute-start(bf16[32,512]{1,0:T(8,128)(2,1)S(1)} %get-tuple-element.260), channel_id=1, source_target_pairs={{0,4},{1,5},{2,6},{3,7},{4,0},{5,1},{6,2},{7,3},{8,12},{9,13},{10,... | collective-permute-start | bytes 98312 | tf_op jit(solution)/shard_map/ppermute | solution.py:329
  108.1 5.7 %collective-permute-start.29 = (bf16[32,512]{1,0:T(8,128)(2,1)S(1)}, bf16[32,512]{1,0:T(8,128)(2,1)S(1)}, u32[]{:S(2)}, u32[]{:S(2)}) collective-permute-start(bf16[32,512]{1,0:T(8,128)(2,1)S(1)} %get-tuple-element.259), channel_id=1, source_target_pairs={{0,6},{1,7},{2,4},{3,5},{4,2},{5,3},{6,0},{7,1},{8,14},{9,15},{10,... | collective-permute-start | bytes 98312 | tf_op jit(solution)/shard_map/ppermute | solution.py:329
  115.7 7.6 %collective-permute-start.30 = (bf16[32,512]{1,0:T(8,128)(2,1)S(1)}, bf16[32,512]{1,0:T(8,128)(2,1)S(1)}, u32[]{:S(2)}, u32[]{:S(2)}) collective-permute-start(bf16[32,512]{1,0:T(8,128)(2,1)S(1)} %convolution_convert_fusion), channel_id=1, source_target_pairs={{0,2},{1,3},{2,0},{3,1},{4,6},{5,7},{6,4},{7,5},{8,10},{9,11},{10,... | collective-permute-start | bytes 98312 | tf_op jit(solution)/shard_map/ppermute | solution.py:329
  115.8 7.5 %collective-permute-start.31 = (bf16[32,512]{1,0:T(8,128)(2,1)S(1)}, bf16[32,512]{1,0:T(8,128)(2,1)S(1)}, u32[]{:S(2)}, u32[]{:S(2)}) collective-permute-start(bf16[32,512]{1,0:T(8,128)(2,1)S(1)} %convolution_convert_fusion), channel_id=1, source_target_pairs={{0,4},{1,5},{2,6},{3,7},{4,0},{5,1},{6,2},{7,3},{8,12},{9,13},{10,... | collective-permute-start | bytes 98312 | tf_op jit(solution)/shard_map/ppermute | solution.py:329
  116.7 6.6 %collective-permute-start.32 = (bf16[32,512]{1,0:T(8,128)(2,1)S(1)}, bf16[32,512]{1,0:T(8,128)(2,1)S(1)}, u32[]{:S(2)}, u32[]{:S(2)}) collective-permute-start(bf16[32,512]{1,0:T(8,128)(2,1)S(1)} %convolution_convert_fusion), channel_id=1, source_target_pairs={{0,6},{1,7},{2,4},{3,5},{4,2},{5,3},{6,0},{7,1},{8,14},{9,15},{10,... | collective-permute-start | bytes 98312 | tf_op jit(solution)/shard_map/ppermute | solution.py:329
  123.4 4.2 %collective-permute-start.35 = (bf16[4,32,512]{2,1,0:T(8,128)(2,1)S(1)}, bf16[4,32,512]{2,1,0:T(8,128)(2,1)S(1)}, u32[]{:S(2)}, u32[]{:S(2)}) collective-permute-start(bf16[4,32,512]{2,1,0:T(8,128)(2,1)S(1)} %pad_maximum_fusion.here), channel_id=1, source_target_pairs={{0,1},{1,0},{2,3},{3,2},{4,5},{5,4},{6,7},{7,6},{8,9},{9,8},{10,11... | collective-permute-start | bytes 393224 | tf_op jit(solution)/shard_map/ppermute | solution.py:329
  123.5 15.9 %collective-permute-start.10 = (bf16[16,12288]{1,0:T(8,128)(2,1)S(1)}, bf16[16,12288]{1,0:T(8,128)(2,1)S(1)}, u32[]{:S(2)}, u32[]{:S(2)}) collective-permute-start(bf16[16,12288]{1,0:T(8,128)(2,1)S(1)} %copy-done.16), channel_id=1, source_target_pairs={{0,8},{8,0},{16,24},{24,16},{1,9},{9,1},{17,25},{25,17},{2,10},{10... | collective-permute-start | bytes 1179656 | tf_op jit(solution)/shard_map/ppermute | solution.py:326
  124.8 16.2 %collective-permute-start.11 = (bf16[16,12288]{1,0:T(8,128)(2,1)S(1)}, bf16[16,12288]{1,0:T(8,128)(2,1)}, u32[]{:S(2)}, u32[]{:S(2)}) collective-permute-start(bf16[16,12288]{1,0:T(8,128)(2,1)S(1)} %copy-done.15), channel_id=1, source_target_pairs={{0,16},{8,24},{16,0},{24,8},{1,17},{9,25},{17,1},{25,9},{2,18},{10... | collective-permute-start | bytes 1179656 | tf_op jit(solution)/shard_map/ppermute | solution.py:326
  126.3 19.0 %collective-permute-start.24 = (bf16[16,12288]{1,0:T(8,128)(2,1)S(1)}, bf16[16,12288]{1,0:T(8,128)(2,1)}, u32[]{:S(2)}, u32[]{:S(2)}) collective-permute-start(bf16[16,12288]{1,0:T(8,128)(2,1)S(1)} %collective-permute-done.9.refs_2_), channel_id=1, source_target_pairs={{0,16},{8,24},{16,0},{24,8},{1,17},{9,25},{17,1},{25,9},{2,18},{10... | collective-permute-start | bytes 1179656 | tf_op jit(solution)/shard_map/ppermute | solution.py:326
  126.8 18.5 %collective-permute-start.25 = (bf16[16,12288]{1,0:T(8,128)(2,1)}, bf16[16,12288]{1,0:T(8,128)(2,1)}, u32[]{:S(2)}, u32[]{:S(2)}) collective-permute-start(bf16[16,12288]{1,0:T(8,128)(2,1)} %collective-permute-done.12.refs_5_), channel_id=1, source_target_pairs={{0,8},{8,0},{16,24},{24,16},{1,9},{9,1},{17,25},{25,17},{2,10},{10... | collective-permute-start | bytes 1179656 | tf_op jit(solution)/shard_map/ppermute | solution.py:326
  138.1 32.3 %collective-permute-start.43 = (bf16[32,12288]{1,0:T(8,128)(2,1)}, bf16[32,12288]{1,0:T(8,128)(2,1)S(1)}, u32[]{:S(2)}, u32[]{:S(2)}) collective-permute-start(bf16[32,12288]{1,0:T(8,128)(2,1)} %get-tuple-element.200), channel_id=1, source_target_pairs={{0,8},{8,0},{16,24},{24,16},{1,9},{9,1},{17,25},{25,17},{2,10},{10... | collective-permute-start | bytes 2359304 | tf_op jit(solution)/shard_map/ppermute | solution.py:326
  139.4 32.6 %collective-permute-start.44 = (bf16[32,12288]{1,0:T(8,128)(2,1)}, bf16[32,12288]{1,0:T(8,128)(2,1)S(1)}, u32[]{:S(2)}, u32[]{:S(2)}) collective-permute-start(bf16[32,12288]{1,0:T(8,128)(2,1)} %get-tuple-element.199), channel_id=1, source_target_pairs={{0,16},{8,24},{16,0},{24,8},{1,17},{9,25},{17,1},{25,9},{2,18},{10... | collective-permute-start | bytes 2359304 | tf_op jit(solution)/shard_map/ppermute | solution.py:326
  153.7 1.5 collective-permute-start.36
  156.1 4.5 %collective-permute-start.37 = (bf16[16,512]{1,0:T(8,128)(2,1)S(1)}, bf16[16,512]{1,0:T(8,128)(2,1)S(1)}, u32[]{:S(2)}, u32[]{:S(2)}) collective-permute-start(bf16[16,512]{1,0:T(8,128)(2,1)S(1)} %get-tuple-element.268), channel_id=1, source_target_pairs={{0,2},{1,3},{2,0},{3,1},{4,6},{5,7},{6,4},{7,5},{8,10},{9,11},{10,... | collective-permute-start | bytes 49160 | tf_op jit(solution)/shard_map/ppermute | solution.py:329
  156.2 4.8 %collective-permute-start.38 = (bf16[16,512]{1,0:T(8,128)(2,1)S(1)}, bf16[16,512]{1,0:T(8,128)(2,1)S(1)}, u32[]{:S(2)}, u32[]{:S(2)}) collective-permute-start(bf16[16,512]{1,0:T(8,128)(2,1)S(1)} %get-tuple-element.267), channel_id=1, source_target_pairs={{0,4},{1,5},{2,6},{3,7},{4,0},{5,1},{6,2},{7,3},{8,12},{9,13},{10,... | collective-permute-start | bytes 49160 | tf_op jit(solution)/shard_map/ppermute | solution.py:329
  159.3 5.5 %collective-permute-start.39 = (bf16[16,512]{1,0:T(8,128)(2,1)S(1)}, bf16[16,512]{1,0:T(8,128)(2,1)S(1)}, u32[]{:S(2)}, u32[]{:S(2)}) collective-permute-start(bf16[16,512]{1,0:T(8,128)(2,1)S(1)} %get-tuple-element.266), channel_id=1, source_target_pairs={{0,6},{1,7},{2,4},{3,5},{4,2},{5,3},{6,0},{7,1},{8,14},{9,15},{10,... | collective-permute-start | bytes 49160 | tf_op jit(solution)/shard_map/ppermute | solution.py:329
  166.0 9.7 %collective-permute-start.40 = (bf16[16,512]{1,0:T(8,128)(2,1)S(1)}, bf16[16,512]{1,0:T(8,128)(2,1)S(1)}, u32[]{:S(2)}, u32[]{:S(2)}) collective-permute-start(bf16[16,512]{1,0:T(8,128)(2,1)S(1)} %convolution_convert_fusion.1), channel_id=1, source_target_pairs={{0,2},{1,3},{2,0},{3,1},{4,6},{5,7},{6,4},{7,5},{8,10},{9,11},{10,... | collective-permute-start | bytes 49160 | tf_op jit(solution)/shard_map/ppermute | solution.py:329
  166.0 10.9 %collective-permute-start.41 = (bf16[16,512]{1,0:T(8,128)(2,1)S(1)}, bf16[16,512]{1,0:T(8,128)(2,1)S(1)}, u32[]{:S(2)}, u32[]{:S(2)}) collective-permute-start(bf16[16,512]{1,0:T(8,128)(2,1)S(1)} %convolution_convert_fusion.1), channel_id=1, source_target_pairs={{0,4},{1,5},{2,6},{3,7},{4,0},{5,1},{6,2},{7,3},{8,12},{9,13},{10,... | collective-permute-start | bytes 49160 | tf_op jit(solution)/shard_map/ppermute | solution.py:329
  167.8 9.1 %collective-permute-start.42 = (bf16[16,512]{1,0:T(8,128)(2,1)S(1)}, bf16[16,512]{1,0:T(8,128)(2,1)S(1)}, u32[]{:S(2)}, u32[]{:S(2)}) collective-permute-start(bf16[16,512]{1,0:T(8,128)(2,1)S(1)} %convolution_convert_fusion.1), channel_id=1, source_target_pairs={{0,6},{1,7},{2,4},{3,5},{4,2},{5,3},{6,0},{7,1},{8,14},{9,15},{10,... | collective-permute-start | bytes 49160 | tf_op jit(solution)/shard_map/ppermute | solution.py:329
  170.4 18.2 %collective-permute-start.56 = (bf16[16,12288]{1,0:T(8,128)(2,1)}, bf16[16,12288]{1,0:T(8,128)(2,1)S(1)}, u32[]{:S(2)}, u32[]{:S(2)}) collective-permute-start(bf16[16,12288]{1,0:T(8,128)(2,1)} %get-tuple-element.171), channel_id=1, source_target_pairs={{0,16},{8,24},{16,0},{24,8},{1,17},{9,25},{17,1},{25,9},{2,18},{10... | collective-permute-start | bytes 1179656 | tf_op jit(solution)/shard_map/ppermute | solution.py:326
  171.9 18.2 %collective-permute-start.57 = (bf16[16,12288]{1,0:T(8,128)(2,1)}, bf16[16,12288]{1,0:T(8,128)(2,1)S(1)}, u32[]{:S(2)}, u32[]{:S(2)}) collective-permute-start(bf16[16,12288]{1,0:T(8,128)(2,1)} %get-tuple-element.172), channel_id=1, source_target_pairs={{0,8},{8,0},{16,24},{24,16},{1,9},{9,1},{17,25},{25,17},{2,10},{10... | collective-permute-start | bytes 1179656 | tf_op jit(solution)/shard_map/ppermute | solution.py:326
  175.7 15.6 %collective-permute-start.58 = (bf16[16,12288]{1,0:T(8,128)(2,1)S(1)}, bf16[16,12288]{1,0:T(8,128)(2,1)}, u32[]{:S(2)}, u32[]{:S(2)}) collective-permute-start(bf16[16,12288]{1,0:T(8,128)(2,1)S(1)} %copy-done.31), channel_id=1, source_target_pairs={{0,8},{8,0},{16,24},{24,16},{1,9},{9,1},{17,25},{25,17},{2,10},{10... | collective-permute-start | bytes 1179656 | tf_op jit(solution)/shard_map/ppermute | solution.py:326
  176.9 1.3 collective-permute-start.45
  187.2 12.4 %collective-permute-start.48 = (bf16[16,12288]{1,0:T(8,128)(2,1)}, bf16[16,12288]{1,0:T(8,128)(2,1)}, u32[]{:S(2)}, u32[]{:S(2)}) collective-permute-start(bf16[16,12288]{1,0:T(8,128)(2,1)} %get-tuple-element.230), channel_id=1, source_target_pairs={{0,8},{8,0},{16,24},{24,16},{1,9},{9,1},{17,25},{25,17},{2,10},{10... | collective-permute-start | bytes 1179656 | tf_op jit(solution)/shard_map/ppermute | solution.py:326
  188.1 12.3 %collective-permute-start.49 = (bf16[16,12288]{1,0:T(8,128)(2,1)}, bf16[16,12288]{1,0:T(8,128)(2,1)}, u32[]{:S(2)}, u32[]{:S(2)}) collective-permute-start(bf16[16,12288]{1,0:T(8,128)(2,1)} %get-tuple-element.229), channel_id=1, source_target_pairs={{0,16},{8,24},{16,0},{24,8},{1,17},{9,25},{17,1},{25,9},{2,18},{10... | collective-permute-start | bytes 1179656 | tf_op jit(solution)/shard_map/ppermute | solution.py:326
  188.6 56.9 %copy-start.11 = (bf16[16,12288]{1,0:T(8,128)(2,1)}, bf16[16,12288]{1,0:T(8,128)(2,1)S(1)}, u32[]{:S(2)}) copy-start(bf16[16,12288]{1,0:T(8,128)(2,1)S(1)} %collective-permute-done.56.refs_2_) | copy-start | bytes 1179652
  188.6 53.3 %collective-permute-start.52 = (bf16[32,12288]{1,0:T(8,128)(2,1)}, bf16[32,12288]{1,0:T(8,128)(2,1)S(1)}, u32[]{:S(2)}, u32[]{:S(2)}) collective-permute-start(bf16[32,12288]{1,0:T(8,128)(2,1)} %get-tuple-element.201), channel_id=1, source_target_pairs={{0,16},{8,24},{16,0},{24,8},{1,17},{9,25},{17,1},{25,9},{2,18},{10... | collective-permute-start | bytes 2359304 | tf_op jit(solution)/shard_map/ppermute | solution.py:326
  190.1 53.0 %collective-permute-start.53 = (bf16[32,12288]{1,0:T(8,128)(2,1)}, bf16[32,12288]{1,0:T(8,128)(2,1)S(1)}, u32[]{:S(2)}, u32[]{:S(2)}) collective-permute-start(bf16[32,12288]{1,0:T(8,128)(2,1)} %get-tuple-element.202), channel_id=1, source_target_pairs={{0,8},{8,0},{16,24},{24,16},{1,9},{9,1},{17,25},{25,17},{2,10},{10... | collective-permute-start | bytes 2359304 | tf_op jit(solution)/shard_map/ppermute | solution.py:326
  191.3 52.7 %collective-permute-start.54 = (bf16[32,12288]{1,0:T(8,128)(2,1)}, bf16[32,12288]{1,0:T(8,128)(2,1)S(1)}, u32[]{:S(2)}, u32[]{:S(2)}) collective-permute-start(bf16[32,12288]{1,0:T(8,128)(2,1)} %get-tuple-element.217), channel_id=1, source_target_pairs={{0,8},{8,0},{16,24},{24,16},{1,9},{9,1},{17,25},{25,17},{2,10},{10... | collective-permute-start | bytes 2359304 | tf_op jit(solution)/shard_map/ppermute | solution.py:326
  199.5 48.9 %collective-permute-start.55 = (bf16[32,12288]{1,0:T(8,128)(2,1)}, bf16[32,12288]{1,0:T(8,128)(2,1)S(1)}, u32[]{:S(2)}, u32[]{:S(2)}) collective-permute-start(bf16[32,12288]{1,0:T(8,128)(2,1)} %get-tuple-element.218), channel_id=1, source_target_pairs={{0,16},{8,24},{16,0},{24,8},{1,17},{9,25},{17,1},{25,9},{2,18},{10... | collective-permute-start | bytes 2359304 | tf_op jit(solution)/shard_map/ppermute | solution.py:326
  200.4 41.0 %collective-permute-start.59 = (bf16[16,12288]{1,0:T(8,128)(2,1)}, bf16[16,12288]{1,0:T(8,128)(2,1)}, u32[]{:S(2)}, u32[]{:S(2)}) collective-permute-start(bf16[16,12288]{1,0:T(8,128)(2,1)} %get-tuple-element.190), channel_id=1, source_target_pairs={{0,16},{8,24},{16,0},{24,8},{1,17},{9,25},{17,1},{25,9},{2,18},{10... | collective-permute-start | bytes 1179656 | tf_op jit(solution)/shard_map/ppermute | solution.py:326
  241.4 12.3 %collective-permute-start.46 = (bf16[16,12288]{1,0:T(8,128)(2,1)}, bf16[16,12288]{1,0:T(8,128)(2,1)}, u32[]{:S(2)}, u32[]{:S(2)}) collective-permute-start(bf16[16,12288]{1,0:T(8,128)(2,1)} %get-tuple-element.231), channel_id=1, source_target_pairs={{0,16},{8,24},{16,0},{24,8},{1,17},{9,25},{17,1},{25,9},{2,18},{10... | collective-permute-start | bytes 1179656 | tf_op jit(solution)/shard_map/ppermute | solution.py:326
  241.9 12.3 %collective-permute-start.47 = (bf16[16,12288]{1,0:T(8,128)(2,1)}, bf16[16,12288]{1,0:T(8,128)(2,1)}, u32[]{:S(2)}, u32[]{:S(2)}) collective-permute-start(bf16[16,12288]{1,0:T(8,128)(2,1)} %get-tuple-element.232), channel_id=1, source_target_pairs={{0,8},{8,0},{16,24},{24,16},{1,9},{9,1},{17,25},{25,17},{2,10},{10... | collective-permute-start | bytes 1179656 | tf_op jit(solution)/shard_map/ppermute | solution.py:326
  243.1 17.3 %collective-permute-start.50 = (bf16[16,12288]{1,0:T(8,128)(2,1)}, bf16[16,12288]{1,0:T(8,128)(2,1)}, u32[]{:S(2)}, u32[]{:S(2)}) collective-permute-start(bf16[16,12288]{1,0:T(8,128)(2,1)} %get-tuple-element.237), channel_id=1, source_target_pairs={{0,8},{8,0},{16,24},{24,16},{1,9},{9,1},{17,25},{25,17},{2,10},{10... | collective-permute-start | bytes 1179656 | tf_op jit(solution)/shard_map/ppermute | solution.py:326
  244.0 16.5 %collective-permute-start.51 = (bf16[16,12288]{1,0:T(8,128)(2,1)}, bf16[16,12288]{1,0:T(8,128)(2,1)}, u32[]{:S(2)}, u32[]{:S(2)}) collective-permute-start(bf16[16,12288]{1,0:T(8,128)(2,1)} %get-tuple-element.238), channel_id=1, source_target_pairs={{0,16},{8,24},{16,0},{24,8},{1,17},{9,25},{17,1},{25,9},{2,18},{10... | collective-permute-start | bytes 1179656 | tf_op jit(solution)/shard_map/ppermute | solution.py:326
  (30 other events, 269.8 us)

commit v3 on v2

--- a/solution.py
+++ b/solution.py
@@ -70,25 +70,24 @@
 
 def chunk_rows(rows, ga):
     unit = max(32, ga * 4)
-    if rows % (4 * unit):
-        return [(0, rows)]
-    return [(rows // 2, rows // 4), (0, rows // 2), (3 * rows // 4, rows // 4)]
-
-
-def stage_order(n):
+    if rows % (4 * unit) or ga % 8:
+        return [(0, rows)], [(0, 0, 1)]
+    return [(0, rows // 2), (rows // 2, rows // 2)], [(0, 0, 1), (1, 0, 2), (1, 1, 2)]
+
+
+def stage_order(outputs):
+    n, parts = outputs[-1][0] + 1, range(len(outputs))
     order = [("Wd", 0), ("We", 0), ("T", 0), ("Wf", 0), ("Wd", 1), ("We", 1), ("M", 0)]
-    order += [("A", 0), ("B", 0), ("Wf", 1), ("Wd", 2), ("We", 2)]
+    order += [("A", 0), ("B", 0), ("Wf", 1)]
     for c in range(n):
-        order += [("A", c), ("Wf", c + 1), ("B", c), ("C", c)]
-        order += [("H", c - 1), ("E", c), ("G", c), ("K", c), ("Wd", c + 3), ("We", c + 3)]
-    order += [("I", c) for c in range(n - 1)]
-    order += [("H", n - 1), ("I", n - 1)]
-    seen, kept = set(), []
-    for item in order:
-        if 0 <= item[1] < n and item not in seen:
-            seen.add(item)
-            kept.append(item)
-    return kept
+        order += [("A", c), ("B", c), ("C", c)]
+        order += [("H", k) for k in parts if outputs[k][0] == c - 1]
+        order += [("E", c)]
+        order += [(stage, k) for k in parts if outputs[k][0] == c for stage in ("G", "K")]
+    order += [("I", k) for k in parts if outputs[k][0] < n - 1]
+    order += [("H", k) for k in parts if outputs[k][0] == n - 1]
+    order += [("I", k) for k in parts if outputs[k][0] == n - 1]
+    return [item for item in dict.fromkeys(order) if item[0] in "GKHI" or item[1] < n]
 
 
 def tile_of(width, parts=4):
@@ -257,26 +256,29 @@
     )(where, *halves, proj)
 
 
-def expand_kernel(nz, where, here, there, proj, *refs):
+def expand_kernel(nz, part, where, here, there, proj, *refs):
     outs, (pieces, mixed) = refs[:8], refs[8:]
     band, core = where[0], where[1]
     half = outs[0].shape[0]
-    rows = 2 * half
+    sub, count = part
+    rows = 2 * half * count
     piece = here.shape[1]
+    each = 2 * half // piece
+    picked = [(k * count + sub) * each + i for k in range(4) for i in range(each)]
 
     @pl.when(pl.program_id(0) == 0)
     def _():
         for k in range(nz):
             pieces[piece_row(piece, rows, 2 * k + core, band) // piece] = here[k]
             pieces[piece_row(piece, rows, 2 * k + 1 - core, band) // piece] = there[k]
-        mixed[...] = jnp.concatenate([pieces[k] for k in range(2 * nz)], axis=0)
+        mixed[...] = jnp.concatenate([pieces[k] for k in picked], axis=0)
 
     value = jnp.dot(mixed[...], proj[...], preferred_element_type=jnp.float32)
     for k, out in enumerate(outs):
         out[...] = value[k * half : (k + 1) * half].astype(out.dtype)
 
 
-def expand(where, nz, rows, here, there, proj):
+def expand(where, nz, part, rows, here, there, proj):
     block, width = proj.shape
     piece = here.shape[1]
     tile = tile_of(width)
@@ -290,7 +292,7 @@
 
     counts = [rows // 2] * 8
     return pl.pallas_call(
-        functools.partial(expand_kernel, nz),
+        functools.partial(expand_kernel, nz, part),
         grid_spec=pltpu.PrefetchScalarGridSpec(
             num_scalar_prefetch=1,
             grid=(width // tile,),
@@ -328,7 +330,7 @@
     def ga_swap(value, bit):
         return lax.ppermute(value, "ga", [(i, i ^ bit) for i in range(nga)])
 
-    chunks = chunk_rows(rows, nga)
+    chunks, outputs = chunk_rows(rows, nga)
     clock = [()]
 
     def now(*values):
@@ -336,6 +338,7 @@
         return out[: len(values)]
 
     state = [dict() for _ in chunks]
+    made = [dict() for _ in outputs]
     shared = {}
 
     def stage_Wd(c, s):
@@ -400,8 +403,11 @@
         return (s["here"],)
 
     def stage_G(c, s):
-        here, there = now(s["here"], s["there"])
-        s["o"] = expand(where, nz, chunks[c][1], here, there, Pr)
+        chunk, sub, count = outputs[c]
+        here, there = now(state[chunk]["here"], state[chunk]["there"])
+        rows = chunks[chunk][1] // count
+        s["first"] = chunks[chunk][0] + sub * rows
+        s["o"] = expand(where, nz, (sub, count), rows, here, there, Pr)
         s["first_y"] = band_swap(s["o"][6], 2)
         s["first_x"] = band_swap(s["o"][7], 1)
         return s["o"][6], s["o"][7]
@@ -422,7 +428,7 @@
     def stage_I(c, s):
         parts = now(s["near0"], s["near1"], s["second0"], s["second1"])
         terms = [s["o"][0], s["o"][1], *parts]
-        shared["out"] = finish(W, kinetic, terms, chunks[c][0], shared.get("out"))
+        shared["out"] = finish(W, kinetic, terms, s["first"], shared.get("out"))
         return ()
 
     def stage_M(c, s):
@@ -435,8 +441,8 @@
         Wd=stage_Wd, We=stage_We, T=stage_T, M=stage_M, Wf=stage_Wf, A=stage_A, B=stage_B, C=stage_C,
         E=stage_E, G=stage_G, K=stage_K, H=stage_H, I=stage_I,
     )
-    for name, c in stage_order(len(chunks)):
-        clock[0] = stages[name](c, state[c])
+    for name, c in stage_order(outputs):
+        clock[0] = stages[name](c, (made if name in "GKHI" else state)[c])
     return shared["out"]
 
 

time: 264 us -> 251 us (0.951)
  starting transfers between devices: 66.2 us -> 49.9 us
  waiting for transfers between devices: 88.8 us -> 105 us
  Pallas kernels: 91.1 us -> 82.7 us
    ppermute x36 -> x30, waiting for transfers between devices: 66.8 us -> 96.5 us  [band_swap(): return lax.ppermute(value, 'band', [(i, i ^ bit) for i in range(4)])]
    ppermute x24 -> x16, waiting for transfers between devices: 22 us -> 8.12 us  [ga_swap(): return lax.ppermute(value, 'ga', [(i, i ^ bit) for i in range(nga)])]
    ppermute x24 -> x16, starting transfers between devices: 28.8 us -> 18 us  [ga_swap(): return lax.ppermute(value, 'ga', [(i, i ^ bit) for i in range(nga)])]
    pallas_call x3 -> x2, Pallas kernels: 26.9 us -> 20 us  [correlate(): pl.pallas_call(functools.partial(correlate_kernel, nz), grid_spec=pltpu.P...]
    ppermute x36 -> x30, starting transfers between devices: 37.3 us -> 31.9 us  [band_swap(): return lax.ppermute(value, 'band', [(i, i ^ bit) for i in range(4)])]
    unnamed x68 -> x44, local copies, waits for them, and re-layouts: 5.5 us -> 3.14 us
    pallas_call x3 -> x2, Pallas kernels: 6.2 us -> 4.69 us  [take_halves(): pl.pallas_call(halves_kernel, grid=(width // tile,), in_specs=[pl.BlockSp...]
  transfers between devices with their start and end apart: 60 -> 46, of which waited for: 22 -> 21; matrix products, arithmetic and copies ran while one was open for 4% -> 3% of each run, Pallas kernels for 33% -> 30%
where the time goes in v3:
time: 251 us; the launch traced here: 250 us
  waiting for transfers between devices  105 us (42%)
  Pallas kernels  82.7 us (33%)
  starting transfers between devices  49.9 us (20%)
  local copies, waits for them, and re-layouts  4.94 us (2%)
  matrix products  4.05 us (2%)
  other arithmetic  3.74 us (1%)
    ppermute x30, waiting for transfers between devices, band_swap(): return lax.ppermute(value, 'band', [(i, i ^ bit) for i in range(4)])  96.5 us
    ppermute x30, starting transfers between devices, band_swap(): return lax.ppermute(value, 'band', [(i, i ^ bit) for i in range(4)])  31.9 us
    pallas_call x3, Pallas kernels, expand(): pl.pallas_call(functools.partial(expand_kernel, nz, part), grid_spec=pltp...  26.1 us
    pallas_call x2, Pallas kernels, correlate(): pl.pallas_call(functools.partial(correlate_kernel, nz), grid_spec=pltpu.P...  20 us
    ppermute x16, starting transfers between devices, ga_swap(): return lax.ppermute(value, 'ga', [(i, i ^ bit) for i in range(nga)])  18 us
    pallas_call x1, Pallas kernels, transpose(): pl.pallas_call(transpose_kernel, grid=(width // tile,), in_specs=[pl.Bloc...  14.6 us
    pallas_call x3, Pallas kernels, finish(): pl.pallas_call(finish_kernel, grid=(width // tile,), in_specs=specs, out_...  9.97 us
    ppermute x16, waiting for transfers between devices, ga_swap(): return lax.ppermute(value, 'ga', [(i, i ^ bit) for i in range(nga)])  8.12 us
  transfers between devices with their start and end apart: 46, of which 21 were waited for; matrix products, arithmetic and copies ran while one was open for 3% of the time, Pallas kernels for 30%

profile of v3, /device:TPU:0, one launch (start us, length us, event | category | flops | bytes accessed | tf_op | source)
XLA Modules:
  0.0 250.2 jit_solution(7591964028201204939)
XLA Ops:
  0.0 2.4 take.2
  2.4 3.0 %collective-permute-start = (bf16[32,12288]{1,0:T(8,128)(2,1)}, bf16[32,12288]{1,0:T(8,128)(2,1)S(1)}, u32[]{:S(2)}, u32[]{:S(2)}) collective-permute-start(bf16[32,12288]{1,0:T(8,128)(2,1)} %get-tuple-element.111.refs_0_), channel_id=1, source_target_pairs={{0,8},{8,0},{16,24},{24,16},{1,9},{9,1},{17,25},{25,17},{2,10},{10... | collective-permute-start | bytes 2359304 | tf_op jit(solution)/shard_map/ppermute | solution.py:328
  5.3 1.5 collective-permute-start.1
  7.4 14.6 %transpose.11.refs_8_ = bf16[12288,512]{1,0:T(8,128)(2,1)} custom-call(bf16[512,12288]{1,0:T(8,128)(2,1)} %proj.5), custom_call_target="tpu_custom_call" | custom-call | flops 100663296 | bytes 25165824 | tf_op jit(solution)/shard_map/transpose/pallas_call | solution.py:111
  22.0 1.9 collective-permute-done.refs_2_
  23.9 2.0 collective-permute-done.1.refs_5_
  25.9 1.5 collective-permute-start.8
  28.6 2.3 take.3
  31.0 1.5 collective-permute-start.2
  32.5 10.3 %collective-permute-done.7.refs_4_ = bf16[32,12288]{1,0:T(8,128)(2,1)S(1)} collective-permute-done((bf16[32,12288]{1,0:T(8,128)(2,1)}, bf16[32,12288]{1,0:T(8,128)(2,1)S(1)}, u32[]{:S(2)}, u32[]{:S(2)}) %collective-permute-start.7) | collective-permute-done | bytes 786464 | tf_op jit(solution)/shard_map/ppermute | solution.py:328
  42.8 0.9 copy-done.7
  43.7 1.5 collective-permute-start.5
  45.2 14.5 %collective-permute-done.8.refs_6_ = bf16[32,12288]{1,0:T(8,128)(2,1)} collective-permute-done((bf16[32,12288]{1,0:T(8,128)(2,1)S(1)}, bf16[32,12288]{1,0:T(8,128)(2,1)}, u32[]{:S(2)}, u32[]{:S(2)}) %collective-permute-start.8) | collective-permute-done | bytes 786464 | tf_op jit(solution)/shard_map/ppermute | solution.py:328
  59.8 10.0 %correlate.2 = (bf16[4,32,512]{2,1,0:T(8,128)(2,1)}, bf16[4,32,512]{2,1,0:T(8,128)(2,1)}) custom-call(s32[2]{0:T(128)} %pad_add_fusion.where, bf16[32,12288]{1,0:T(8,128)(2,1)} %get-tuple-element.111.refs_0_, bf16[32,12288]{1,0:T(8,128)(2,1)} %get-tuple-element.112.refs_1_, bf16[32,12288]{1,0:T(8,128)(2,1)} %copy-done.5, ...), custom_call_target="tpu_custom_call" | custom-call | flops 3221225472 | bytes 18874368 | tf_op jit(solution)/shard_map/correlate/pallas_call | solution.py:239
  71.4 0.9 add_convert_fusion.1
  73.0 3.6 %collective-permute-start.15 = (bf16[32,512]{1,0:T(8,128)(2,1)}, bf16[32,512]{1,0:T(8,128)(2,1)}, u32[]{:S(2)}, u32[]{:S(2)}) collective-permute-start(bf16[32,512]{1,0:T(8,128)(2,1)} %get-tuple-element.224), channel_id=1, source_target_pairs={{0,6},{1,7},{2,4},{3,5},{4,2},{5,3},{6,0},{7,1},{8,14},{9,15},{10,... | collective-permute-start | bytes 98312 | tf_op jit(solution)/shard_map/ppermute | solution.py:331
  77.4 0.8 convolution_bitcast_fusion
  78.2 0.9 copy.10
  79.3 2.4 collective-permute-done.14
  81.8 2.0 convolution_convert_fusion.1
  83.8 1.7 collective-permute-start.18
  85.9 2.3 collective-permute-start.16
  88.8 1.5 collective-permute-start.4
  90.3 0.9 collective-permute-start.11
  91.2 1.1 collective-permute-start.12
  92.4 1.3 collective-permute-done.19.there
  94.4 9.8 %expand.3 = (bf16[32,12288]{1,0:T(8,128)(2,1)}, bf16[32,12288]{1,0:T(8,128)(2,1)}, bf16[32,12288]{1,0:T(8,128)(2,1)}, bf16[32,12288]{1,0:T(8,128)(2,1)}, bf16[32...) custom-call(s32[2]{0:T(128)} %pad_add_fusion.where, ...), custom_call_target="tpu_custom_call" | custom-call | flops 3221225472 | bytes 18874368 | tf_op jit(solution)/shard_map/expand/pallas_call | solution.py:294
  104.2 1.6 collective-permute-start.28
  105.8 2.9 %collective-permute-done.3.refs_3_ = bf16[32,12288]{1,0:T(8,128)(2,1)} collective-permute-done((bf16[32,12288]{1,0:T(8,128)(2,1)S(1)}, bf16[32,12288]{1,0:T(8,128)(2,1)}, u32[]{:S(2)}, u32[]{:S(2)}) %collective-permute-start.3) | collective-permute-done | bytes 786464 | tf_op jit(solution)/shard_map/ppermute | solution.py:328
  109.3 16.9 %collective-permute-done.11.refs_6_ = bf16[32,12288]{1,0:T(8,128)(2,1)} collective-permute-done((bf16[32,12288]{1,0:T(8,128)(2,1)S(1)}, bf16[32,12288]{1,0:T(8,128)(2,1)}, u32[]{:S(2)}, u32[]{:S(2)}) %collective-permute-start.11) | collective-permute-done | bytes 786464 | tf_op jit(solution)/shard_map/ppermute | solution.py:328
  126.1 10.0 %correlate.3 = (bf16[4,32,512]{2,1,0:T(8,128)(2,1)}, bf16[4,32,512]{2,1,0:T(8,128)(2,1)}) custom-call(s32[2]{0:T(128)} %pad_add_fusion.where, bf16[32,12288]{1,0:T(8,128)(2,1)} %get-tuple-element.120.refs_0_, bf16[32,12288]{1,0:T(8,128)(2,1)} %get-tuple-element.119.refs_1_, bf16[32,12288]{1,0:T(8,128)(2,1)} %copy-done.3, ...), custom_call_target="tpu_custom_call" | custom-call | flops 3221225472 | bytes 18874368 | tf_op jit(solution)/shard_map/correlate/pallas_call | solution.py:239
  136.2 1.6 collective-permute-done.20
  137.7 0.9 add_convert_fusion
  138.7 1.7 collective-permute-start.23
  140.4 2.7 %collective-permute-start.21 = (bf16[32,512]{1,0:T(8,128)(2,1)S(1)}, bf16[32,512]{1,0:T(8,128)(2,1)S(1)}, u32[]{:S(2)}, u32[]{:S(2)}) collective-permute-start(bf16[32,512]{1,0:T(8,128)(2,1)S(1)} %get-tuple-element.219), channel_id=1, source_target_pairs={{0,2},{1,3},{2,0},{3,1},{4,6},{5,7},{6,4},{7,5},{8,10},{9,11},{10,... | collective-permute-start | bytes 98312 | tf_op jit(solution)/shard_map/ppermute | solution.py:331
  143.1 1.3 collective-permute-done.23
  144.5 0.9 collective-permute-done.22
  145.6 1.2 convolution_convert_fusion
  146.8 1.9 collective-permute-start.26
  148.7 1.1 collective-permute-start.25
  149.8 1.5 collective-permute-start.24
  151.3 1.5 collective-permute-start.42
  152.8 0.9 copy-done.8
  153.7 2.8 %join.3 = (bf16[32,12288]{1,0:T(8,128)(2,1)}, bf16[32,12288]{1,0:T(8,128)(2,1)}) custom-call(bf16[32,12288]{1,0:T(8,128)(2,1)} %get-tuple-element.157.a, bf16[32,12288]{1,0:T(8,128)(2,1)} %collective-permute-done.28.b, bf16[32,12288]{1,0:T(8,128)(2,1)} %get-tuple-element.159.c, bf16[32,12288]{1,0:T(8,128)(2,1)} %copy-done.8), custom_call_target="tpu_custom_call" | custom-call | flops 786432 | bytes 4718592 | tf_op jit(solution)/shard_map/join/pallas_call | solution.py:156
  156.7 1.6 collective-permute-start.43
  158.9 8.2 %expand.4 = (bf16[16,12288]{1,0:T(8,128)(2,1)}, bf16[16,12288]{1,0:T(8,128)(2,1)}, bf16[16,12288]{1,0:T(8,128)(2,1)}, bf16[16,12288]{1,0:T(8,128)(2,1)}, bf16[16...) custom-call(s32[2]{0:T(128)} %pad_add_fusion.where, ...), custom_call_target="tpu_custom_call" | custom-call | flops 1610612736 | bytes 15728640 | tf_op jit(solution)/shard_map/expand/pallas_call | solution.py:294
  167.6 1.3 collective-permute-start.34
  168.9 8.2 %expand.5 = (bf16[16,12288]{1,0:T(8,128)(2,1)}, bf16[16,12288]{1,0:T(8,128)(2,1)}, bf16[16,12288]{1,0:T(8,128)(2,1)}, bf16[16,12288]{1,0:T(8,128)(2,1)}, bf16[16...) custom-call(s32[2]{0:T(128)} %pad_add_fusion.where, ...), custom_call_target="tpu_custom_call" | custom-call | flops 1610612736 | bytes 15728640 | tf_op jit(solution)/shard_map/expand/pallas_call | solution.py:294
  177.0 1.6 collective-permute-start.33
  179.9 6.0 %collective-permute-done.34.d = bf16[16,12288]{1,0:T(8,128)(2,1)} collective-permute-done((bf16[16,12288]{1,0:T(8,128)(2,1)}, bf16[16,12288]{1,0:T(8,128)(2,1)}, u32[]{:S(2)}, u32[]{:S(2)}) %collective-permute-start.34) | collective-permute-done | bytes 393248 | tf_op jit(solution)/shard_map/ppermute | solution.py:328
  185.9 1.5 collective-permute-start.32
  187.9 1.5 collective-permute-done.33.b
  190.2 2.3 join.4
  192.5 18.7 %collective-permute-done.32.d = bf16[16,12288]{1,0:T(8,128)(2,1)} collective-permute-done((bf16[16,12288]{1,0:T(8,128)(2,1)}, bf16[16,12288]{1,0:T(8,128)(2,1)}, u32[]{:S(2)}, u32[]{:S(2)}) %collective-permute-start.32) | collective-permute-done | bytes 393248 | tf_op jit(solution)/shard_map/ppermute | solution.py:328
  211.2 1.5 collective-permute-start.40
  212.7 2.3 join.5
  215.5 4.1 %collective-permute-done.39.refs_3_ = bf16[16,12288]{1,0:T(8,128)(2,1)} collective-permute-done((bf16[16,12288]{1,0:T(8,128)(2,1)}, bf16[16,12288]{1,0:T(8,128)(2,1)}, u32[]{:S(2)}, u32[]{:S(2)}) %collective-permute-start.39) | collective-permute-done | bytes 393248 | tf_op jit(solution)/shard_map/ppermute | solution.py:328
  219.6 1.5 collective-permute-start.31
  222.2 5.9 %collective-permute-done.40.refs_4_ = bf16[16,12288]{1,0:T(8,128)(2,1)} collective-permute-done((bf16[16,12288]{1,0:T(8,128)(2,1)}, bf16[16,12288]{1,0:T(8,128)(2,1)}, u32[]{:S(2)}, u32[]{:S(2)}) %collective-permute-start.40) | collective-permute-done | bytes 393248 | tf_op jit(solution)/shard_map/ppermute | solution.py:328
  228.6 4.1 %finish.3.refs_6_ = bf16[128,12288]{1,0:T(8,128)(2,1)} custom-call(bf16[128,12288]{1,0:T(8,128)(2,1)} %bands.5, f32[1,12288]{1,0:T(1,128)} %bitcast.54, bf16[32,12288]{1,0:T(8,128)(2,1)} %get-tuple-element.207.refs_0_, bf16[32,12288]{1,0:T(8,128)(2,1)} %get-tuple-element.208.refs_1_, bf16[32,12288]{1,0:T(8,128)(2,1)} %copy-done.9, ...), custom_call_target="tpu_custom_call" | custom-call | flops 6291456 | bytes 7864320 | tf_op jit(solution)/shard_map/finish/pallas_call | solution.py:192
  232.7 3.0 %collective-permute-done.41.refs_5_ = bf16[16,12288]{1,0:T(8,128)(2,1)} collective-permute-done((bf16[16,12288]{1,0:T(8,128)(2,1)}, bf16[16,12288]{1,0:T(8,128)(2,1)}, u32[]{:S(2)}, u32[]{:S(2)}) %collective-permute-start.41) | collective-permute-done | bytes 393248 | tf_op jit(solution)/shard_map/ppermute | solution.py:328
  236.5 7.9 %collective-permute-done.36.refs_4_ = bf16[16,12288]{1,0:T(8,128)(2,1)} collective-permute-done((bf16[16,12288]{1,0:T(8,128)(2,1)}, bf16[16,12288]{1,0:T(8,128)(2,1)}, u32[]{:S(2)}, u32[]{:S(2)}) %collective-permute-start.36) | collective-permute-done | bytes 393248 | tf_op jit(solution)/shard_map/ppermute | solution.py:328
  244.4 2.9 %finish.4.refs_6_ = bf16[128,12288]{1,0:T(8,128)(2,1)} custom-call(bf16[128,12288]{1,0:T(8,128)(2,1)} %bands.5, f32[1,12288]{1,0:T(1,128)} %bitcast.55, bf16[16,12288]{1,0:T(8,128)(2,1)} %get-tuple-element.201.refs_0_, bf16[16,12288]{1,0:T(8,128)(2,1)} %get-tuple-element.202.refs_1_, ...), custom_call_target="tpu_custom_call", output_to_operand_aliasing={{}: (8, {})} | custom-call | flops 3145728 | bytes 3932160 | tf_op jit(solution)/shard_map/finish/pallas_call | solution.py:192
  247.3 2.9 %finish.5 = bf16[128,12288]{1,0:T(8,128)(2,1)} custom-call(bf16[128,12288]{1,0:T(8,128)(2,1)} %bands.5, f32[1,12288]{1,0:T(1,128)} %bitcast.56, bf16[16,12288]{1,0:T(8,128)(2,1)} %get-tuple-element.177.refs_0_, bf16[16,12288]{1,0:T(8,128)(2,1)} %get-tuple-element.178.refs_1_, ...), custom_call_target="tpu_custom_call", output_to_operand_aliasing={{}: (8, {})} | custom-call | flops 3145728 | bytes 3932160 | tf_op jit(solution)/shard_map/finish/pallas_call | solution.py:192
  (103 shorter events, 14.3 us)
Async XLA Ops:
  2.4 21.6 %collective-permute-start = (bf16[32,12288]{1,0:T(8,128)(2,1)}, bf16[32,12288]{1,0:T(8,128)(2,1)S(1)}, u32[]{:S(2)}, u32[]{:S(2)}) collective-permute-start(bf16[32,12288]{1,0:T(8,128)(2,1)} %get-tuple-element.111.refs_0_), channel_id=1, source_target_pairs={{0,8},{8,0},{16,24},{24,16},{1,9},{9,1},{17,25},{25,17},{2,10},{10... | collective-permute-start | bytes 2359304 | tf_op jit(solution)/shard_map/ppermute | solution.py:328
  5.3 20.6 %collective-permute-start.1 = (bf16[32,12288]{1,0:T(8,128)(2,1)}, bf16[32,12288]{1,0:T(8,128)(2,1)S(1)}, u32[]{:S(2)}, u32[]{:S(2)}) collective-permute-start(bf16[32,12288]{1,0:T(8,128)(2,1)} %get-tuple-element.112.refs_1_), channel_id=1, source_target_pairs={{0,16},{8,24},{16,0},{24,8},{1,17},{9,25},{17,1},{25,9},{2,18},{10... | collective-permute-start | bytes 2359304 | tf_op jit(solution)/shard_map/ppermute | solution.py:328
  6.8 36.0 %collective-permute-start.7 = (bf16[32,12288]{1,0:T(8,128)(2,1)}, bf16[32,12288]{1,0:T(8,128)(2,1)S(1)}, u32[]{:S(2)}, u32[]{:S(2)}) collective-permute-start(bf16[32,12288]{1,0:T(8,128)(2,1)} %get-tuple-element.111.refs_0_), channel_id=1, source_target_pairs={{0,16},{8,24},{16,0},{24,8},{1,17},{9,25},{17,1},{25,9},{2,18},{10... | collective-permute-start | bytes 2359304 | tf_op jit(solution)/shard_map/ppermute | solution.py:328
  7.3 37.9 %collective-permute-start.6 = (bf16[32,12288]{1,0:T(8,128)(2,1)}, bf16[32,12288]{1,0:T(8,128)(2,1)}, u32[]{:S(2)}, u32[]{:S(2)}) collective-permute-start(bf16[32,12288]{1,0:T(8,128)(2,1)} %get-tuple-element.112.refs_1_), channel_id=1, source_target_pairs={{0,8},{8,0},{16,24},{24,16},{1,9},{9,1},{17,25},{25,17},{2,10},{10... | collective-permute-start | bytes 2359304 | tf_op jit(solution)/shard_map/ppermute | solution.py:328
  23.9 35.8 %copy-start.5 = (bf16[32,12288]{1,0:T(8,128)(2,1)}, bf16[32,12288]{1,0:T(8,128)(2,1)S(1)}, u32[]{:S(2)}) copy-start(bf16[32,12288]{1,0:T(8,128)(2,1)S(1)} %collective-permute-done.refs_2_) | copy-start | bytes 2359300
  25.9 33.8 %copy-start.6 = (bf16[32,12288]{1,0:T(8,128)(2,1)}, bf16[32,12288]{1,0:T(8,128)(2,1)S(1)}, u32[]{:S(2)}) copy-start(bf16[32,12288]{1,0:T(8,128)(2,1)S(1)} %collective-permute-done.1.refs_5_) | copy-start | bytes 2359300
  25.9 33.8 %collective-permute-start.8 = (bf16[32,12288]{1,0:T(8,128)(2,1)S(1)}, bf16[32,12288]{1,0:T(8,128)(2,1)}, u32[]{:S(2)}, u32[]{:S(2)}) collective-permute-start(bf16[32,12288]{1,0:T(8,128)(2,1)S(1)} %collective-permute-done.refs_2_), channel_id=1, source_target_pairs={{0,16},{8,24},{16,0},{24,8},{1,17},{9,25},{17,1},{25,9},{2,18},{10... | collective-permute-start | bytes 2359304 | tf_op jit(solution)/shard_map/ppermute | solution.py:328
  27.5 32.3 %collective-permute-start.9 = (bf16[32,12288]{1,0:T(8,128)(2,1)S(1)}, bf16[32,12288]{1,0:T(8,128)(2,1)}, u32[]{:S(2)}, u32[]{:S(2)}) collective-permute-start(bf16[32,12288]{1,0:T(8,128)(2,1)S(1)} %collective-permute-done.1.refs_5_), channel_id=1, source_target_pairs={{0,8},{8,0},{16,24},{24,16},{1,9},{9,1},{17,25},{25,17},{2,10},{10... | collective-permute-start | bytes 2359304 | tf_op jit(solution)/shard_map/ppermute | solution.py:328
  31.0 48.3 %collective-permute-start.2 = (bf16[32,12288]{1,0:T(8,128)(2,1)}, bf16[32,12288]{1,0:T(8,128)(2,1)S(1)}, u32[]{:S(2)}, u32[]{:S(2)}) collective-permute-start(bf16[32,12288]{1,0:T(8,128)(2,1)} %get-tuple-element.120.refs_0_), channel_id=1, source_target_pairs={{0,8},{8,0},{16,24},{24,16},{1,9},{9,1},{17,25},{25,17},{2,10},{10... | collective-permute-start | bytes 2359304 | tf_op jit(solution)/shard_map/ppermute | solution.py:328
  43.7 27.3 %copy-start.20 = (s32[256]{0:T(256)S(1)}, s32[256]{0:T(256)}, u32[]{:S(2)}) copy-start(s32[256]{0:T(256)} %param.8) | copy-start | bytes 3076
  43.7 33.7 %copy-start.16 = (f32[4,8,8]{2,1,0:T(8,128)S(1)}, f32[4,8,8]{2,1,0:T(8,128)}, u32[]{:S(2)}) copy-start(f32[4,8,8]{2,1,0:T(8,128)} %param.9) | copy-start | bytes 3076
  43.7 35.6 %collective-permute-start.5 = (bf16[32,12288]{1,0:T(8,128)(2,1)}, bf16[32,12288]{1,0:T(8,128)(2,1)S(1)}, u32[]{:S(2)}, u32[]{:S(2)}) collective-permute-start(bf16[32,12288]{1,0:T(8,128)(2,1)} %get-tuple-element.119.refs_1_), channel_id=1, source_target_pairs={{0,16},{8,24},{16,0},{24,8},{1,17},{9,25},{17,1},{25,9},{2,18},{10... | collective-permute-start | bytes 2359304 | tf_op jit(solution)/shard_map/ppermute | solution.py:328
  69.8 18.5 %copy-start.2 = (bf16[32,12288]{1,0:T(8,128)(2,1)S(1)}, bf16[32,12288]{1,0:T(8,128)(2,1)}, u32[]{:S(2)}) copy-start(bf16[32,12288]{1,0:T(8,128)(2,1)} %get-tuple-element.119.refs_1_) | copy-start | bytes 2359300
  69.8 19.0 %copy-start.1 = (bf16[32,12288]{1,0:T(8,128)(2,1)S(1)}, bf16[32,12288]{1,0:T(8,128)(2,1)}, u32[]{:S(2)}) copy-start(bf16[32,12288]{1,0:T(8,128)(2,1)} %get-tuple-element.120.refs_0_) | copy-start | bytes 2359300
  69.8 1.6 collective-permute-start.10
  73.0 6.3 %collective-permute-start.15 = (bf16[32,512]{1,0:T(8,128)(2,1)}, bf16[32,512]{1,0:T(8,128)(2,1)}, u32[]{:S(2)}, u32[]{:S(2)}) collective-permute-start(bf16[32,512]{1,0:T(8,128)(2,1)} %get-tuple-element.224), channel_id=1, source_target_pairs={{0,6},{1,7},{2,4},{3,5},{4,2},{5,3},{6,0},{7,1},{8,14},{9,15},{10,... | collective-permute-start | bytes 98312 | tf_op jit(solution)/shard_map/ppermute | solution.py:331
  76.6 5.1 %collective-permute-start.14 = (bf16[32,512]{1,0:T(8,128)(2,1)}, bf16[32,512]{1,0:T(8,128)(2,1)}, u32[]{:S(2)}, u32[]{:S(2)}) collective-permute-start(bf16[32,512]{1,0:T(8,128)(2,1)} %get-tuple-element.225), channel_id=1, source_target_pairs={{0,4},{1,5},{2,6},{3,7},{4,0},{5,1},{6,2},{7,3},{8,12},{9,13},{10,... | collective-permute-start | bytes 98312 | tf_op jit(solution)/shard_map/ppermute | solution.py:331
  76.6 5.1 %collective-permute-start.13 = (bf16[32,512]{1,0:T(8,128)(2,1)}, bf16[32,512]{1,0:T(8,128)(2,1)}, u32[]{:S(2)}, u32[]{:S(2)}) collective-permute-start(bf16[32,512]{1,0:T(8,128)(2,1)} %get-tuple-element.226), channel_id=1, source_target_pairs={{0,2},{1,3},{2,0},{3,1},{4,6},{5,7},{6,4},{7,5},{8,10},{9,11},{10,... | collective-permute-start | bytes 98312 | tf_op jit(solution)/shard_map/ppermute | solution.py:331
  79.3 24.9 %copy-start.3 = (bf16[32,12288]{1,0:T(8,128)(2,1)}, bf16[32,12288]{1,0:T(8,128)(2,1)S(1)}, u32[]{:S(2)}) copy-start(bf16[32,12288]{1,0:T(8,128)(2,1)S(1)} %collective-permute-done.2.refs_2_) | copy-start | bytes 2359300
  79.3 24.9 %copy-start.4 = (bf16[32,12288]{1,0:T(8,128)(2,1)}, bf16[32,12288]{1,0:T(8,128)(2,1)S(1)}, u32[]{:S(2)}) copy-start(bf16[32,12288]{1,0:T(8,128)(2,1)S(1)} %collective-permute-done.5.refs_5_) | copy-start | bytes 2359300
  83.8 6.5 %collective-permute-start.18 = (bf16[32,512]{1,0:T(8,128)(2,1)S(1)}, bf16[32,512]{1,0:T(8,128)(2,1)S(1)}, u32[]{:S(2)}, u32[]{:S(2)}) collective-permute-start(bf16[32,512]{1,0:T(8,128)(2,1)S(1)} %convolution_convert_fusion.1), channel_id=1, source_target_pairs={{0,6},{1,7},{2,4},{3,5},{4,2},{5,3},{6,0},{7,1},{8,14},{9,15},{10,... | collective-permute-start | bytes 98312 | tf_op jit(solution)/shard_map/ppermute | solution.py:331
  85.5 5.7 %collective-permute-start.17 = (bf16[32,512]{1,0:T(8,128)(2,1)S(1)}, bf16[32,512]{1,0:T(8,128)(2,1)S(1)}, u32[]{:S(2)}, u32[]{:S(2)}) collective-permute-start(bf16[32,512]{1,0:T(8,128)(2,1)S(1)} %convolution_convert_fusion.1), channel_id=1, source_target_pairs={{0,4},{1,5},{2,6},{3,7},{4,0},{5,1},{6,2},{7,3},{8,12},{9,13},{10,... | collective-permute-start | bytes 98312 | tf_op jit(solution)/shard_map/ppermute | solution.py:331
  85.9 6.4 %collective-permute-start.16 = (bf16[32,512]{1,0:T(8,128)(2,1)S(1)}, bf16[32,512]{1,0:T(8,128)(2,1)S(1)}, u32[]{:S(2)}, u32[]{:S(2)}) collective-permute-start(bf16[32,512]{1,0:T(8,128)(2,1)S(1)} %convolution_convert_fusion.1), channel_id=1, source_target_pairs={{0,2},{1,3},{2,0},{3,1},{4,6},{5,7},{6,4},{7,5},{8,10},{9,11},{10,... | collective-permute-start | bytes 98312 | tf_op jit(solution)/shard_map/ppermute | solution.py:331
  88.2 20.5 %collective-permute-start.3 = (bf16[32,12288]{1,0:T(8,128)(2,1)S(1)}, bf16[32,12288]{1,0:T(8,128)(2,1)}, u32[]{:S(2)}, u32[]{:S(2)}) collective-permute-start(bf16[32,12288]{1,0:T(8,128)(2,1)S(1)} %copy-done.2), channel_id=1, source_target_pairs={{0,8},{8,0},{16,24},{24,16},{1,9},{9,1},{17,25},{25,17},{2,10},{10... | collective-permute-start | bytes 2359304 | tf_op jit(solution)/shard_map/ppermute | solution.py:328
  88.8 20.5 %collective-permute-start.4 = (bf16[32,12288]{1,0:T(8,128)(2,1)S(1)}, bf16[32,12288]{1,0:T(8,128)(2,1)}, u32[]{:S(2)}, u32[]{:S(2)}) collective-permute-start(bf16[32,12288]{1,0:T(8,128)(2,1)S(1)} %copy-done.1), channel_id=1, source_target_pairs={{0,16},{8,24},{16,0},{24,8},{1,17},{9,25},{17,1},{25,9},{2,18},{10... | collective-permute-start | bytes 2359304 | tf_op jit(solution)/shard_map/ppermute | solution.py:328
  90.3 35.8 %collective-permute-start.11 = (bf16[32,12288]{1,0:T(8,128)(2,1)S(1)}, bf16[32,12288]{1,0:T(8,128)(2,1)}, u32[]{:S(2)}, u32[]{:S(2)}) collective-permute-start(bf16[32,12288]{1,0:T(8,128)(2,1)S(1)} %collective-permute-done.2.refs_2_), channel_id=1, source_target_pairs={{0,16},{8,24},{16,0},{24,8},{1,17},{9,25},{17,1},{25,9},{2,18},{10... | collective-permute-start | bytes 2359304 | tf_op jit(solution)/shard_map/ppermute | solution.py:328
  91.2 34.9 %collective-permute-start.12 = (bf16[32,12288]{1,0:T(8,128)(2,1)S(1)}, bf16[32,12288]{1,0:T(8,128)(2,1)}, u32[]{:S(2)}, u32[]{:S(2)}) collective-permute-start(bf16[32,12288]{1,0:T(8,128)(2,1)S(1)} %collective-permute-done.5.refs_5_), channel_id=1, source_target_pairs={{0,8},{8,0},{16,24},{24,16},{1,9},{9,1},{17,25},{25,17},{2,10},{10... | collective-permute-start | bytes 2359304 | tf_op jit(solution)/shard_map/ppermute | solution.py:328
  92.4 1.4 copy-start.14
  92.4 1.4 collective-permute-start.19
  104.2 47.1 %collective-permute-start.28 = (bf16[32,12288]{1,0:T(8,128)(2,1)}, bf16[32,12288]{1,0:T(8,128)(2,1)}, u32[]{:S(2)}, u32[]{:S(2)}) collective-permute-start(bf16[32,12288]{1,0:T(8,128)(2,1)} %get-tuple-element.143), channel_id=1, source_target_pairs={{0,16},{8,24},{16,0},{24,8},{1,17},{9,25},{17,1},{25,9},{2,18},{10... | collective-permute-start | bytes 2359304 | tf_op jit(solution)/shard_map/ppermute | solution.py:328
  105.8 39.8 %copy-start.17 = (s32[512]{0:T(512)S(1)}, s32[512]{0:T(512)}, u32[]{:S(2)}) copy-start(s32[512]{0:T(512)} %get-tuple-element.227) | copy-start | bytes 6148
  105.8 39.8 %copy-start.18 = (s32[512]{0:T(512)S(1)}, s32[512]{0:T(512)}, u32[]{:S(2)}) copy-start(s32[512]{0:T(512)} %get-tuple-element.228) | copy-start | bytes 6148
  105.8 39.8 %copy-start.21 = (pred[512]{0:T(512)(128)(4,1)S(1)}, pred[512]{0:T(512)(128)(4,1)}, u32[]{:S(2)}) copy-start(pred[512]{0:T(512)(128)(4,1)} %fusion.37) | copy-start | bytes 1540
  108.8 44.1 %collective-permute-start.27 = (bf16[32,12288]{1,0:T(8,128)(2,1)}, bf16[32,12288]{1,0:T(8,128)(2,1)S(1)}, u32[]{:S(2)}, u32[]{:S(2)}) collective-permute-start(bf16[32,12288]{1,0:T(8,128)(2,1)} %get-tuple-element.144), channel_id=1, source_target_pairs={{0,8},{8,0},{16,24},{24,16},{1,9},{9,1},{17,25},{25,17},{2,10},{10... | collective-permute-start | bytes 2359304 | tf_op jit(solution)/shard_map/ppermute | solution.py:328
  136.2 1.6 collective-permute-start.20
  138.7 5.8 %collective-permute-start.23 = (bf16[32,512]{1,0:T(8,128)(2,1)S(1)}, bf16[32,512]{1,0:T(8,128)(2,1)S(1)}, u32[]{:S(2)}, u32[]{:S(2)}) collective-permute-start(bf16[32,512]{1,0:T(8,128)(2,1)S(1)} %get-tuple-element.217), channel_id=1, source_target_pairs={{0,6},{1,7},{2,4},{3,5},{4,2},{5,3},{6,0},{7,1},{8,14},{9,15},{10,... | collective-permute-start | bytes 98312 | tf_op jit(solution)/shard_map/ppermute | solution.py:331
  140.4 5.0 %collective-permute-start.22 = (bf16[32,512]{1,0:T(8,128)(2,1)S(1)}, bf16[32,512]{1,0:T(8,128)(2,1)S(1)}, u32[]{:S(2)}, u32[]{:S(2)}) collective-permute-start(bf16[32,512]{1,0:T(8,128)(2,1)S(1)} %get-tuple-element.218), channel_id=1, source_target_pairs={{0,4},{1,5},{2,6},{3,7},{4,0},{5,1},{6,2},{7,3},{8,12},{9,13},{10,... | collective-permute-start | bytes 98312 | tf_op jit(solution)/shard_map/ppermute | solution.py:331
  140.4 5.2 %collective-permute-start.21 = (bf16[32,512]{1,0:T(8,128)(2,1)S(1)}, bf16[32,512]{1,0:T(8,128)(2,1)S(1)}, u32[]{:S(2)}, u32[]{:S(2)}) collective-permute-start(bf16[32,512]{1,0:T(8,128)(2,1)S(1)} %get-tuple-element.219), channel_id=1, source_target_pairs={{0,2},{1,3},{2,0},{3,1},{4,6},{5,7},{6,4},{7,5},{8,10},{9,11},{10,... | collective-permute-start | bytes 98312 | tf_op jit(solution)/shard_map/ppermute | solution.py:331
  146.8 9.7 %collective-permute-start.26 = (bf16[32,512]{1,0:T(8,128)(2,1)S(1)}, bf16[32,512]{1,0:T(8,128)(2,1)S(1)}, u32[]{:S(2)}, u32[]{:S(2)}) collective-permute-start(bf16[32,512]{1,0:T(8,128)(2,1)S(1)} %convolution_convert_fusion), channel_id=1, source_target_pairs={{0,6},{1,7},{2,4},{3,5},{4,2},{5,3},{6,0},{7,1},{8,14},{9,15},{10,... | collective-permute-start | bytes 98312 | tf_op jit(solution)/shard_map/ppermute | solution.py:331
  148.7 7.8 %collective-permute-start.25 = (bf16[32,512]{1,0:T(8,128)(2,1)S(1)}, bf16[32,512]{1,0:T(8,128)(2,1)S(1)}, u32[]{:S(2)}, u32[]{:S(2)}) collective-permute-start(bf16[32,512]{1,0:T(8,128)(2,1)S(1)} %convolution_convert_fusion), channel_id=1, source_target_pairs={{0,4},{1,5},{2,6},{3,7},{4,0},{5,1},{6,2},{7,3},{8,12},{9,13},{10,... | collective-permute-start | bytes 98312 | tf_op jit(solution)/shard_map/ppermute | solution.py:331
  149.8 6.7 %collective-permute-start.24 = (bf16[32,512]{1,0:T(8,128)(2,1)S(1)}, bf16[32,512]{1,0:T(8,128)(2,1)S(1)}, u32[]{:S(2)}, u32[]{:S(2)}) collective-permute-start(bf16[32,512]{1,0:T(8,128)(2,1)S(1)} %convolution_convert_fusion), channel_id=1, source_target_pairs={{0,2},{1,3},{2,0},{3,1},{4,6},{5,7},{6,4},{7,5},{8,10},{9,11},{10,... | collective-permute-start | bytes 98312 | tf_op jit(solution)/shard_map/ppermute | solution.py:331
  151.3 27.3 %collective-permute-start.42 = (bf16[32,12288]{1,0:T(8,128)(2,1)}, bf16[32,12288]{1,0:T(8,128)(2,1)S(1)}, u32[]{:S(2)}, u32[]{:S(2)}) collective-permute-start(bf16[32,12288]{1,0:T(8,128)(2,1)} %get-tuple-element.145), channel_id=1, source_target_pairs={{0,16},{8,24},{16,0},{24,8},{1,17},{9,25},{17,1},{25,9},{2,18},{10... | collective-permute-start | bytes 2359304 | tf_op jit(solution)/shard_map/ppermute | solution.py:328
  156.6 1.7 copy-start
  156.6 1.6 collective-permute-start.29
  156.7 30.7 %collective-permute-start.43 = (bf16[32,12288]{1,0:T(8,128)(2,1)}, bf16[32,12288]{1,0:T(8,128)(2,1)S(1)}, u32[]{:S(2)}, u32[]{:S(2)}) collective-permute-start(bf16[32,12288]{1,0:T(8,128)(2,1)} %get-tuple-element.146), channel_id=1, source_target_pairs={{0,8},{8,0},{16,24},{24,16},{1,9},{9,1},{17,25},{25,17},{2,10},{10... | collective-permute-start | bytes 2359304 | tf_op jit(solution)/shard_map/ppermute | solution.py:328
  167.1 12.3 %collective-permute-start.35 = (bf16[16,12288]{1,0:T(8,128)(2,1)}, bf16[16,12288]{1,0:T(8,128)(2,1)}, u32[]{:S(2)}, u32[]{:S(2)}) collective-permute-start(bf16[16,12288]{1,0:T(8,128)(2,1)} %get-tuple-element.171), channel_id=1, source_target_pairs={{0,16},{8,24},{16,0},{24,8},{1,17},{9,25},{17,1},{25,9},{2,18},{10... | collective-permute-start | bytes 1179656 | tf_op jit(solution)/shard_map/ppermute | solution.py:328
  167.6 18.3 %collective-permute-start.34 = (bf16[16,12288]{1,0:T(8,128)(2,1)}, bf16[16,12288]{1,0:T(8,128)(2,1)}, u32[]{:S(2)}, u32[]{:S(2)}) collective-permute-start(bf16[16,12288]{1,0:T(8,128)(2,1)} %get-tuple-element.172), channel_id=1, source_target_pairs={{0,8},{8,0},{16,24},{24,16},{1,9},{9,1},{17,25},{25,17},{2,10},{10... | collective-permute-start | bytes 1179656 | tf_op jit(solution)/shard_map/ppermute | solution.py:328
  177.0 42.6 %copy-start.19 = (bf16[16,12288]{1,0:T(8,128)(2,1)S(1)}, bf16[16,12288]{1,0:T(8,128)(2,1)}, u32[]{:S(2)}) copy-start(bf16[16,12288]{1,0:T(8,128)(2,1)} %get-tuple-element.184) | copy-start | bytes 1179652
  177.0 12.4 %collective-permute-start.33 = (bf16[16,12288]{1,0:T(8,128)(2,1)}, bf16[16,12288]{1,0:T(8,128)(2,1)}, u32[]{:S(2)}, u32[]{:S(2)}) collective-permute-start(bf16[16,12288]{1,0:T(8,128)(2,1)} %get-tuple-element.181), channel_id=1, source_target_pairs={{0,16},{8,24},{16,0},{24,8},{1,17},{9,25},{17,1},{25,9},{2,18},{10... | collective-permute-start | bytes 1179656 | tf_op jit(solution)/shard_map/ppermute | solution.py:328
  178.6 49.9 %copy-start.9 = (bf16[32,12288]{1,0:T(8,128)(2,1)}, bf16[32,12288]{1,0:T(8,128)(2,1)S(1)}, u32[]{:S(2)}) copy-start(bf16[32,12288]{1,0:T(8,128)(2,1)S(1)} %collective-permute-done.42.refs_2_) | copy-start | bytes 2359300
  178.6 42.5 %collective-permute-start.44 = (bf16[32,12288]{1,0:T(8,128)(2,1)}, bf16[32,12288]{1,0:T(8,128)(2,1)S(1)}, u32[]{:S(2)}, u32[]{:S(2)}) collective-permute-start(bf16[32,12288]{1,0:T(8,128)(2,1)} %get-tuple-element.161), channel_id=1, source_target_pairs={{0,8},{8,0},{16,24},{24,16},{1,9},{9,1},{17,25},{25,17},{2,10},{10... | collective-permute-start | bytes 2359304 | tf_op jit(solution)/shard_map/ppermute | solution.py:328
  179.4 42.2 %collective-permute-start.45 = (bf16[32,12288]{1,0:T(8,128)(2,1)}, bf16[32,12288]{1,0:T(8,128)(2,1)S(1)}, u32[]{:S(2)}, u32[]{:S(2)}) collective-permute-start(bf16[32,12288]{1,0:T(8,128)(2,1)} %get-tuple-element.162), channel_id=1, source_target_pairs={{0,16},{8,24},{16,0},{24,8},{1,17},{9,25},{17,1},{25,9},{2,18},{10... | collective-permute-start | bytes 2359304 | tf_op jit(solution)/shard_map/ppermute | solution.py:328
  185.9 25.3 %collective-permute-start.32 = (bf16[16,12288]{1,0:T(8,128)(2,1)}, bf16[16,12288]{1,0:T(8,128)(2,1)}, u32[]{:S(2)}, u32[]{:S(2)}) collective-permute-start(bf16[16,12288]{1,0:T(8,128)(2,1)} %get-tuple-element.182), channel_id=1, source_target_pairs={{0,8},{8,0},{16,24},{24,16},{1,9},{9,1},{17,25},{25,17},{2,10},{10... | collective-permute-start | bytes 1179656 | tf_op jit(solution)/shard_map/ppermute | solution.py:328
  187.4 41.1 %copy-start.10 = (bf16[32,12288]{1,0:T(8,128)(2,1)}, bf16[32,12288]{1,0:T(8,128)(2,1)S(1)}, u32[]{:S(2)}) copy-start(bf16[32,12288]{1,0:T(8,128)(2,1)S(1)} %collective-permute-done.43.refs_3_) | copy-start | bytes 2359300
  187.4 27.5 %collective-permute-start.38 = (bf16[16,12288]{1,0:T(8,128)(2,1)}, bf16[16,12288]{1,0:T(8,128)(2,1)}, u32[]{:S(2)}, u32[]{:S(2)}) collective-permute-start(bf16[16,12288]{1,0:T(8,128)(2,1)} %get-tuple-element.173), channel_id=1, source_target_pairs={{0,16},{8,24},{16,0},{24,8},{1,17},{9,25},{17,1},{25,9},{2,18},{10... | collective-permute-start | bytes 1179656 | tf_op jit(solution)/shard_map/ppermute | solution.py:328
  189.4 30.2 %collective-permute-start.39 = (bf16[16,12288]{1,0:T(8,128)(2,1)}, bf16[16,12288]{1,0:T(8,128)(2,1)}, u32[]{:S(2)}, u32[]{:S(2)}) collective-permute-start(bf16[16,12288]{1,0:T(8,128)(2,1)} %get-tuple-element.174), channel_id=1, source_target_pairs={{0,8},{8,0},{16,24},{24,16},{1,9},{9,1},{17,25},{25,17},{2,10},{10... | collective-permute-start | bytes 1179656 | tf_op jit(solution)/shard_map/ppermute | solution.py:328
  211.2 16.9 %collective-permute-start.40 = (bf16[16,12288]{1,0:T(8,128)(2,1)}, bf16[16,12288]{1,0:T(8,128)(2,1)}, u32[]{:S(2)}, u32[]{:S(2)}) collective-permute-start(bf16[16,12288]{1,0:T(8,128)(2,1)} %get-tuple-element.190), channel_id=1, source_target_pairs={{0,8},{8,0},{16,24},{24,16},{1,9},{9,1},{17,25},{25,17},{2,10},{10... | collective-permute-start | bytes 1179656 | tf_op jit(solution)/shard_map/ppermute | solution.py:328
  214.9 20.8 %collective-permute-start.30 = (bf16[16,12288]{1,0:T(8,128)(2,1)}, bf16[16,12288]{1,0:T(8,128)(2,1)}, u32[]{:S(2)}, u32[]{:S(2)}) collective-permute-start(bf16[16,12288]{1,0:T(8,128)(2,1)} %get-tuple-element.183), channel_id=1, source_target_pairs={{0,16},{8,24},{16,0},{24,8},{1,17},{9,25},{17,1},{25,9},{2,18},{10... | collective-permute-start | bytes 1179656 | tf_op jit(solution)/shard_map/ppermute | solution.py:328
  219.6 16.9 %collective-permute-start.31 = (bf16[16,12288]{1,0:T(8,128)(2,1)S(1)}, bf16[16,12288]{1,0:T(8,128)(2,1)}, u32[]{:S(2)}, u32[]{:S(2)}) collective-permute-start(bf16[16,12288]{1,0:T(8,128)(2,1)S(1)} %copy-done.19), channel_id=1, source_target_pairs={{0,8},{8,0},{16,24},{24,16},{1,9},{9,1},{17,25},{25,17},{2,10},{10... | collective-permute-start | bytes 1179656 | tf_op jit(solution)/shard_map/ppermute | solution.py:328
  221.1 7.4 %copy-start.11 = (bf16[32,12288]{1,0:T(8,128)(2,1)}, bf16[32,12288]{1,0:T(8,128)(2,1)S(1)}, u32[]{:S(2)}) copy-start(bf16[32,12288]{1,0:T(8,128)(2,1)S(1)} %collective-permute-done.44.refs_4_) | copy-start | bytes 2359300
  221.1 14.6 %collective-permute-start.41 = (bf16[16,12288]{1,0:T(8,128)(2,1)}, bf16[16,12288]{1,0:T(8,128)(2,1)}, u32[]{:S(2)}, u32[]{:S(2)}) collective-permute-start(bf16[16,12288]{1,0:T(8,128)(2,1)} %get-tuple-element.191), channel_id=1, source_target_pairs={{0,16},{8,24},{16,0},{24,8},{1,17},{9,25},{17,1},{25,9},{2,18},{10... | collective-permute-start | bytes 1179656 | tf_op jit(solution)/shard_map/ppermute | solution.py:328
  221.6 6.9 %copy-start.12 = (bf16[32,12288]{1,0:T(8,128)(2,1)}, bf16[32,12288]{1,0:T(8,128)(2,1)S(1)}, u32[]{:S(2)}) copy-start(bf16[32,12288]{1,0:T(8,128)(2,1)S(1)} %collective-permute-done.45.refs_5_) | copy-start | bytes 2359300
  221.6 22.7 %collective-permute-start.36 = (bf16[16,12288]{1,0:T(8,128)(2,1)}, bf16[16,12288]{1,0:T(8,128)(2,1)}, u32[]{:S(2)}, u32[]{:S(2)}) collective-permute-start(bf16[16,12288]{1,0:T(8,128)(2,1)} %get-tuple-element.195), channel_id=1, source_target_pairs={{0,8},{8,0},{16,24},{24,16},{1,9},{9,1},{17,25},{25,17},{2,10},{10... | collective-permute-start | bytes 1179656 | tf_op jit(solution)/shard_map/ppermute | solution.py:328
  228.0 16.3 %collective-permute-start.37 = (bf16[16,12288]{1,0:T(8,128)(2,1)}, bf16[16,12288]{1,0:T(8,128)(2,1)}, u32[]{:S(2)}, u32[]{:S(2)}) collective-permute-start(bf16[16,12288]{1,0:T(8,128)(2,1)} %get-tuple-element.196), channel_id=1, source_target_pairs={{0,16},{8,24},{16,0},{24,8},{1,17},{9,25},{17,1},{25,9},{2,18},{10... | collective-permute-start | bytes 1179656 | tf_op jit(solution)/shard_map/ppermute | solution.py:328
  (4 other events, 3.1 us)
